TPU v7x, 32 devices: a whole 2x2x4 slice. The times are simulated.
32 devices in a mesh: head: 4 (over z), doc: 8 (over y, x, core).
Axes of the slice: x: 2, y: 2, z: 4, core: 2. Of those that a mesh axis runs over, the one named last changes fastest.
Arguments:
- packed_query_rows: bfloat16 [4096, 4096], P(('doc', 'head')), may hold values from -160 to 160
- packed_key_rows: bfloat16 [4096, 1024], P(('doc', 'head')), may hold values from -6 to 6
- packed_value_rows: bfloat16 [4096, 1024], P(('doc', 'head')), may hold values from -6 to 6
- doc_lengths: int32 [16], replicated, may hold values from 1 to 2048, 4096 in all
Outputs:
- attended: bfloat16 [4096, 4096], P(('doc', 'head'))
Inputs may be any that keep to these rules, and one draw needn't show every extreme that they name: `doc_lengths`: the documents lie end to end in order and their lengths sum to 4096.
All inputs are finite; a program needn't handle non-finite values.
Results may differ from a plain program's by a relative error of at most 0.011.
Values may be sent and summed in bfloat16 or wider, within the bound.
No kernel may reach another device: no remote copies, remote signals or barrier semaphores. Data moves between devices by JAX's collectives and lax.ppermute only.
A program may use at most 64 MiB of HBM per device.

v0:
```python
import functools
import math

import jax
import jax.numpy as jnp
from jax import lax
from jax.experimental import pallas as pl
from jax.experimental.pallas import tpu as pltpu
from jax.sharding import PartitionSpec as P

KEY_VALUE_HEADS = 8
HEAD_SIZE = 128
NEGATIVE = -1e30
HALVES = 2


def attend_kernel(steps, half, back, slots, opening, closing, parts, place_ref, lengths_ref, *refs):
    width = KEY_VALUE_HEADS
    q_refs, refs = refs[:width], refs[width:]
    units, refs = refs[: len(steps)], refs[len(steps) :]
    if not opening:
        acc_in, stat_in = refs[:2]
        refs = refs[2:]
    if closing:
        out_refs, refs = refs[: len(slots)], refs[len(slots) :]
        acc_ref, stat_ref = refs[:2]
    else:
        acc_out, stat_out = refs[:2]
        acc_ref, stat_ref = refs[2:4]
    q_ref = refs[-2]
    q_sem = refs[-1]
    rows, columns = q_refs[0].shape
    heads = columns // HEAD_SIZE
    lanes = heads * rows
    shard = parts * rows
    chunk = width // HALVES
    depth = place_ref[0]
    member = place_ref[1]
    group = place_ref[2]
    scale = math.log2(math.e) / math.sqrt(HEAD_SIZE)
    first_slot = slots[0]

    copies = [
        pltpu.make_async_copy(q_refs[slot], q_ref.at[slot - first_slot], q_sem) for slot in slots
    ]
    for copy in copies:
        copy.start()
    for copy in copies:
        copy.wait()

    def one_block(turn, _):
        slot = first_slot + turn
        doc = jnp.bitwise_xor(member, slot)
        root = ((group * width + doc) * parts + depth) * rows
        at = root + lax.broadcasted_iota(jnp.int32, (1, rows), 1)

        def add_doc(i, carry):
            closed, low, high, firsts = carry
            length = lengths_ref[i]
            closed = closed + length
            low = low + jnp.where(closed <= root, length, 0)
            high = high + jnp.where(closed <= root + rows - 1, length, 0)
            firsts = firsts + jnp.where(closed <= at, length, 0)
            return closed, low, high, firsts

        zero = jnp.int32(0)
        _, low, high, firsts = lax.fori_loop(
            0,
            lengths_ref.shape[0],
            add_doc,
            (zero, zero, zero, jnp.zeros((1, rows), jnp.int32)),
            unroll=8,
        )
        if opening:
            acc_ref[...] = jnp.zeros_like(acc_ref)
            stat_ref[0:1, :] = jnp.full((1, lanes), NEGATIVE, jnp.float32)
            stat_ref[1:2, :] = jnp.zeros((1, lanes), jnp.float32)
        else:
            acc_ref[...] = acc_in[slot]
            stat_ref[...] = stat_in[slot]
        q_block = q_ref[turn]
        queries = jnp.concatenate(
            [q_block[:, h * HEAD_SIZE : (h + 1) * HEAD_SIZE] for h in range(heads)], axis=0
        )

        def absorb(where, base, masked):
            keys = jnp.concatenate([ref[where, :, 0:HEAD_SIZE] for ref in units], axis=0)
            values = jnp.concatenate([ref[where, :, HEAD_SIZE:] for ref in units], axis=0)
            scores = lax.dot_general(
                keys, queries, (((1,), (1,)), ((), ())), preferred_element_type=jnp.float32
            )
            if masked:
                pieces = []
                for step in steps:
                    behind = depth - step
                    behind = jnp.where(behind < 0, behind + parts, behind)
                    spot = base + behind * rows + lax.broadcasted_iota(jnp.int32, (rows, rows), 0)
                    seen = (spot >= firsts) & (spot <= at)
                    pieces.append(jnp.concatenate([seen] * heads, axis=1))
                scores = jnp.where(jnp.concatenate(pieces, axis=0), scores, NEGATIVE)
            before = stat_ref[0:1, :]
            peak = jnp.maximum(before, jnp.max(scores, axis=0, keepdims=True))
            weights = jnp.exp2((scores - peak) * scale)
            total = jnp.sum(weights, axis=0, keepdims=True)
            gain = lax.dot_general(
                values,
                weights.astype(jnp.bfloat16),
                (((0,), (0,)), ((), ())),
                preferred_element_type=jnp.float32,
            )
            shrink = jnp.exp2((before - peak) * scale)
            stat_ref[0:1, :] = peak
            stat_ref[1:2, :] = stat_ref[1:2, :] * shrink + total
            acc_ref[...] = acc_ref[...] * shrink + gain

        origin = group - back
        lowest = lax.div(low, shard) - origin * width
        bottom = jnp.bitwise_xor(lax.div(member, chunk), half) * chunk
        start = jnp.maximum(lowest, bottom)
        stop = jnp.minimum(doc + back * width, bottom + chunk - 1) + 1

        def visit(key_doc, _):
            base = (origin * width + key_doc) * shard
            where = jnp.bitwise_xor(member, key_doc) - half * chunk
            clear = (base >= high) & (key_doc != doc + back * width)

            @pl.when(clear)
            def _():
                absorb(where, base, False)

            @pl.when(jnp.logical_not(clear))
            def _():
                absorb(where, base, True)

            return 0

        lax.fori_loop(start, stop, visit, 0)
        if closing:
            done = acc_ref[...] / stat_ref[1:2, :]
            for i in range(len(slots)):

                @pl.when(turn == i)
                def _():
                    for h in range(heads):
                        out_refs[i][:, h * HEAD_SIZE : (h + 1) * HEAD_SIZE] = (
                            done[:, h * rows : (h + 1) * rows].T.astype(out_refs[i].dtype)
                        )
        else:
            acc_out[slot] = acc_ref[...]
            stat_out[slot] = stat_ref[...]
        return 0

    lax.fori_loop(0, len(slots), one_block, 0)


def attend(place, doc_lengths, queries, units, steps, half, slots, state, closing, parts, back=0):
    width = KEY_VALUE_HEADS
    rows, columns = queries[0].shape
    lanes = columns // HEAD_SIZE * rows
    vmem = pl.BlockSpec(memory_space=pltpu.VMEM)
    smem = pl.BlockSpec(memory_space=pltpu.SMEM)
    hbm = pl.BlockSpec(memory_space=pl.ANY)
    opening = state is None
    held = () if opening else tuple(state)
    tokens = len(steps) * rows
    accs = jax.ShapeDtypeStruct((width, HEAD_SIZE, lanes), jnp.float32)
    stats = jax.ShapeDtypeStruct((width, 8, lanes), jnp.float32)
    if closing:
        out_shape = [jax.ShapeDtypeStruct((rows, columns), queries[0].dtype) for _ in slots]
        aliases = {}
    else:
        out_shape = [accs, stats]
        first = 2 + width + len(steps)
        aliases = {} if opening else {first: 0, first + 1: 1}
    work = len(slots) * 2 * tokens * lanes * HEAD_SIZE * 4
    return pl.pallas_call(
        functools.partial(
            attend_kernel, tuple(steps), half, back, tuple(slots), opening, closing, parts
        ),
        out_shape=out_shape,
        in_specs=[smem, smem] + [hbm] * width + [vmem] * (len(steps) + len(held)),
        out_specs=[vmem] * len(out_shape),
        input_output_aliases=aliases,
        cost_estimate=pl.CostEstimate(
            flops=work, bytes_accessed=4 * width * HEAD_SIZE * lanes, transcendentals=0
        ),
        scratch_shapes=[
            pltpu.VMEM((HEAD_SIZE, lanes), jnp.float32),
            pltpu.VMEM((8, lanes), jnp.float32),
            pltpu.VMEM((len(slots), rows, columns), queries[0].dtype),
            pltpu.SemaphoreType.DMA,
        ],
    )(place, doc_lengths, *queries, *units, *held)


def swap(block, k):
    if k == 0:
        return block
    length = lax.axis_size("doc")
    return lax.ppermute(block, "doc", [(i, i ^ k) for i in range(length)])


def on_device(packed_query_rows, packed_key_rows, packed_value_rows, doc_lengths):
    width = KEY_VALUE_HEADS
    chunk = width // HALVES
    docs, parts = lax.axis_size("doc"), lax.axis_size("head")
    index = lax.axis_index("doc")
    member, group = index % width, index // width
    place = jnp.stack([lax.axis_index("head"), member, group]).astype(jnp.int32)

    def cut(value, k):
        size = value.shape[1] // width
        return lax.dynamic_slice_in_dim(value, jnp.bitwise_xor(member, k) * size, size, 1)

    ring = [(i, (i + 1) % parts) for i in range(parts)]
    pairs = [
        swap(jnp.concatenate([cut(packed_key_rows, k), cut(packed_value_rows, k)], axis=1), k)
        for k in range(width)
    ]
    units = []
    for half in range(HALVES):
        units.append([jnp.stack(pairs[half * chunk : (half + 1) * chunk])])
    queries = [swap(cut(packed_query_rows, k), k) for k in range(width)]
    for _ in range(1, parts):
        for half in range(HALVES):
            units[half].append(lax.ppermute(units[half][-1], "head", ring))

    attends = functools.partial(attend, place, doc_lengths, queries)
    everyone = list(range(width))
    early = list(range(parts - 1))
    state = None
    if docs > width:
        over = [(i, i + width) for i in range(docs - width)]
        for half in range(HALVES):
            far = [lax.ppermute(piece, "doc", over) for piece in units[half]]
            state = attends(far, list(range(parts)), half, everyone, state, False, parts, back=1)
    for half in range(HALVES):
        state = attends(units[half][:-1], early, half, everyone, state, False, parts)
    for half in range(HALVES - 1):
        state = attends(units[half][-1:], [parts - 1], half, everyone, state, False, parts)
    half = HALVES - 1
    results = {}
    for turn in reversed(range(HALVES)):
        slots = list(range(turn * chunk, (turn + 1) * chunk))
        outs = attends(units[half][-1:], [parts - 1], half, slots, state, True, parts)
        for slot, out in zip(slots, outs):
            results[slot] = swap(out, slot)
    stacked = jnp.stack([results[k] for k in range(width)])
    order = [jnp.bitwise_xor(member, k) for k in range(width)]
    return jnp.concatenate(
        [lax.dynamic_index_in_dim(stacked, order[k], 0, keepdims=False) for k in range(width)],
        axis=1,
    )


def solution(mesh):
    in_specs = (P(("doc", "head"), None), P(("doc", "head"), None), P(("doc", "head"), None), P())
    out_specs = P(("doc", "head"), None)

    return jax.shard_map(
        on_device, mesh=mesh, in_specs=in_specs, out_specs=out_specs, check_vma=False
    )
```

profile of v0, /device:TPU:0, one launch (start us, length us, event | category | flops | bytes accessed | tf_op | source)
XLA Modules:
  0.0 107.7 jit_solution(2138082880946541606)
XLA Ops:
  0.0 1.1 %constant_dynamic-slice_fusion.6 = (bf16[128,128]{1,0:T(8,128)(2,1)S(1)}, bf16[128,128]{1,0:T(8,128)(2,1)S(1)}, bf16[128,128]{1,0:T(8,128)(2,1)S(1)}, bf16[128,1...) fusion(bf16[128,1024]{1,0:T(8,128)(2,1)} %param.6, ...), kind=kLoop, calls=%fused_computation.32 | loop fusion | bytes 1048608 | tf_op jit(solution)/shard_map/dynamic_slice | solution.py:213
  1.2 2.5 %collective-permute-start.16 = (bf16[128,256]{1,0:T(8,128)(2,1)S(1)}, bf16[128,256]{1,0:T(8,128)(2,1)S(1)}, u32[]{:S(2)}, u32[]{:S(2)}) collective-permute-start(bf16[128,256]{1,0:T(8,128)(2,1)S(1)} %pad_maximum_fusion.8), channel_id=1, source_target_pairs={{0,3},{1,2},{2,1},{3,0},{4,7},{5,6},{6,5},{7,4},{8,11},{9,10},{10,... | collective-permute-start | bytes 196616 | tf_op jit(solution)/shard_map/ppermute | solution.py:200
  3.6 0.7 collective-permute-start.14
  4.4 0.1 collective-permute-start.15
  4.5 2.1 %collective-permute-start.7 = (bf16[128,256]{1,0:T(8,128)(2,1)S(1)}, bf16[128,256]{1,0:T(8,128)(2,1)S(1)}, u32[]{:S(2)}, u32[]{:S(2)}) collective-permute-start(bf16[128,256]{1,0:T(8,128)(2,1)S(1)} %pad_maximum_fusion.2), channel_id=1, source_target_pairs={{0,4},{1,5},{2,6},{3,7},{4,0},{5,1},{6,2},{7,3},{8,12},{9,13},{10,... | collective-permute-start | bytes 196616 | tf_op jit(solution)/shard_map/ppermute | solution.py:200
  6.6 0.1 collective-permute-start.8
  6.8 0.0 collective-permute-done.16
  6.9 2.7 %collective-permute-start.9 = (bf16[128,256]{1,0:T(8,128)(2,1)S(1)}, bf16[128,256]{1,0:T(8,128)(2,1)S(1)}, u32[]{:S(2)}, u32[]{:S(2)}) collective-permute-start(bf16[128,256]{1,0:T(8,128)(2,1)S(1)} %pad_maximum_fusion.4), channel_id=1, source_target_pairs={{0,6},{1,7},{2,4},{3,5},{4,2},{5,3},{6,0},{7,1},{8,14},{9,15},{10,... | collective-permute-start | bytes 196616 | tf_op jit(solution)/shard_map/ppermute | solution.py:200
  9.5 0.0 collective-permute-done.14
  9.5 0.1 collective-permute-start.10
  9.6 0.0 collective-permute-done.15
  9.7 1.7 %collective-permute-start.17 = (bf16[4,128,256]{2,1,0:T(8,128)(2,1)S(1)}, bf16[4,128,256]{2,1,0:T(8,128)(2,1)S(1)}, u32[]{:S(2)}, u32[]{:S(2)}) collective-permute-start(bf16[4,128,256]{2,1,0:T(8,128)(2,1)S(1)} %pad_maximum_fusion.1.refs_8_), channel_id=1, source_target_pairs={{0,8},{8,16},{16,24},{24,0},{1,9},{9,17},{17,25},{25,1},{2,10},{10... | collective-permute-start | bytes 786440 | tf_op jit(solution)/shard_map/ppermute | solution.py:226
  11.4 0.0 collective-permute-done.7
  11.4 0.0 collective-permute-done.8
  11.4 0.8 collective-permute-done.9
  12.2 2.4 %collective-permute-done.10 = bf16[128,256]{1,0:T(8,128)(2,1)S(1)} collective-permute-done((bf16[128,256]{1,0:T(8,128)(2,1)S(1)}, bf16[128,256]{1,0:T(8,128)(2,1)S(1)}, u32[]{:S(2)}, u32[]{:S(2)}) %collective-permute-start.10) | collective-permute-done | bytes 65568 | tf_op jit(solution)/shard_map/ppermute | solution.py:200
  14.6 0.0 copy-start.10
  14.6 1.6 %collective-permute-start.11 = (bf16[4,128,256]{2,1,0:T(8,128)(2,1)S(1)}, bf16[4,128,256]{2,1,0:T(8,128)(2,1)S(1)}, u32[]{:S(2)}, u32[]{:S(2)}) collective-permute-start(bf16[4,128,256]{2,1,0:T(8,128)(2,1)S(1)} %pad_maximum_fusion.refs_8_), channel_id=1, source_target_pairs={{0,8},{8,16},{16,24},{24,0},{1,9},{9,17},{17,25},{25,1},{2,10},{10... | collective-permute-start | bytes 786440 | tf_op jit(solution)/shard_map/ppermute | solution.py:226
  16.2 0.7 constant_dynamic-slice_fusion.16
  17.0 0.5 collective-permute-start.1
  17.4 1.4 %collective-permute-start.2 = (bf16[128,512]{1,0:T(8,128)(2,1)S(1)}, bf16[128,512]{1,0:T(8,128)(2,1)S(1)}, u32[]{:S(2)}, u32[]{:S(2)}) collective-permute-start(bf16[128,512]{1,0:T(8,128)(2,1)S(1)} %get-tuple-element.36), channel_id=1, source_target_pairs={{0,3},{1,2},{2,1},{3,0},{4,7},{5,6},{6,5},{7,4},{8,11},{9,10},{10,... | collective-permute-start | bytes 393224 | tf_op jit(solution)/shard_map/ppermute | solution.py:200
  18.8 1.9 %collective-permute-done.17.refs_9_ = bf16[4,128,256]{2,1,0:T(8,128)(2,1)S(1)} collective-permute-done((bf16[4,128,256]{2,1,0:T(8,128)(2,1)S(1)}, bf16[4,128,256]{2,1,0:T(8,128)(2,1)S(1)}, u32[]{:S(2)}, u32[]{:S(2)}) %collective-permute-start.17) | collective-permute-done | bytes 262176 | tf_op jit(solution)/shard_map/ppermute | solution.py:226
  20.7 0.0 collective-permute-start.18
  20.7 5.6 %collective-permute-done.11.refs_9_ = bf16[4,128,256]{2,1,0:T(8,128)(2,1)S(1)} collective-permute-done((bf16[4,128,256]{2,1,0:T(8,128)(2,1)S(1)}, bf16[4,128,256]{2,1,0:T(8,128)(2,1)S(1)}, u32[]{:S(2)}, u32[]{:S(2)}) %collective-permute-start.11) | collective-permute-done | bytes 262176 | tf_op jit(solution)/shard_map/ppermute | solution.py:226
  26.3 0.0 collective-permute-start.12
  26.3 1.7 %collective-permute-start.3 = (bf16[128,512]{1,0:T(8,128)(2,1)S(1)}, bf16[128,512]{1,0:T(8,128)(2,1)S(1)}, u32[]{:S(2)}, u32[]{:S(2)}) collective-permute-start(bf16[128,512]{1,0:T(8,128)(2,1)S(1)} %get-tuple-element.35), channel_id=1, source_target_pairs={{0,4},{1,5},{2,6},{3,7},{4,0},{5,1},{6,2},{7,3},{8,12},{9,13},{10,... | collective-permute-start | bytes 393224 | tf_op jit(solution)/shard_map/ppermute | solution.py:200
  28.0 0.0 collective-permute-done.2.refs_3_
  28.1 1.5 %collective-permute-start.5 = (bf16[128,512]{1,0:T(8,128)(2,1)S(1)}, bf16[128,512]{1,0:T(8,128)(2,1)S(1)}, u32[]{:S(2)}, u32[]{:S(2)}) collective-permute-start(bf16[128,512]{1,0:T(8,128)(2,1)S(1)} %get-tuple-element.40), channel_id=1, source_target_pairs={{0,6},{1,7},{2,4},{3,5},{4,2},{5,3},{6,0},{7,1},{8,14},{9,15},{10,... | collective-permute-start | bytes 393224 | tf_op jit(solution)/shard_map/ppermute | solution.py:200
  29.6 5.0 %collective-permute-done.3.refs_4_ = bf16[128,512]{1,0:T(8,128)(2,1)S(1)} collective-permute-done((bf16[128,512]{1,0:T(8,128)(2,1)S(1)}, bf16[128,512]{1,0:T(8,128)(2,1)S(1)}, u32[]{:S(2)}, u32[]{:S(2)}) %collective-permute-start.3) | collective-permute-done | bytes 131104 | tf_op jit(solution)/shard_map/ppermute | solution.py:200
  34.6 0.6 pad_add_fusion.place_ref
  35.2 0.0 collective-permute-done.18.refs_10_
  35.2 1.4 %collective-permute-start.19 = (bf16[4,128,256]{2,1,0:T(8,128)(2,1)S(1)}, bf16[4,128,256]{2,1,0:T(8,128)(2,1)S(1)}, u32[]{:S(2)}, u32[]{:S(2)}) collective-permute-start(bf16[4,128,256]{2,1,0:T(8,128)(2,1)S(1)} %collective-permute-done.18.refs_10_), channel_id=1, source_target_pairs={{0,8},{8,16},{16,24},{24,0},{1,9},{9,17},{17,25},{25,1},{2,10},{10... | collective-permute-start | bytes 786440 | tf_op jit(solution)/shard_map/ppermute | solution.py:226
  36.6 0.6 collective-permute-done.12.refs_10_
  37.1 1.0 collective-permute-start.13
  38.1 0.0 collective-permute-done.4.refs_5_
  38.2 0.0 collective-permute-done.5.refs_6_
  38.2 1.9 %collective-permute-done.6.refs_7_ = bf16[128,512]{1,0:T(8,128)(2,1)S(1)} collective-permute-done((bf16[128,512]{1,0:T(8,128)(2,1)S(1)}, bf16[128,512]{1,0:T(8,128)(2,1)S(1)}, u32[]{:S(2)}, u32[]{:S(2)}) %collective-permute-start.6) | collective-permute-done | bytes 131104 | tf_op jit(solution)/shard_map/ppermute | solution.py:200
  40.1 0.6 copy-done.6
  40.7 12.2 %shard_map.46 = (f32[8,128,512]{2,1,0:T(8,128)}, f32[8,8,512]{2,1,0:T(8,128)}) custom-call(s32[3]{0:T(128)} %pad_add_fusion.place_ref, s32[16]{0:T(128)} %lengths_ref.9, bf16[128,512]{1,0:T(8,128)(2,1)} %get-tuple-element.39.refs_0_, bf16[128,512]{1,0:T(8,128)(2,1)} %copy-done, bf16[128,512]{1,0:T(8,128)(2,1)} %copy-done.1, bf16[128,512]{1,0:T(8,128)(2,1)} %copy-done.2, ...), custom_call_target="tpu_custom_call" | custom-call | flops 1610612736 | bytes 2097152 | tf_op jit(solution)/shard_map/pallas_call | solution.py:176
  53.0 9.9 %shard_map.47 = (f32[8,128,512]{2,1,0:T(8,128)}, f32[8,8,512]{2,1,0:T(8,128)}) custom-call(s32[3]{0:T(128)} %pad_add_fusion.place_ref, s32[16]{0:T(128)} %lengths_ref.9, bf16[128,512]{1,0:T(8,128)(2,1)} %get-tuple-element.39.refs_0_, bf16[128,512]{1,0:T(8,128)(2,1)} %copy-done, ...), custom_call_target="tpu_custom_call", output_to_operand_aliasing={{0}: (13, {}), {1}: (14, {})} | custom-call | flops 1610612736 | bytes 2097152 | tf_op jit(solution)/shard_map/pallas_call | solution.py:176
  62.9 0.0 copy-start.11
  62.9 0.7 copy-done.11
  63.6 10.3 %shard_map.48 = (f32[8,128,512]{2,1,0:T(8,128)}, f32[8,8,512]{2,1,0:T(8,128)}) custom-call(s32[3]{0:T(128)} %pad_add_fusion.place_ref, s32[16]{0:T(128)} %lengths_ref.9, bf16[128,512]{1,0:T(8,128)(2,1)} %get-tuple-element.39.refs_0_, bf16[128,512]{1,0:T(8,128)(2,1)} %copy-done, ...), custom_call_target="tpu_custom_call", output_to_operand_aliasing={{0}: (11, {}), {1}: (12, {})} | custom-call | flops 536870912 | bytes 2097152 | tf_op jit(solution)/shard_map/pallas_call | solution.py:176
  73.9 0.0 collective-permute-done.13.refs_8_
  73.9 0.0 copy-start.8
  73.9 0.7 copy-done.8
  74.6 7.7 %shard_map.50 = (bf16[128,512]{1,0:T(8,128)(2,1)}, bf16[128,512]{1,0:T(8,128)(2,1)}, bf16[128,512]{1,0:T(8,128)(2,1)}, bf16[128,512]{1,0:T(8,128)(2,1)}) custom-call(s32[3]{0:T(128)} %pad_add_fusion.place_ref, s32[16]{0:T(128)} %lengths_ref.9, bf16[128,512]{1,0:T(8,128)(2,1)} %get-tuple-element.39.refs_0_, bf16[128,512]{1,0:T(8,128)(2,1)} %copy-done, ...), custom_call_target="tpu_custom_call" | custom-call | flops 268435456 | bytes 2097152 | tf_op jit(solution)/shard_map/pallas_call | solution.py:176
  82.3 0.1 collective-permute-start.23
  82.4 4.4 %shard_map.49 = (bf16[128,512]{1,0:T(8,128)(2,1)}, bf16[128,512]{1,0:T(8,128)(2,1)}, bf16[128,512]{1,0:T(8,128)(2,1)}, bf16[128,512]{1,0:T(8,128)(2,1)}) custom-call(s32[3]{0:T(128)} %pad_add_fusion.place_ref, s32[16]{0:T(128)} %lengths_ref.9, bf16[128,512]{1,0:T(8,128)(2,1)} %get-tuple-element.39.refs_0_, bf16[128,512]{1,0:T(8,128)(2,1)} %copy-done, ...), custom_call_target="tpu_custom_call" | custom-call | flops 268435456 | bytes 2097152 | tf_op jit(solution)/shard_map/pallas_call | solution.py:176
  86.9 1.4 %collective-permute-start.20 = (bf16[128,512]{1,0:T(8,128)(2,1)}, bf16[128,512]{1,0:T(8,128)(2,1)S(1)}, u32[]{:S(2)}, u32[]{:S(2)}) collective-permute-start(bf16[128,512]{1,0:T(8,128)(2,1)} %get-tuple-element.26), channel_id=1, source_target_pairs={{0,1},{1,0},{2,3},{3,2},{4,5},{5,4},{6,7},{7,6},{8,9},{9,8},{10,11... | collective-permute-start | bytes 393224 | tf_op jit(solution)/shard_map/ppermute | solution.py:200
  88.3 1.5 %collective-permute-start.21 = (bf16[128,512]{1,0:T(8,128)(2,1)}, bf16[128,512]{1,0:T(8,128)(2,1)S(1)}, u32[]{:S(2)}, u32[]{:S(2)}) collective-permute-start(bf16[128,512]{1,0:T(8,128)(2,1)} %get-tuple-element.27), channel_id=1, source_target_pairs={{0,2},{1,3},{2,0},{3,1},{4,6},{5,7},{6,4},{7,5},{8,10},{9,11},{10,... | collective-permute-start | bytes 393224 | tf_op jit(solution)/shard_map/ppermute | solution.py:200
  89.8 0.0 collective-permute-start.22
  89.9 4.3 %collective-permute-start.24 = (bf16[128,512]{1,0:T(8,128)(2,1)S(1)}, bf16[128,512]{1,0:T(8,128)(2,1)S(1)}, u32[]{:S(2)}, u32[]{:S(2)}) collective-permute-start(bf16[128,512]{1,0:T(8,128)(2,1)S(1)} %copy-done.19), channel_id=1, source_target_pairs={{0,5},{1,4},{2,7},{3,6},{4,1},{5,0},{6,3},{7,2},{8,13},{9,12},{10,... | collective-permute-start | bytes 393224 | tf_op jit(solution)/shard_map/ppermute | solution.py:200
  94.2 0.9 bitcast_dynamic-update-slice_fusion.15
  95.1 1.3 %collective-permute-start.25 = (bf16[128,512]{1,0:T(8,128)(2,1)S(1)}, bf16[128,512]{1,0:T(8,128)(2,1)S(1)}, u32[]{:S(2)}, u32[]{:S(2)}) collective-permute-start(bf16[128,512]{1,0:T(8,128)(2,1)S(1)} %copy-done.18), channel_id=1, source_target_pairs={{0,6},{1,7},{2,4},{3,5},{4,2},{5,3},{6,0},{7,1},{8,14},{9,15},{10,... | collective-permute-start | bytes 393224 | tf_op jit(solution)/shard_map/ppermute | solution.py:200
  96.5 0.0 collective-permute-done.21
  96.5 2.4 %collective-permute-start.26 = (bf16[128,512]{1,0:T(8,128)(2,1)S(1)}, bf16[128,512]{1,0:T(8,128)(2,1)S(1)}, u32[]{:S(2)}, u32[]{:S(2)}) collective-permute-start(bf16[128,512]{1,0:T(8,128)(2,1)S(1)} %copy-done.17), channel_id=1, source_target_pairs={{0,7},{1,6},{2,5},{3,4},{4,3},{5,2},{6,1},{7,0},{8,15},{9,14},{10,... | collective-permute-start | bytes 393224 | tf_op jit(solution)/shard_map/ppermute | solution.py:200
  98.9 0.0 collective-permute-done.22
  99.0 4.3 %collective-permute-done.24 = bf16[128,512]{1,0:T(8,128)(2,1)S(1)} collective-permute-done((bf16[128,512]{1,0:T(8,128)(2,1)S(1)}, bf16[128,512]{1,0:T(8,128)(2,1)S(1)}, u32[]{:S(2)}, u32[]{:S(2)}) %collective-permute-start.24) | collective-permute-done | bytes 131104 | tf_op jit(solution)/shard_map/ppermute | solution.py:200
  103.2 0.8 collective-permute-done.25
  104.1 1.8 %collective-permute-done.26 = bf16[128,512]{1,0:T(8,128)(2,1)S(1)} collective-permute-done((bf16[128,512]{1,0:T(8,128)(2,1)S(1)}, bf16[128,512]{1,0:T(8,128)(2,1)S(1)}, u32[]{:S(2)}, u32[]{:S(2)}) %collective-permute-start.26) | collective-permute-done | bytes 131104 | tf_op jit(solution)/shard_map/ppermute | solution.py:200
  106.1 0.0 copy-start.12
  106.1 1.0 copy-done.12
  107.1 0.7 bitcast_dynamic-update-slice_fusion
  (64 shorter events, 0.4 us)
Async XLA Ops:
  0.0 16.2 %copy-start.7 = (bf16[128,4096]{1,0:T(8,128)(2,1)S(1)}, bf16[128,4096]{1,0:T(8,128)(2,1)}, u32[]{:S(2)}) copy-start(bf16[128,4096]{1,0:T(8,128)(2,1)} %param.4) | copy-start | bytes 3145732
  1.2 5.7 %collective-permute-start.16 = (bf16[128,256]{1,0:T(8,128)(2,1)S(1)}, bf16[128,256]{1,0:T(8,128)(2,1)S(1)}, u32[]{:S(2)}, u32[]{:S(2)}) collective-permute-start(bf16[128,256]{1,0:T(8,128)(2,1)S(1)} %pad_maximum_fusion.8), channel_id=1, source_target_pairs={{0,3},{1,2},{2,1},{3,0},{4,7},{5,6},{6,5},{7,4},{8,11},{9,10},{10,... | collective-permute-start | bytes 196616 | tf_op jit(solution)/shard_map/ppermute | solution.py:200
  3.6 5.9 %collective-permute-start.14 = (bf16[128,256]{1,0:T(8,128)(2,1)S(1)}, bf16[128,256]{1,0:T(8,128)(2,1)S(1)}, u32[]{:S(2)}, u32[]{:S(2)}) collective-permute-start(bf16[128,256]{1,0:T(8,128)(2,1)S(1)} %pad_maximum_fusion.6), channel_id=1, source_target_pairs={{0,1},{1,0},{2,3},{3,2},{4,5},{5,4},{6,7},{7,6},{8,9},{9,8},{10,11... | collective-permute-start | bytes 196616 | tf_op jit(solution)/shard_map/ppermute | solution.py:200
  4.4 5.2 %collective-permute-start.15 = (bf16[128,256]{1,0:T(8,128)(2,1)S(1)}, bf16[128,256]{1,0:T(8,128)(2,1)S(1)}, u32[]{:S(2)}, u32[]{:S(2)}) collective-permute-start(bf16[128,256]{1,0:T(8,128)(2,1)S(1)} %pad_maximum_fusion.7), channel_id=1, source_target_pairs={{0,2},{1,3},{2,0},{3,1},{4,6},{5,7},{6,4},{7,5},{8,10},{9,11},{10,... | collective-permute-start | bytes 196616 | tf_op jit(solution)/shard_map/ppermute | solution.py:200
  4.5 6.9 %collective-permute-start.7 = (bf16[128,256]{1,0:T(8,128)(2,1)S(1)}, bf16[128,256]{1,0:T(8,128)(2,1)S(1)}, u32[]{:S(2)}, u32[]{:S(2)}) collective-permute-start(bf16[128,256]{1,0:T(8,128)(2,1)S(1)} %pad_maximum_fusion.2), channel_id=1, source_target_pairs={{0,4},{1,5},{2,6},{3,7},{4,0},{5,1},{6,2},{7,3},{8,12},{9,13},{10,... | collective-permute-start | bytes 196616 | tf_op jit(solution)/shard_map/ppermute | solution.py:200
  6.6 4.8 %collective-permute-start.8 = (bf16[128,256]{1,0:T(8,128)(2,1)S(1)}, bf16[128,256]{1,0:T(8,128)(2,1)S(1)}, u32[]{:S(2)}, u32[]{:S(2)}) collective-permute-start(bf16[128,256]{1,0:T(8,128)(2,1)S(1)} %pad_maximum_fusion.3), channel_id=1, source_target_pairs={{0,5},{1,4},{2,7},{3,6},{4,1},{5,0},{6,3},{7,2},{8,13},{9,12},{10,... | collective-permute-start | bytes 196616 | tf_op jit(solution)/shard_map/ppermute | solution.py:200
  6.9 5.3 %collective-permute-start.9 = (bf16[128,256]{1,0:T(8,128)(2,1)S(1)}, bf16[128,256]{1,0:T(8,128)(2,1)S(1)}, u32[]{:S(2)}, u32[]{:S(2)}) collective-permute-start(bf16[128,256]{1,0:T(8,128)(2,1)S(1)} %pad_maximum_fusion.4), channel_id=1, source_target_pairs={{0,6},{1,7},{2,4},{3,5},{4,2},{5,3},{6,0},{7,1},{8,14},{9,15},{10,... | collective-permute-start | bytes 196616 | tf_op jit(solution)/shard_map/ppermute | solution.py:200
  9.5 5.0 %collective-permute-start.10 = (bf16[128,256]{1,0:T(8,128)(2,1)S(1)}, bf16[128,256]{1,0:T(8,128)(2,1)S(1)}, u32[]{:S(2)}, u32[]{:S(2)}) collective-permute-start(bf16[128,256]{1,0:T(8,128)(2,1)S(1)} %pad_maximum_fusion.5), channel_id=1, source_target_pairs={{0,7},{1,6},{2,5},{3,4},{4,3},{5,2},{6,1},{7,0},{8,15},{9,14},{10,... | collective-permute-start | bytes 196616 | tf_op jit(solution)/shard_map/ppermute | solution.py:200
  9.6 30.4 %copy-start.9 = (bf16[4,128,256]{2,1,0:T(8,128)(2,1)}, bf16[4,128,256]{2,1,0:T(8,128)(2,1)S(1)}, u32[]{:S(2)}) copy-start(bf16[4,128,256]{2,1,0:T(8,128)(2,1)S(1)} %pad_maximum_fusion.1.refs_8_) | copy-start | bytes 786436
  9.7 11.0 %collective-permute-start.17 = (bf16[4,128,256]{2,1,0:T(8,128)(2,1)S(1)}, bf16[4,128,256]{2,1,0:T(8,128)(2,1)S(1)}, u32[]{:S(2)}, u32[]{:S(2)}) collective-permute-start(bf16[4,128,256]{2,1,0:T(8,128)(2,1)S(1)} %pad_maximum_fusion.1.refs_8_), channel_id=1, source_target_pairs={{0,8},{8,16},{16,24},{24,0},{1,9},{9,17},{17,25},{25,1},{2,10},{10... | collective-permute-start | bytes 786440 | tf_op jit(solution)/shard_map/ppermute | solution.py:226
  14.6 38.4 %copy-start.10 = (bf16[4,128,256]{2,1,0:T(8,128)(2,1)}, bf16[4,128,256]{2,1,0:T(8,128)(2,1)S(1)}, u32[]{:S(2)}) copy-start(bf16[4,128,256]{2,1,0:T(8,128)(2,1)S(1)} %pad_maximum_fusion.refs_8_) | copy-start | bytes 786436
  14.6 11.7 %collective-permute-start.11 = (bf16[4,128,256]{2,1,0:T(8,128)(2,1)S(1)}, bf16[4,128,256]{2,1,0:T(8,128)(2,1)S(1)}, u32[]{:S(2)}, u32[]{:S(2)}) collective-permute-start(bf16[4,128,256]{2,1,0:T(8,128)(2,1)S(1)} %pad_maximum_fusion.refs_8_), channel_id=1, source_target_pairs={{0,8},{8,16},{16,24},{24,0},{1,9},{9,17},{17,25},{25,1},{2,10},{10... | collective-permute-start | bytes 786440 | tf_op jit(solution)/shard_map/ppermute | solution.py:226
  17.0 9.4 %collective-permute-start = (bf16[128,512]{1,0:T(8,128)(2,1)S(1)}, bf16[128,512]{1,0:T(8,128)(2,1)S(1)}, u32[]{:S(2)}, u32[]{:S(2)}) collective-permute-start(bf16[128,512]{1,0:T(8,128)(2,1)S(1)} %get-tuple-element.38), channel_id=1, source_target_pairs={{0,1},{1,0},{2,3},{3,2},{4,5},{5,4},{6,7},{7,6},{8,9},{9,8},{10,11... | collective-permute-start | bytes 393224 | tf_op jit(solution)/shard_map/ppermute | solution.py:200
  17.0 11.1 %collective-permute-start.1 = (bf16[128,512]{1,0:T(8,128)(2,1)S(1)}, bf16[128,512]{1,0:T(8,128)(2,1)S(1)}, u32[]{:S(2)}, u32[]{:S(2)}) collective-permute-start(bf16[128,512]{1,0:T(8,128)(2,1)S(1)} %get-tuple-element.37), channel_id=1, source_target_pairs={{0,2},{1,3},{2,0},{3,1},{4,6},{5,7},{6,4},{7,5},{8,10},{9,11},{10,... | collective-permute-start | bytes 393224 | tf_op jit(solution)/shard_map/ppermute | solution.py:200
  17.4 10.6 %collective-permute-start.2 = (bf16[128,512]{1,0:T(8,128)(2,1)S(1)}, bf16[128,512]{1,0:T(8,128)(2,1)S(1)}, u32[]{:S(2)}, u32[]{:S(2)}) collective-permute-start(bf16[128,512]{1,0:T(8,128)(2,1)S(1)} %get-tuple-element.36), channel_id=1, source_target_pairs={{0,3},{1,2},{2,1},{3,0},{4,7},{5,6},{6,5},{7,4},{8,11},{9,10},{10,... | collective-permute-start | bytes 393224 | tf_op jit(solution)/shard_map/ppermute | solution.py:200
  20.7 19.4 %copy-start.13 = (bf16[4,128,256]{2,1,0:T(8,128)(2,1)}, bf16[4,128,256]{2,1,0:T(8,128)(2,1)S(1)}, u32[]{:S(2)}) copy-start(bf16[4,128,256]{2,1,0:T(8,128)(2,1)S(1)} %collective-permute-done.17.refs_9_) | copy-start | bytes 786436
  20.7 14.5 %collective-permute-start.18 = (bf16[4,128,256]{2,1,0:T(8,128)(2,1)S(1)}, bf16[4,128,256]{2,1,0:T(8,128)(2,1)S(1)}, u32[]{:S(2)}, u32[]{:S(2)}) collective-permute-start(bf16[4,128,256]{2,1,0:T(8,128)(2,1)S(1)} %collective-permute-done.17.refs_9_), channel_id=1, source_target_pairs={{0,8},{8,16},{16,24},{24,0},{1,9},{9,17},{17,25},{25,1},{2,10},{10... | collective-permute-start | bytes 786440 | tf_op jit(solution)/shard_map/ppermute | solution.py:226
  26.3 26.6 %copy-start.14 = (bf16[4,128,256]{2,1,0:T(8,128)(2,1)}, bf16[4,128,256]{2,1,0:T(8,128)(2,1)S(1)}, u32[]{:S(2)}) copy-start(bf16[4,128,256]{2,1,0:T(8,128)(2,1)S(1)} %collective-permute-done.11.refs_9_) | copy-start | bytes 786436
  26.3 10.8 %collective-permute-start.12 = (bf16[4,128,256]{2,1,0:T(8,128)(2,1)S(1)}, bf16[4,128,256]{2,1,0:T(8,128)(2,1)S(1)}, u32[]{:S(2)}, u32[]{:S(2)}) collective-permute-start(bf16[4,128,256]{2,1,0:T(8,128)(2,1)S(1)} %collective-permute-done.11.refs_9_), channel_id=1, source_target_pairs={{0,8},{8,16},{16,24},{24,0},{1,9},{9,17},{17,25},{25,1},{2,10},{10... | collective-permute-start | bytes 786440 | tf_op jit(solution)/shard_map/ppermute | solution.py:226
  26.3 13.8 %copy-start = (bf16[128,512]{1,0:T(8,128)(2,1)}, bf16[128,512]{1,0:T(8,128)(2,1)S(1)}, u32[]{:S(2)}) copy-start(bf16[128,512]{1,0:T(8,128)(2,1)S(1)} %collective-permute-done.refs_1_) | copy-start | bytes 393220
  26.3 8.2 %collective-permute-start.3 = (bf16[128,512]{1,0:T(8,128)(2,1)S(1)}, bf16[128,512]{1,0:T(8,128)(2,1)S(1)}, u32[]{:S(2)}, u32[]{:S(2)}) collective-permute-start(bf16[128,512]{1,0:T(8,128)(2,1)S(1)} %get-tuple-element.35), channel_id=1, source_target_pairs={{0,4},{1,5},{2,6},{3,7},{4,0},{5,1},{6,2},{7,3},{8,12},{9,13},{10,... | collective-permute-start | bytes 393224 | tf_op jit(solution)/shard_map/ppermute | solution.py:200
  28.0 12.1 %copy-start.1 = (bf16[128,512]{1,0:T(8,128)(2,1)}, bf16[128,512]{1,0:T(8,128)(2,1)S(1)}, u32[]{:S(2)}) copy-start(bf16[128,512]{1,0:T(8,128)(2,1)S(1)} %collective-permute-done.1.refs_2_) | copy-start | bytes 393220
  28.0 10.1 %collective-permute-start.4 = (bf16[128,512]{1,0:T(8,128)(2,1)S(1)}, bf16[128,512]{1,0:T(8,128)(2,1)S(1)}, u32[]{:S(2)}, u32[]{:S(2)}) collective-permute-start(bf16[128,512]{1,0:T(8,128)(2,1)S(1)} %get-tuple-element.34), channel_id=1, source_target_pairs={{0,5},{1,4},{2,7},{3,6},{4,1},{5,0},{6,3},{7,2},{8,13},{9,12},{10,... | collective-permute-start | bytes 393224 | tf_op jit(solution)/shard_map/ppermute | solution.py:200
  28.0 12.0 %copy-start.2 = (bf16[128,512]{1,0:T(8,128)(2,1)}, bf16[128,512]{1,0:T(8,128)(2,1)S(1)}, u32[]{:S(2)}) copy-start(bf16[128,512]{1,0:T(8,128)(2,1)S(1)} %collective-permute-done.2.refs_3_) | copy-start | bytes 393220
  28.1 10.1 %collective-permute-start.5 = (bf16[128,512]{1,0:T(8,128)(2,1)S(1)}, bf16[128,512]{1,0:T(8,128)(2,1)S(1)}, u32[]{:S(2)}, u32[]{:S(2)}) collective-permute-start(bf16[128,512]{1,0:T(8,128)(2,1)S(1)} %get-tuple-element.40), channel_id=1, source_target_pairs={{0,6},{1,7},{2,4},{3,5},{4,2},{5,3},{6,0},{7,1},{8,14},{9,15},{10,... | collective-permute-start | bytes 393224 | tf_op jit(solution)/shard_map/ppermute | solution.py:200
  34.5 5.6 %copy-start.3 = (bf16[128,512]{1,0:T(8,128)(2,1)}, bf16[128,512]{1,0:T(8,128)(2,1)S(1)}, u32[]{:S(2)}) copy-start(bf16[128,512]{1,0:T(8,128)(2,1)S(1)} %collective-permute-done.3.refs_4_) | copy-start | bytes 393220
  34.5 5.5 %collective-permute-start.6 = (bf16[128,512]{1,0:T(8,128)(2,1)S(1)}, bf16[128,512]{1,0:T(8,128)(2,1)S(1)}, u32[]{:S(2)}, u32[]{:S(2)}) collective-permute-start(bf16[128,512]{1,0:T(8,128)(2,1)S(1)} %get-tuple-element.33), channel_id=1, source_target_pairs={{0,7},{1,6},{2,5},{3,4},{4,3},{5,2},{6,1},{7,0},{8,15},{9,14},{10,... | collective-permute-start | bytes 393224 | tf_op jit(solution)/shard_map/ppermute | solution.py:200
  35.2 4.9 %copy-start.16 = (bf16[4,128,256]{2,1,0:T(8,128)(2,1)}, bf16[4,128,256]{2,1,0:T(8,128)(2,1)S(1)}, u32[]{:S(2)}) copy-start(bf16[4,128,256]{2,1,0:T(8,128)(2,1)S(1)} %collective-permute-done.18.refs_10_) | copy-start | bytes 786436
  35.2 27.7 %collective-permute-start.19 = (bf16[4,128,256]{2,1,0:T(8,128)(2,1)S(1)}, bf16[4,128,256]{2,1,0:T(8,128)(2,1)S(1)}, u32[]{:S(2)}, u32[]{:S(2)}) collective-permute-start(bf16[4,128,256]{2,1,0:T(8,128)(2,1)S(1)} %collective-permute-done.18.refs_10_), channel_id=1, source_target_pairs={{0,8},{8,16},{16,24},{24,0},{1,9},{9,17},{17,25},{25,1},{2,10},{10... | collective-permute-start | bytes 786440 | tf_op jit(solution)/shard_map/ppermute | solution.py:226
  37.1 15.8 %copy-start.15 = (bf16[4,128,256]{2,1,0:T(8,128)(2,1)}, bf16[4,128,256]{2,1,0:T(8,128)(2,1)S(1)}, u32[]{:S(2)}) copy-start(bf16[4,128,256]{2,1,0:T(8,128)(2,1)S(1)} %collective-permute-done.12.refs_10_) | copy-start | bytes 786436
  37.1 36.8 %collective-permute-start.13 = (bf16[4,128,256]{2,1,0:T(8,128)(2,1)S(1)}, bf16[4,128,256]{2,1,0:T(8,128)(2,1)S(1)}, u32[]{:S(2)}, u32[]{:S(2)}) collective-permute-start(bf16[4,128,256]{2,1,0:T(8,128)(2,1)S(1)} %collective-permute-done.12.refs_10_), channel_id=1, source_target_pairs={{0,8},{8,16},{16,24},{24,0},{1,9},{9,17},{17,25},{25,1},{2,10},{10... | collective-permute-start | bytes 786440 | tf_op jit(solution)/shard_map/ppermute | solution.py:226
  38.2 2.0 %copy-start.4 = (bf16[128,512]{1,0:T(8,128)(2,1)}, bf16[128,512]{1,0:T(8,128)(2,1)S(1)}, u32[]{:S(2)}) copy-start(bf16[128,512]{1,0:T(8,128)(2,1)S(1)} %collective-permute-done.4.refs_5_) | copy-start | bytes 393220
  38.2 2.0 %copy-start.5 = (bf16[128,512]{1,0:T(8,128)(2,1)}, bf16[128,512]{1,0:T(8,128)(2,1)S(1)}, u32[]{:S(2)}) copy-start(bf16[128,512]{1,0:T(8,128)(2,1)S(1)} %collective-permute-done.5.refs_6_) | copy-start | bytes 393220
  40.1 0.7 copy-start.6
  62.9 0.7 copy-start.11
  73.9 0.7 copy-start.8
  82.3 7.5 %copy-start.19 = (bf16[128,512]{1,0:T(8,128)(2,1)S(1)}, bf16[128,512]{1,0:T(8,128)(2,1)}, u32[]{:S(2)}) copy-start(bf16[128,512]{1,0:T(8,128)(2,1)} %get-tuple-element.30) | copy-start | bytes 393220
  82.3 12.8 %copy-start.18 = (bf16[128,512]{1,0:T(8,128)(2,1)S(1)}, bf16[128,512]{1,0:T(8,128)(2,1)}, u32[]{:S(2)}) copy-start(bf16[128,512]{1,0:T(8,128)(2,1)} %get-tuple-element.31) | copy-start | bytes 393220
  82.3 14.1 %copy-start.17 = (bf16[128,512]{1,0:T(8,128)(2,1)S(1)}, bf16[128,512]{1,0:T(8,128)(2,1)}, u32[]{:S(2)}) copy-start(bf16[128,512]{1,0:T(8,128)(2,1)} %get-tuple-element.32) | copy-start | bytes 393220
  82.3 16.6 %collective-permute-start.23 = (bf16[128,512]{1,0:T(8,128)(2,1)}, bf16[128,512]{1,0:T(8,128)(2,1)S(1)}, u32[]{:S(2)}, u32[]{:S(2)}) collective-permute-start(bf16[128,512]{1,0:T(8,128)(2,1)} %get-tuple-element.29), channel_id=1, source_target_pairs={{0,4},{1,5},{2,6},{3,7},{4,0},{5,1},{6,2},{7,3},{8,12},{9,13},{10,... | collective-permute-start | bytes 393224 | tf_op jit(solution)/shard_map/ppermute | solution.py:200
  86.9 8.2 %collective-permute-start.20 = (bf16[128,512]{1,0:T(8,128)(2,1)}, bf16[128,512]{1,0:T(8,128)(2,1)S(1)}, u32[]{:S(2)}, u32[]{:S(2)}) collective-permute-start(bf16[128,512]{1,0:T(8,128)(2,1)} %get-tuple-element.26), channel_id=1, source_target_pairs={{0,1},{1,0},{2,3},{3,2},{4,5},{5,4},{6,7},{7,6},{8,9},{9,8},{10,11... | collective-permute-start | bytes 393224 | tf_op jit(solution)/shard_map/ppermute | solution.py:200
  88.3 8.2 %collective-permute-start.21 = (bf16[128,512]{1,0:T(8,128)(2,1)}, bf16[128,512]{1,0:T(8,128)(2,1)S(1)}, u32[]{:S(2)}, u32[]{:S(2)}) collective-permute-start(bf16[128,512]{1,0:T(8,128)(2,1)} %get-tuple-element.27), channel_id=1, source_target_pairs={{0,2},{1,3},{2,0},{3,1},{4,6},{5,7},{6,4},{7,5},{8,10},{9,11},{10,... | collective-permute-start | bytes 393224 | tf_op jit(solution)/shard_map/ppermute | solution.py:200
  89.8 9.1 %collective-permute-start.22 = (bf16[128,512]{1,0:T(8,128)(2,1)}, bf16[128,512]{1,0:T(8,128)(2,1)S(1)}, u32[]{:S(2)}, u32[]{:S(2)}) collective-permute-start(bf16[128,512]{1,0:T(8,128)(2,1)} %get-tuple-element.28), channel_id=1, source_target_pairs={{0,3},{1,2},{2,1},{3,0},{4,7},{5,6},{6,5},{7,4},{8,11},{9,10},{10,... | collective-permute-start | bytes 393224 | tf_op jit(solution)/shard_map/ppermute | solution.py:200
  89.9 13.4 %collective-permute-start.24 = (bf16[128,512]{1,0:T(8,128)(2,1)S(1)}, bf16[128,512]{1,0:T(8,128)(2,1)S(1)}, u32[]{:S(2)}, u32[]{:S(2)}) collective-permute-start(bf16[128,512]{1,0:T(8,128)(2,1)S(1)} %copy-done.19), channel_id=1, source_target_pairs={{0,5},{1,4},{2,7},{3,6},{4,1},{5,0},{6,3},{7,2},{8,13},{9,12},{10,... | collective-permute-start | bytes 393224 | tf_op jit(solution)/shard_map/ppermute | solution.py:200
  95.1 8.9 %collective-permute-start.25 = (bf16[128,512]{1,0:T(8,128)(2,1)S(1)}, bf16[128,512]{1,0:T(8,128)(2,1)S(1)}, u32[]{:S(2)}, u32[]{:S(2)}) collective-permute-start(bf16[128,512]{1,0:T(8,128)(2,1)S(1)} %copy-done.18), channel_id=1, source_target_pairs={{0,6},{1,7},{2,4},{3,5},{4,2},{5,3},{6,0},{7,1},{8,14},{9,15},{10,... | collective-permute-start | bytes 393224 | tf_op jit(solution)/shard_map/ppermute | solution.py:200
  96.5 9.4 %collective-permute-start.26 = (bf16[128,512]{1,0:T(8,128)(2,1)S(1)}, bf16[128,512]{1,0:T(8,128)(2,1)S(1)}, u32[]{:S(2)}, u32[]{:S(2)}) collective-permute-start(bf16[128,512]{1,0:T(8,128)(2,1)S(1)} %copy-done.17), channel_id=1, source_target_pairs={{0,7},{1,6},{2,5},{3,4},{4,3},{5,2},{6,1},{7,0},{8,15},{9,14},{10,... | collective-permute-start | bytes 393224 | tf_op jit(solution)/shard_map/ppermute | solution.py:200
  106.1 1.0 copy-start.12
where the time goes:
time: 108 us
  Pallas kernels  44.5 us (41%)
  starting transfers between devices  30.2 us (28%)
  waiting for transfers between devices  25 us (23%)
  local copies, waits for them, and re-layouts  6.66 us (6%)
    pallas_call x5, Pallas kernels, attend(): pl.pallas_call(functools.partial(attend_kernel, tuple(steps), half, back,...  44.5 us
    ppermute x21, starting transfers between devices, swap(): return lax.ppermute(block, 'doc', [(i, i ^ k) for i in range(length)])  24.4 us
    ppermute x21, waiting for transfers between devices, swap(): return lax.ppermute(block, 'doc', [(i, i ^ k) for i in range(length)])  17 us
    ppermute x6, waiting for transfers between devices, on_device(): units[half].append(lax.ppermute(units[half][-1], 'head', ring))  8.04 us
    ppermute x6, starting transfers between devices, on_device(): units[half].append(lax.ppermute(units[half][-1], 'head', ring))  5.8 us
    unnamed x54, local copies, waits for them, and re-layouts  4.12 us
  transfers between devices with their start and end apart: 27, of which 10 were waited for; matrix products, arithmetic and copies ran while one was open for 2% of the time, Pallas kernels for 34%

commit v1 on v0

v1 whole, which is shorter than its diff:
```python
import functools
import math

import jax
import jax.numpy as jnp
from jax import lax
from jax.experimental import pallas as pl
from jax.experimental.pallas import tpu as pltpu
from jax.sharding import PartitionSpec as P

KEY_VALUE_HEADS = 8
HEAD_SIZE = 128
NEGATIVE = -1e30
HALVES = 2


def attend_kernel(half, back, slots, opening, closing, parts, place_ref, bounds_ref, firsts_ref, *refs):
    width = KEY_VALUE_HEADS
    count = len(slots)
    q_refs, refs = refs[:count], refs[count:]
    units, refs = refs[:parts], refs[parts:]
    if not opening:
        acc_in, stat_in = refs[:2]
        refs = refs[2:]
    if closing:
        out_refs, refs = refs[:count], refs[count:]
        acc_ref, stat_ref, q_ref, out_ref, sem = refs
    else:
        acc_out, stat_out, acc_ref, stat_ref, q_ref = refs
    rows, columns = q_refs[0].shape
    heads = columns // HEAD_SIZE
    lanes = heads * rows
    shard = parts * rows
    chunk = width // HALVES
    depth = place_ref[0]
    member = place_ref[1]
    group = place_ref[2]
    scale = math.log2(math.e) / math.sqrt(HEAD_SIZE)

    for i in range(count):
        for h in range(heads):
            q_ref[i, h * rows : (h + 1) * rows, :] = q_refs[i][:, h * HEAD_SIZE : (h + 1) * HEAD_SIZE]

    def one_block(turn, _):
        slot = slots[0] + turn
        doc = jnp.bitwise_xor(member, slot)
        root = ((group * width + doc) * parts + depth) * rows
        at = root + lax.broadcasted_iota(jnp.int32, (1, rows), 1)
        low = bounds_ref[slot, 0]
        high = bounds_ref[slot, 1]
        if opening:
            acc_ref[...] = jnp.zeros_like(acc_ref)
            stat_ref[0:1, :] = jnp.full((1, lanes), NEGATIVE, jnp.float32)
            stat_ref[1:2, :] = jnp.zeros((1, lanes), jnp.float32)
        else:
            acc_ref[...] = acc_in[slot]
            stat_ref[...] = stat_in[slot]

        def absorb(where, base, masked):
            keys = jnp.concatenate([ref[where, :, 0:HEAD_SIZE] for ref in units], axis=0)
            values = jnp.concatenate([ref[where, :, HEAD_SIZE:] for ref in units], axis=0)
            scores = lax.dot_general(
                keys, q_ref[turn], (((1,), (1,)), ((), ())), preferred_element_type=jnp.float32
            )
            if masked:
                firsts = firsts_ref[pl.ds(slot, 1), :]
                pieces = []
                for step in range(parts):
                    behind = depth - step
                    behind = jnp.where(behind < 0, behind + parts, behind)
                    spot = base + behind * rows + lax.broadcasted_iota(jnp.int32, (rows, rows), 0)
                    seen = (spot >= firsts) & (spot <= at)
                    pieces.append(jnp.concatenate([seen] * heads, axis=1))
                scores = jnp.where(jnp.concatenate(pieces, axis=0), scores, NEGATIVE)
            before = stat_ref[0:1, :]
            peak = jnp.maximum(before, jnp.max(scores, axis=0, keepdims=True))
            weights = jnp.exp2((scores - peak) * scale)
            total = jnp.sum(weights, axis=0, keepdims=True)
            gain = lax.dot_general(
                values,
                weights.astype(jnp.bfloat16),
                (((0,), (0,)), ((), ())),
                preferred_element_type=jnp.float32,
            )
            shrink = jnp.exp2((before - peak) * scale)
            stat_ref[0:1, :] = peak
            stat_ref[1:2, :] = stat_ref[1:2, :] * shrink + total
            acc_ref[...] = acc_ref[...] * shrink + gain

        origin = group - back
        lowest = lax.div(low, shard) - origin * width
        bottom = jnp.bitwise_xor(lax.div(member, chunk), half) * chunk
        start = jnp.maximum(lowest, bottom)
        stop = jnp.minimum(doc + back * width, bottom + chunk - 1) + 1

        def visit(key_doc, _):
            base = (origin * width + key_doc) * shard
            where = jnp.bitwise_xor(member, key_doc) - half * chunk
            clear = (base >= high) & (key_doc != doc + back * width)

            @pl.when(clear)
            def _():
                absorb(where, base, False)

            @pl.when(jnp.logical_not(clear))
            def _():
                absorb(where, base, True)

            return 0

        lax.fori_loop(start, stop, visit, 0)
        if closing:
            done = (acc_ref[...] / stat_ref[1:2, :]).astype(out_ref.dtype)
            for h in range(heads):
                out_ref[turn, :, h * HEAD_SIZE : (h + 1) * HEAD_SIZE] = (
                    done[:, h * rows : (h + 1) * rows].T
                )
        else:
            acc_out[slot] = acc_ref[...]
            stat_out[slot] = stat_ref[...]
        return 0

    lax.fori_loop(0, count, one_block, 0)
    if closing:
        copies = [
            pltpu.make_async_copy(out_ref.at[i], out_refs[i], sem.at[i]) for i in range(count)
        ]
        for copy in copies:
            copy.start()
        for copy in copies:
            copy.wait()


def attend(place, tables, queries, units, half, slots, state, closing, parts, back=0):
    width = KEY_VALUE_HEADS
    bounds, firsts = tables
    rows, columns = queries[0].shape
    lanes = columns // HEAD_SIZE * rows
    vmem = pl.BlockSpec(memory_space=pltpu.VMEM)
    smem = pl.BlockSpec(memory_space=pltpu.SMEM)
    hbm = pl.BlockSpec(memory_space=pltpu.HBM)
    opening = state is None
    held = () if opening else tuple(state)
    count = len(slots)
    scratch = [
        pltpu.VMEM((HEAD_SIZE, lanes), jnp.float32),
        pltpu.VMEM((8, lanes), jnp.float32),
        pltpu.VMEM((count, lanes, HEAD_SIZE), queries[0].dtype),
    ]
    if closing:
        out_shape = [jax.ShapeDtypeStruct((rows, columns), queries[0].dtype) for _ in slots]
        out_specs = [hbm] * count
        aliases = {}
        scratch += [
            pltpu.VMEM((count, rows, columns), queries[0].dtype),
            pltpu.SemaphoreType.DMA((count,)),
        ]
    else:
        out_shape = [
            jax.ShapeDtypeStruct((width, HEAD_SIZE, lanes), jnp.float32),
            jax.ShapeDtypeStruct((width, 8, lanes), jnp.float32),
        ]
        out_specs = [vmem, vmem]
        first = 3 + count + len(units)
        aliases = {} if opening else {first: 0, first + 1: 1}
    work = count * 2 * parts * rows * lanes * HEAD_SIZE * 4
    return pl.pallas_call(
        functools.partial(attend_kernel, half, back, tuple(slots), opening, closing, parts),
        out_shape=out_shape,
        in_specs=[smem, smem] + [vmem] * (1 + count + len(units) + len(held)),
        out_specs=out_specs,
        input_output_aliases=aliases,
        cost_estimate=pl.CostEstimate(
            flops=work, bytes_accessed=4 * width * HEAD_SIZE * lanes, transcendentals=0
        ),
        scratch_shapes=scratch,
    )(place, bounds, firsts, *[queries[slot] for slot in slots], *units, *held)


def doc_starts(doc_lengths, positions):
    closing = jnp.cumsum(doc_lengths)
    passed = closing[None, :] <= positions[:, None]
    return jnp.sum(jnp.where(passed, doc_lengths[None, :], 0), axis=1)


def swap(block, k):
    if k == 0:
        return block
    length = lax.axis_size("doc")
    return lax.ppermute(block, "doc", [(i, i ^ k) for i in range(length)])


def on_device(packed_query_rows, packed_key_rows, packed_value_rows, doc_lengths):
    width = KEY_VALUE_HEADS
    chunk = width // HALVES
    docs, parts = lax.axis_size("doc"), lax.axis_size("head")
    index = lax.axis_index("doc")
    member, group = index % width, index // width
    depth = lax.axis_index("head")
    place = jnp.stack([depth, member, group]).astype(jnp.int32)
    rows = packed_query_rows.shape[0]
    blocks = (group * width + jnp.bitwise_xor(member, jnp.arange(width))) * parts + depth
    spots = blocks[:, None] * rows + jnp.arange(rows)[None, :]
    firsts = doc_starts(doc_lengths, spots.reshape(-1)).reshape(width, rows).astype(jnp.int32)
    tables = (jnp.stack([firsts[:, 0], firsts[:, -1]], axis=1), firsts)

    def cut(value, k):
        size = value.shape[1] // width
        return lax.dynamic_slice_in_dim(value, jnp.bitwise_xor(member, k) * size, size, 1)

    ring = [(i, (i + 1) % parts) for i in range(parts)]
    pairs = [
        swap(jnp.concatenate([cut(packed_key_rows, k), cut(packed_value_rows, k)], axis=1), k)
        for k in range(width)
    ]
    units = []
    for half in range(HALVES):
        units.append([jnp.stack(pairs[half * chunk : (half + 1) * chunk])])
    queries = [swap(cut(packed_query_rows, k), k) for k in range(width)]
    for _ in range(1, parts):
        for half in range(HALVES):
            units[half].append(lax.ppermute(units[half][-1], "head", ring))

    attends = functools.partial(attend, place, tables, queries)
    everyone = list(range(width))
    state = None
    if docs > width:
        over = [(i, i + width) for i in range(docs - width)]
        for half in range(HALVES):
            far = [lax.ppermute(piece, "doc", over) for piece in units[half]]
            state = attends(far, half, everyone, state, False, parts, back=1)
    for half in range(HALVES - 1):
        state = attends(units[half], half, everyone, state, False, parts)
    results = {}
    for turn in reversed(range(HALVES)):
        slots = list(range(turn * chunk, (turn + 1) * chunk))
        outs = attends(units[HALVES - 1], HALVES - 1, slots, state, True, parts)
        for slot, out in zip(slots, outs):
            results[slot] = swap(out, slot)
    stacked = jnp.stack([results[k] for k in range(width)])
    order = [jnp.bitwise_xor(member, k) for k in range(width)]
    return jnp.concatenate(
        [lax.dynamic_index_in_dim(stacked, order[k], 0, keepdims=False) for k in range(width)],
        axis=1,
    )


def solution(mesh):
    in_specs = (P(("doc", "head"), None), P(("doc", "head"), None), P(("doc", "head"), None), P())
    out_specs = P(("doc", "head"), None)

    return jax.shard_map(
        on_device, mesh=mesh, in_specs=in_specs, out_specs=out_specs, check_vma=False
    )
```

time: 108 us -> 91.3 us (0.85)
  Pallas kernels: 44.5 us -> 25.1 us
  waiting for transfers between devices: 25 us -> 26.6 us
    pallas_call x5 -> x3, Pallas kernels: 44.5 us -> 25.1 us  [attend(): pl.pallas_call(functools.partial(attend_kernel, half, back, tuple(slots),...]
    ppermute x6, waiting for transfers between devices: 8.04 us -> 15.1 us  [on_device(): units[half].append(lax.ppermute(units[half][-1], 'head', ring))]
    ppermute x21, waiting for transfers between devices: 17 us -> 11.5 us  [swap(): return lax.ppermute(block, 'doc', [(i, i ^ k) for i in range(length)])]
    ppermute x21, starting transfers between devices: 24.4 us -> 26.9 us  [swap(): return lax.ppermute(block, 'doc', [(i, i ^ k) for i in range(length)])]
    ppermute x6, starting transfers between devices: 5.8 us -> 4.01 us  [on_device(): units[half].append(lax.ppermute(units[half][-1], 'head', ring))]
    unnamed x54 -> x58, local copies, waits for them, and re-layouts: 4.12 us -> 3.44 us
  transfers between devices with their start and end apart: 27 -> 27, of which waited for: 10 -> 10; matrix products, arithmetic and copies ran while one was open for 2% -> 4% of each run, Pallas kernels for 34% -> 18%
where the time goes in v1:
time: 91.3 us; the launch traced here: 91 us
  starting transfers between devices  30.9 us (34%)
  waiting for transfers between devices  26.6 us (29%)
  Pallas kernels  25.1 us (27%)
  local copies, waits for them, and re-layouts  6.16 us (7%)
  other arithmetic  1.71 us (2%)
    ppermute x21, starting transfers between devices, swap(): return lax.ppermute(block, 'doc', [(i, i ^ k) for i in range(length)])  26.9 us
    pallas_call x3, Pallas kernels, attend(): pl.pallas_call(functools.partial(attend_kernel, half, back, tuple(slots),...  25.1 us
    ppermute x6, waiting for transfers between devices, on_device(): units[half].append(lax.ppermute(units[half][-1], 'head', ring))  15.1 us
    ppermute x21, waiting for transfers between devices, swap(): return lax.ppermute(block, 'doc', [(i, i ^ k) for i in range(length)])  11.5 us
    ppermute x6, starting transfers between devices, on_device(): units[half].append(lax.ppermute(units[half][-1], 'head', ring))  4.01 us
    unnamed x58, local copies, waits for them, and re-layouts  3.44 us
    dynamic_slice x2, local copies, waits for them, and re-layouts, cut(): lax.dynamic_slice_in_dim(value, jnp.bitwise_xor(member, k) * size, size, 1)  1.89 us
  transfers between devices with their start and end apart: 27, of which 10 were waited for; matrix products, arithmetic and copies ran while one was open for 4% of the time, Pallas kernels for 18%

profile of v1, /device:TPU:0, one launch (start us, length us, event | category | flops | bytes accessed | tf_op | source)
XLA Modules:
  0.0 91.0 jit_solution(11589224485612499044)
XLA Ops:
  0.0 1.1 %constant_dynamic-slice_fusion.6 = (bf16[128,128]{1,0:T(8,128)(2,1)S(1)}, bf16[128,128]{1,0:T(8,128)(2,1)S(1)}, bf16[128,128]{1,0:T(8,128)(2,1)S(1)}, bf16[128,1...) fusion(bf16[128,1024]{1,0:T(8,128)(2,1)} %param.6, ...), kind=kLoop, calls=%fused_computation.33 | loop fusion | bytes 1048608 | tf_op jit(solution)/shard_map/dynamic_slice | solution.py:209
  1.2 0.6 collective-permute-start.14
  1.7 2.6 %collective-permute-start.15 = (bf16[128,256]{1,0:T(8,128)(2,1)S(1)}, bf16[128,256]{1,0:T(8,128)(2,1)S(1)}, u32[]{:S(2)}, u32[]{:S(2)}) collective-permute-start(bf16[128,256]{1,0:T(8,128)(2,1)S(1)} %pad_maximum_fusion.7), channel_id=1, source_target_pairs={{0,2},{1,3},{2,0},{3,1},{4,6},{5,7},{6,4},{7,5},{8,10},{9,11},{10,... | collective-permute-start | bytes 196616 | tf_op jit(solution)/shard_map/ppermute | solution.py:190
  4.3 0.2 collective-permute-start.16
  4.5 1.8 %collective-permute-start.3 = (bf16[128,256]{1,0:T(8,128)(2,1)S(1)}, bf16[128,256]{1,0:T(8,128)(2,1)S(1)}, u32[]{:S(2)}, u32[]{:S(2)}) collective-permute-start(bf16[128,256]{1,0:T(8,128)(2,1)S(1)} %pad_maximum_fusion.2), channel_id=1, source_target_pairs={{0,4},{1,5},{2,6},{3,7},{4,0},{5,1},{6,2},{7,3},{8,12},{9,13},{10,... | collective-permute-start | bytes 196616 | tf_op jit(solution)/shard_map/ppermute | solution.py:190
  6.3 0.1 collective-permute-start.4
  6.6 0.0 collective-permute-done.14
  6.6 2.6 %collective-permute-start.5 = (bf16[128,256]{1,0:T(8,128)(2,1)S(1)}, bf16[128,256]{1,0:T(8,128)(2,1)S(1)}, u32[]{:S(2)}, u32[]{:S(2)}) collective-permute-start(bf16[128,256]{1,0:T(8,128)(2,1)S(1)} %pad_maximum_fusion.4), channel_id=1, source_target_pairs={{0,6},{1,7},{2,4},{3,5},{4,2},{5,3},{6,0},{7,1},{8,14},{9,15},{10,... | collective-permute-start | bytes 196616 | tf_op jit(solution)/shard_map/ppermute | solution.py:190
  9.1 0.0 collective-permute-done.15
  9.2 0.2 collective-permute-start.6
  9.3 0.0 collective-permute-done.16
  9.4 1.7 %collective-permute-start.17 = (bf16[4,128,256]{2,1,0:T(8,128)(2,1)S(1)}, bf16[4,128,256]{2,1,0:T(8,128)(2,1)S(1)}, u32[]{:S(2)}, u32[]{:S(2)}) collective-permute-start(bf16[4,128,256]{2,1,0:T(8,128)(2,1)S(1)} %pad_maximum_fusion.1.refs_8_), channel_id=1, source_target_pairs={{0,8},{8,16},{16,24},{24,0},{1,9},{9,17},{17,25},{25,1},{2,10},{10... | collective-permute-start | bytes 786440 | tf_op jit(solution)/shard_map/ppermute | solution.py:222
  11.1 0.8 constant_dynamic-slice_fusion.8
  11.9 0.0 collective-permute-done.3
  11.9 0.7 collective-permute-start
  12.6 0.0 collective-permute-done.4
  12.6 1.0 %collective-permute-start.1 = (bf16[128,512]{1,0:T(8,128)(2,1)S(1)}, bf16[128,512]{1,0:T(8,128)(2,1)S(1)}, u32[]{:S(2)}, u32[]{:S(2)}) collective-permute-start(bf16[128,512]{1,0:T(8,128)(2,1)S(1)} %get-tuple-element.29), channel_id=1, source_target_pairs={{0,2},{1,3},{2,0},{3,1},{4,6},{5,7},{6,4},{7,5},{8,10},{9,11},{10,... | collective-permute-start | bytes 393224 | tf_op jit(solution)/shard_map/ppermute | solution.py:190
  13.5 0.0 collective-permute-done.5
  13.5 1.5 %collective-permute-start.10 = (bf16[128,512]{1,0:T(8,128)(2,1)S(1)}, bf16[128,512]{1,0:T(8,128)(2,1)S(1)}, u32[]{:S(2)}, u32[]{:S(2)}) collective-permute-start(bf16[128,512]{1,0:T(8,128)(2,1)S(1)} %get-tuple-element.27), channel_id=1, source_target_pairs={{0,4},{1,5},{2,6},{3,7},{4,0},{5,1},{6,2},{7,3},{8,12},{9,13},{10,... | collective-permute-start | bytes 393224 | tf_op jit(solution)/shard_map/ppermute | solution.py:190
  15.1 0.0 copy-start.2
  15.1 1.6 %collective-permute-start.7 = (bf16[4,128,256]{2,1,0:T(8,128)(2,1)S(1)}, bf16[4,128,256]{2,1,0:T(8,128)(2,1)S(1)}, u32[]{:S(2)}, u32[]{:S(2)}) collective-permute-start(bf16[4,128,256]{2,1,0:T(8,128)(2,1)S(1)} %pad_maximum_fusion.refs_4_), channel_id=1, source_target_pairs={{0,8},{8,16},{16,24},{24,0},{1,9},{9,17},{17,25},{25,1},{2,10},{10... | collective-permute-start | bytes 786440 | tf_op jit(solution)/shard_map/ppermute | solution.py:222
  16.7 3.6 %collective-permute-done.17.refs_9_ = bf16[4,128,256]{2,1,0:T(8,128)(2,1)S(1)} collective-permute-done((bf16[4,128,256]{2,1,0:T(8,128)(2,1)S(1)}, bf16[4,128,256]{2,1,0:T(8,128)(2,1)S(1)}, u32[]{:S(2)}, u32[]{:S(2)}) %collective-permute-start.17) | collective-permute-done | bytes 262176 | tf_op jit(solution)/shard_map/ppermute | solution.py:222
  20.3 0.0 collective-permute-start.18
  20.3 0.1 add_bitcast_fusion
  20.4 0.1 copy.13
  20.5 0.1 reduce
  20.6 0.1 select_reduce_fusion
  20.7 0.3 collective-permute-start.11
  21.1 5.1 %collective-permute-done.7.refs_5_ = bf16[4,128,256]{2,1,0:T(8,128)(2,1)S(1)} collective-permute-done((bf16[4,128,256]{2,1,0:T(8,128)(2,1)S(1)}, bf16[4,128,256]{2,1,0:T(8,128)(2,1)S(1)}, u32[]{:S(2)}, u32[]{:S(2)}) %collective-permute-start.7) | collective-permute-done | bytes 262176 | tf_op jit(solution)/shard_map/ppermute | solution.py:222
  26.2 5.6 %collective-permute-done.18.refs_10_ = bf16[4,128,256]{2,1,0:T(8,128)(2,1)S(1)} collective-permute-done((bf16[4,128,256]{2,1,0:T(8,128)(2,1)S(1)}, bf16[4,128,256]{2,1,0:T(8,128)(2,1)S(1)}, u32[]{:S(2)}, u32[]{:S(2)}) %collective-permute-start.18) | collective-permute-done | bytes 262176 | tf_op jit(solution)/shard_map/ppermute | solution.py:222
  31.8 0.1 fusion
  31.8 2.5 %collective-permute-start.12 = (bf16[128,512]{1,0:T(8,128)(2,1)S(1)}, bf16[128,512]{1,0:T(8,128)(2,1)S(1)}, u32[]{:S(2)}, u32[]{:S(2)}) collective-permute-start(bf16[128,512]{1,0:T(8,128)(2,1)S(1)} %get-tuple-element.32), channel_id=1, source_target_pairs={{0,6},{1,7},{2,4},{3,5},{4,2},{5,3},{6,0},{7,1},{8,14},{9,15},{10,... | collective-permute-start | bytes 393224 | tf_op jit(solution)/shard_map/ppermute | solution.py:190
  34.3 0.0 collective-permute-done.10.refs_4_.refs_0_
  34.3 0.0 collective-permute-start.13
  34.3 1.7 %collective-permute-start.2 = (bf16[128,512]{1,0:T(8,128)(2,1)S(1)}, bf16[128,512]{1,0:T(8,128)(2,1)S(1)}, u32[]{:S(2)}, u32[]{:S(2)}) collective-permute-start(bf16[128,512]{1,0:T(8,128)(2,1)S(1)} %get-tuple-element.28), channel_id=1, source_target_pairs={{0,3},{1,2},{2,1},{3,0},{4,7},{5,6},{6,5},{7,4},{8,11},{9,10},{10,... | collective-permute-start | bytes 393224 | tf_op jit(solution)/shard_map/ppermute | solution.py:190
  36.0 0.7 pad_add_fusion.bounds_ref
  36.7 0.7 collective-permute-done.8.refs_6_
  37.4 0.6 collective-permute-start.9
  38.0 0.6 pad_add_fusion.1.place_ref
  38.6 2.4 %collective-permute-done.13.refs_7_.refs_3_ = bf16[128,512]{1,0:T(8,128)(2,1)S(1)} collective-permute-done((bf16[128,512]{1,0:T(8,128)(2,1)S(1)}, bf16[128,512]{1,0:T(8,128)(2,1)S(1)}, u32[]{:S(2)}, u32[]{:S(2)}) %collective-permute-start.13) | collective-permute-done | bytes 131104 | tf_op jit(solution)/shard_map/ppermute | solution.py:190
  41.0 1.9 %collective-permute-done.2.refs_3_ = bf16[128,512]{1,0:T(8,128)(2,1)S(1)} collective-permute-done((bf16[128,512]{1,0:T(8,128)(2,1)S(1)}, bf16[128,512]{1,0:T(8,128)(2,1)S(1)}, u32[]{:S(2)}, u32[]{:S(2)}) %collective-permute-start.2) | collective-permute-done | bytes 131104 | tf_op jit(solution)/shard_map/ppermute | solution.py:190
  42.9 0.1 collective-permute-done.19.refs_11_
  43.1 0.4 copy-done.16
  43.5 0.2 copy-done.10
  43.7 12.4 %shard_map.46 = (f32[8,128,512]{2,1,0:T(8,128)}, f32[8,8,512]{2,1,0:T(8,128)}) custom-call(s32[3]{0:T(128)} %pad_add_fusion.1.place_ref, s32[8,2]{1,0:T(8,128)} %pad_add_fusion.bounds_ref, s32[8,128]{1,0:T(8,128)} %bitcast.56, bf16[128,512]{1,0:T(8,128)(2,1)} %get-tuple-element.31.refs_0_, bf16[128,512]{1,0:T(8,128)(2,1)} %copy-done.12, ...), custom_call_target="tpu_custom_call" | custom-call | flops 2147483648 | bytes 2097152 | tf_op jit(solution)/shard_map/pallas_call | solution.py:167
  56.2 0.7 copy-done.11
  56.9 9.1 %shard_map.48 = (bf16[128,512]{1,0:T(8,128)(2,1)}, bf16[128,512]{1,0:T(8,128)(2,1)}, bf16[128,512]{1,0:T(8,128)(2,1)}, bf16[128,512]{1,0:T(8,128)(2,1)}) custom-call(s32[3]{0:T(128)} %pad_add_fusion.1.place_ref, s32[8,2]{1,0:T(8,128)} %pad_add_fusion.bounds_ref, s32[8,128]{1,0:T(8,128)} %bitcast.57, bf16[128,512]{1,0:T(8,128)(2,1)} %copy-done.14, ...), custom_call_target="tpu_custom_call" | custom-call | flops 1073741824 | bytes 2097152 | tf_op jit(solution)/shard_map/pallas_call | solution.py:167
  66.0 0.1 collective-permute-start.23
  66.0 3.6 %shard_map.47 = (bf16[128,512]{1,0:T(8,128)(2,1)}, bf16[128,512]{1,0:T(8,128)(2,1)}, bf16[128,512]{1,0:T(8,128)(2,1)}, bf16[128,512]{1,0:T(8,128)(2,1)}) custom-call(s32[3]{0:T(128)} %pad_add_fusion.1.place_ref, s32[8,2]{1,0:T(8,128)} %pad_add_fusion.bounds_ref, s32[8,128]{1,0:T(8,128)} %bitcast.58, bf16[128,512]{1,0:T(8,128)(2,1)} %get-tuple-element.31.refs_0_, ...), custom_call_target="tpu_custom_call" | custom-call | flops 1073741824 | bytes 2097152 | tf_op jit(solution)/shard_map/pallas_call | solution.py:167
  69.6 0.4 collective-permute-start.20
  70.0 1.7 %collective-permute-start.21 = (bf16[128,512]{1,0:T(8,128)(2,1)}, bf16[128,512]{1,0:T(8,128)(2,1)S(1)}, u32[]{:S(2)}, u32[]{:S(2)}) collective-permute-start(bf16[128,512]{1,0:T(8,128)(2,1)} %get-tuple-element.19), channel_id=1, source_target_pairs={{0,2},{1,3},{2,0},{3,1},{4,6},{5,7},{6,4},{7,5},{8,10},{9,11},{10,... | collective-permute-start | bytes 393224 | tf_op jit(solution)/shard_map/ppermute | solution.py:190
  71.6 6.0 %collective-permute-start.24 = (bf16[128,512]{1,0:T(8,128)(2,1)S(1)}, bf16[128,512]{1,0:T(8,128)(2,1)S(1)}, u32[]{:S(2)}, u32[]{:S(2)}) collective-permute-start(bf16[128,512]{1,0:T(8,128)(2,1)S(1)} %copy-done.21), channel_id=1, source_target_pairs={{0,5},{1,4},{2,7},{3,6},{4,1},{5,0},{6,3},{7,2},{8,13},{9,12},{10,... | collective-permute-start | bytes 393224 | tf_op jit(solution)/shard_map/ppermute | solution.py:190
  77.6 0.9 %bitcast_dynamic-update-slice_fusion.15 = bf16[8,128,512]{2,1,0:T(8,128)(2,1)S(1)} fusion(bf16[128,512]{1,0:T(8,128)(2,1)} %get-tuple-element.17), kind=kLoop, calls=%fused_computation.17 | loop fusion | bytes 262144
  78.5 0.0 collective-permute-done.20
  78.5 1.0 %collective-permute-start.25 = (bf16[128,512]{1,0:T(8,128)(2,1)S(1)}, bf16[128,512]{1,0:T(8,128)(2,1)S(1)}, u32[]{:S(2)}, u32[]{:S(2)}) collective-permute-start(bf16[128,512]{1,0:T(8,128)(2,1)S(1)} %copy-done.20), channel_id=1, source_target_pairs={{0,6},{1,7},{2,4},{3,5},{4,2},{5,3},{6,0},{7,1},{8,14},{9,15},{10,... | collective-permute-start | bytes 393224 | tf_op jit(solution)/shard_map/ppermute | solution.py:190
  79.6 0.0 collective-permute-done.21
  79.6 2.3 %collective-permute-start.26 = (bf16[128,512]{1,0:T(8,128)(2,1)S(1)}, bf16[128,512]{1,0:T(8,128)(2,1)S(1)}, u32[]{:S(2)}, u32[]{:S(2)}) collective-permute-start(bf16[128,512]{1,0:T(8,128)(2,1)S(1)} %copy-done.19), channel_id=1, source_target_pairs={{0,7},{1,6},{2,5},{3,4},{4,3},{5,2},{6,1},{7,0},{8,15},{9,14},{10,... | collective-permute-start | bytes 393224 | tf_op jit(solution)/shard_map/ppermute | solution.py:190
  81.9 0.0 collective-permute-done.22
  82.0 4.6 %collective-permute-done.24 = bf16[128,512]{1,0:T(8,128)(2,1)S(1)} collective-permute-done((bf16[128,512]{1,0:T(8,128)(2,1)S(1)}, bf16[128,512]{1,0:T(8,128)(2,1)S(1)}, u32[]{:S(2)}, u32[]{:S(2)}) %collective-permute-start.24) | collective-permute-done | bytes 131104 | tf_op jit(solution)/shard_map/ppermute | solution.py:190
  86.6 0.9 collective-permute-done.25
  87.5 1.7 %collective-permute-done.26 = bf16[128,512]{1,0:T(8,128)(2,1)S(1)} collective-permute-done((bf16[128,512]{1,0:T(8,128)(2,1)S(1)}, bf16[128,512]{1,0:T(8,128)(2,1)S(1)}, u32[]{:S(2)}, u32[]{:S(2)}) %collective-permute-start.26) | collective-permute-done | bytes 131104 | tf_op jit(solution)/shard_map/ppermute | solution.py:190
  89.4 0.0 copy-start.4
  89.4 1.0 %copy-done.4 = bf16[128,4096]{1,0:T(8,128)(2,1)} copy-done((bf16[128,4096]{1,0:T(8,128)(2,1)}, bf16[128,4096]{1,0:T(8,128)(2,1)S(1)}, u32[]{:S(2)}) %copy-start.4) | copy-done | bytes 1048600
  90.4 0.7 bitcast_dynamic-update-slice_fusion
  (74 shorter events, 0.5 us)
Async XLA Ops:
  0.0 11.1 %copy-start = (bf16[128,4096]{1,0:T(8,128)(2,1)S(1)}, bf16[128,4096]{1,0:T(8,128)(2,1)}, u32[]{:S(2)}) copy-start(bf16[128,4096]{1,0:T(8,128)(2,1)} %param.4) | copy-start | bytes 3145732
  1.2 5.4 %collective-permute-start.14 = (bf16[128,256]{1,0:T(8,128)(2,1)S(1)}, bf16[128,256]{1,0:T(8,128)(2,1)S(1)}, u32[]{:S(2)}, u32[]{:S(2)}) collective-permute-start(bf16[128,256]{1,0:T(8,128)(2,1)S(1)} %pad_maximum_fusion.6), channel_id=1, source_target_pairs={{0,1},{1,0},{2,3},{3,2},{4,5},{5,4},{6,7},{7,6},{8,9},{9,8},{10,11... | collective-permute-start | bytes 196616 | tf_op jit(solution)/shard_map/ppermute | solution.py:190
  1.7 18.7 %copy-start.5 = (s32[16]{0:T(128)S(1)}, s32[16]{0:T(128)}, u32[]{:S(2)}) copy-start(s32[16]{0:T(128)} %param.7) | copy-start | bytes 196
  1.7 7.4 %collective-permute-start.15 = (bf16[128,256]{1,0:T(8,128)(2,1)S(1)}, bf16[128,256]{1,0:T(8,128)(2,1)S(1)}, u32[]{:S(2)}, u32[]{:S(2)}) collective-permute-start(bf16[128,256]{1,0:T(8,128)(2,1)S(1)} %pad_maximum_fusion.7), channel_id=1, source_target_pairs={{0,2},{1,3},{2,0},{3,1},{4,6},{5,7},{6,4},{7,5},{8,10},{9,11},{10,... | collective-permute-start | bytes 196616 | tf_op jit(solution)/shard_map/ppermute | solution.py:190
  4.3 5.0 %collective-permute-start.16 = (bf16[128,256]{1,0:T(8,128)(2,1)S(1)}, bf16[128,256]{1,0:T(8,128)(2,1)S(1)}, u32[]{:S(2)}, u32[]{:S(2)}) collective-permute-start(bf16[128,256]{1,0:T(8,128)(2,1)S(1)} %pad_maximum_fusion.8), channel_id=1, source_target_pairs={{0,3},{1,2},{2,1},{3,0},{4,7},{5,6},{6,5},{7,4},{8,11},{9,10},{10,... | collective-permute-start | bytes 196616 | tf_op jit(solution)/shard_map/ppermute | solution.py:190
  4.5 7.4 %collective-permute-start.3 = (bf16[128,256]{1,0:T(8,128)(2,1)S(1)}, bf16[128,256]{1,0:T(8,128)(2,1)S(1)}, u32[]{:S(2)}, u32[]{:S(2)}) collective-permute-start(bf16[128,256]{1,0:T(8,128)(2,1)S(1)} %pad_maximum_fusion.2), channel_id=1, source_target_pairs={{0,4},{1,5},{2,6},{3,7},{4,0},{5,1},{6,2},{7,3},{8,12},{9,13},{10,... | collective-permute-start | bytes 196616 | tf_op jit(solution)/shard_map/ppermute | solution.py:190
  6.3 6.3 %collective-permute-start.4 = (bf16[128,256]{1,0:T(8,128)(2,1)S(1)}, bf16[128,256]{1,0:T(8,128)(2,1)S(1)}, u32[]{:S(2)}, u32[]{:S(2)}) collective-permute-start(bf16[128,256]{1,0:T(8,128)(2,1)S(1)} %pad_maximum_fusion.3), channel_id=1, source_target_pairs={{0,5},{1,4},{2,7},{3,6},{4,1},{5,0},{6,3},{7,2},{8,13},{9,12},{10,... | collective-permute-start | bytes 196616 | tf_op jit(solution)/shard_map/ppermute | solution.py:190
  6.6 7.0 %collective-permute-start.5 = (bf16[128,256]{1,0:T(8,128)(2,1)S(1)}, bf16[128,256]{1,0:T(8,128)(2,1)S(1)}, u32[]{:S(2)}, u32[]{:S(2)}) collective-permute-start(bf16[128,256]{1,0:T(8,128)(2,1)S(1)} %pad_maximum_fusion.4), channel_id=1, source_target_pairs={{0,6},{1,7},{2,4},{3,5},{4,2},{5,3},{6,0},{7,1},{8,14},{9,15},{10,... | collective-permute-start | bytes 196616 | tf_op jit(solution)/shard_map/ppermute | solution.py:190
  9.2 5.9 %collective-permute-start.6 = (bf16[128,256]{1,0:T(8,128)(2,1)S(1)}, bf16[128,256]{1,0:T(8,128)(2,1)S(1)}, u32[]{:S(2)}, u32[]{:S(2)}) collective-permute-start(bf16[128,256]{1,0:T(8,128)(2,1)S(1)} %pad_maximum_fusion.5), channel_id=1, source_target_pairs={{0,7},{1,6},{2,5},{3,4},{4,3},{5,2},{6,1},{7,0},{8,15},{9,14},{10,... | collective-permute-start | bytes 196616 | tf_op jit(solution)/shard_map/ppermute | solution.py:190
  9.4 33.6 %copy-start.1 = (bf16[4,128,256]{2,1,0:T(8,128)(2,1)}, bf16[4,128,256]{2,1,0:T(8,128)(2,1)S(1)}, u32[]{:S(2)}) copy-start(bf16[4,128,256]{2,1,0:T(8,128)(2,1)S(1)} %pad_maximum_fusion.1.refs_8_) | copy-start | bytes 786436
  9.4 10.9 %collective-permute-start.17 = (bf16[4,128,256]{2,1,0:T(8,128)(2,1)S(1)}, bf16[4,128,256]{2,1,0:T(8,128)(2,1)S(1)}, u32[]{:S(2)}, u32[]{:S(2)}) collective-permute-start(bf16[4,128,256]{2,1,0:T(8,128)(2,1)S(1)} %pad_maximum_fusion.1.refs_8_), channel_id=1, source_target_pairs={{0,8},{8,16},{16,24},{24,0},{1,9},{9,17},{17,25},{25,1},{2,10},{10... | collective-permute-start | bytes 786440 | tf_op jit(solution)/shard_map/ppermute | solution.py:222
  11.9 8.8 %collective-permute-start = (bf16[128,512]{1,0:T(8,128)(2,1)S(1)}, bf16[128,512]{1,0:T(8,128)(2,1)S(1)}, u32[]{:S(2)}, u32[]{:S(2)}) collective-permute-start(bf16[128,512]{1,0:T(8,128)(2,1)S(1)} %get-tuple-element.30), channel_id=1, source_target_pairs={{0,1},{1,0},{2,3},{3,2},{4,5},{5,4},{6,7},{7,6},{8,9},{9,8},{10,11... | collective-permute-start | bytes 393224 | tf_op jit(solution)/shard_map/ppermute | solution.py:190
  12.6 19.3 %collective-permute-start.1 = (bf16[128,512]{1,0:T(8,128)(2,1)S(1)}, bf16[128,512]{1,0:T(8,128)(2,1)S(1)}, u32[]{:S(2)}, u32[]{:S(2)}) collective-permute-start(bf16[128,512]{1,0:T(8,128)(2,1)S(1)} %get-tuple-element.29), channel_id=1, source_target_pairs={{0,2},{1,3},{2,0},{3,1},{4,6},{5,7},{6,4},{7,5},{8,10},{9,11},{10,... | collective-permute-start | bytes 393224 | tf_op jit(solution)/shard_map/ppermute | solution.py:190
  13.5 20.8 %collective-permute-start.10 = (bf16[128,512]{1,0:T(8,128)(2,1)S(1)}, bf16[128,512]{1,0:T(8,128)(2,1)S(1)}, u32[]{:S(2)}, u32[]{:S(2)}) collective-permute-start(bf16[128,512]{1,0:T(8,128)(2,1)S(1)} %get-tuple-element.27), channel_id=1, source_target_pairs={{0,4},{1,5},{2,6},{3,7},{4,0},{5,1},{6,2},{7,3},{8,12},{9,13},{10,... | collective-permute-start | bytes 393224 | tf_op jit(solution)/shard_map/ppermute | solution.py:190
  15.1 41.0 %copy-start.2 = (bf16[4,128,256]{2,1,0:T(8,128)(2,1)}, bf16[4,128,256]{2,1,0:T(8,128)(2,1)S(1)}, u32[]{:S(2)}) copy-start(bf16[4,128,256]{2,1,0:T(8,128)(2,1)S(1)} %pad_maximum_fusion.refs_4_) | copy-start | bytes 786436
  15.1 11.0 %collective-permute-start.7 = (bf16[4,128,256]{2,1,0:T(8,128)(2,1)S(1)}, bf16[4,128,256]{2,1,0:T(8,128)(2,1)S(1)}, u32[]{:S(2)}, u32[]{:S(2)}) collective-permute-start(bf16[4,128,256]{2,1,0:T(8,128)(2,1)S(1)} %pad_maximum_fusion.refs_4_), channel_id=1, source_target_pairs={{0,8},{8,16},{16,24},{24,0},{1,9},{9,17},{17,25},{25,1},{2,10},{10... | collective-permute-start | bytes 786440 | tf_op jit(solution)/shard_map/ppermute | solution.py:222
  20.3 22.7 %copy-start.6 = (bf16[4,128,256]{2,1,0:T(8,128)(2,1)}, bf16[4,128,256]{2,1,0:T(8,128)(2,1)S(1)}, u32[]{:S(2)}) copy-start(bf16[4,128,256]{2,1,0:T(8,128)(2,1)S(1)} %collective-permute-done.17.refs_9_) | copy-start | bytes 786436
  20.3 11.5 %collective-permute-start.18 = (bf16[4,128,256]{2,1,0:T(8,128)(2,1)S(1)}, bf16[4,128,256]{2,1,0:T(8,128)(2,1)S(1)}, u32[]{:S(2)}, u32[]{:S(2)}) collective-permute-start(bf16[4,128,256]{2,1,0:T(8,128)(2,1)S(1)} %collective-permute-done.17.refs_9_), channel_id=1, source_target_pairs={{0,8},{8,16},{16,24},{24,0},{1,9},{9,17},{17,25},{25,1},{2,10},{10... | collective-permute-start | bytes 786440 | tf_op jit(solution)/shard_map/ppermute | solution.py:222
  20.7 22.3 %copy-start.3 = (s32[1024]{0:T(1024)}, s32[1024]{0:T(1024)S(1)}, u32[]{:S(2)}) copy-start(s32[1024]{0:T(1024)S(1)} %select_reduce_fusion) | copy-start | bytes 12292
  20.7 22.3 %copy-start.12 = (bf16[128,512]{1,0:T(8,128)(2,1)}, bf16[128,512]{1,0:T(8,128)(2,1)S(1)}, u32[]{:S(2)}) copy-start(bf16[128,512]{1,0:T(8,128)(2,1)S(1)} %collective-permute-done.refs_1_) | copy-start | bytes 393220
  20.7 13.6 %collective-permute-start.11 = (bf16[128,512]{1,0:T(8,128)(2,1)S(1)}, bf16[128,512]{1,0:T(8,128)(2,1)S(1)}, u32[]{:S(2)}, u32[]{:S(2)}) collective-permute-start(bf16[128,512]{1,0:T(8,128)(2,1)S(1)} %get-tuple-element.26), channel_id=1, source_target_pairs={{0,5},{1,4},{2,7},{3,6},{4,1},{5,0},{6,3},{7,2},{8,13},{9,12},{10,... | collective-permute-start | bytes 393224 | tf_op jit(solution)/shard_map/ppermute | solution.py:190
  26.1 30.0 %copy-start.7 = (bf16[4,128,256]{2,1,0:T(8,128)(2,1)}, bf16[4,128,256]{2,1,0:T(8,128)(2,1)S(1)}, u32[]{:S(2)}) copy-start(bf16[4,128,256]{2,1,0:T(8,128)(2,1)S(1)} %collective-permute-done.7.refs_5_) | copy-start | bytes 786436
  26.1 11.2 %collective-permute-start.8 = (bf16[4,128,256]{2,1,0:T(8,128)(2,1)S(1)}, bf16[4,128,256]{2,1,0:T(8,128)(2,1)S(1)}, u32[]{:S(2)}, u32[]{:S(2)}) collective-permute-start(bf16[4,128,256]{2,1,0:T(8,128)(2,1)S(1)} %collective-permute-done.7.refs_5_), channel_id=1, source_target_pairs={{0,8},{8,16},{16,24},{24,0},{1,9},{9,17},{17,25},{25,1},{2,10},{10... | collective-permute-start | bytes 786440 | tf_op jit(solution)/shard_map/ppermute | solution.py:222
  31.8 11.3 %copy-start.9 = (bf16[4,128,256]{2,1,0:T(8,128)(2,1)}, bf16[4,128,256]{2,1,0:T(8,128)(2,1)S(1)}, u32[]{:S(2)}) copy-start(bf16[4,128,256]{2,1,0:T(8,128)(2,1)S(1)} %collective-permute-done.18.refs_10_) | copy-start | bytes 786436
  31.8 11.2 %collective-permute-start.19 = (bf16[4,128,256]{2,1,0:T(8,128)(2,1)S(1)}, bf16[4,128,256]{2,1,0:T(8,128)(2,1)S(1)}, u32[]{:S(2)}, u32[]{:S(2)}) collective-permute-start(bf16[4,128,256]{2,1,0:T(8,128)(2,1)S(1)} %collective-permute-done.18.refs_10_), channel_id=1, source_target_pairs={{0,8},{8,16},{16,24},{24,0},{1,9},{9,17},{17,25},{25,1},{2,10},{10... | collective-permute-start | bytes 786440 | tf_op jit(solution)/shard_map/ppermute | solution.py:222
  31.8 11.2 %copy-start.13 = (bf16[128,512]{1,0:T(8,128)(2,1)}, bf16[128,512]{1,0:T(8,128)(2,1)S(1)}, u32[]{:S(2)}) copy-start(bf16[128,512]{1,0:T(8,128)(2,1)S(1)} %collective-permute-done.1.refs_2_) | copy-start | bytes 393220
  31.8 6.8 %collective-permute-start.12 = (bf16[128,512]{1,0:T(8,128)(2,1)S(1)}, bf16[128,512]{1,0:T(8,128)(2,1)S(1)}, u32[]{:S(2)}, u32[]{:S(2)}) collective-permute-start(bf16[128,512]{1,0:T(8,128)(2,1)S(1)} %get-tuple-element.32), channel_id=1, source_target_pairs={{0,6},{1,7},{2,4},{3,5},{4,2},{5,3},{6,0},{7,1},{8,14},{9,15},{10,... | collective-permute-start | bytes 393224 | tf_op jit(solution)/shard_map/ppermute | solution.py:190
  34.3 8.7 %copy-start.14 = (bf16[128,512]{1,0:T(8,128)(2,1)}, bf16[128,512]{1,0:T(8,128)(2,1)S(1)}, u32[]{:S(2)}) copy-start(bf16[128,512]{1,0:T(8,128)(2,1)S(1)} %collective-permute-done.10.refs_4_.refs_0_) | copy-start | bytes 393220
  34.3 6.7 %collective-permute-start.13 = (bf16[128,512]{1,0:T(8,128)(2,1)S(1)}, bf16[128,512]{1,0:T(8,128)(2,1)S(1)}, u32[]{:S(2)}, u32[]{:S(2)}) collective-permute-start(bf16[128,512]{1,0:T(8,128)(2,1)S(1)} %get-tuple-element.25), channel_id=1, source_target_pairs={{0,7},{1,6},{2,5},{3,4},{4,3},{5,2},{6,1},{7,0},{8,15},{9,14},{10,... | collective-permute-start | bytes 393224 | tf_op jit(solution)/shard_map/ppermute | solution.py:190
  34.3 8.7 %copy-start.15 = (bf16[128,512]{1,0:T(8,128)(2,1)}, bf16[128,512]{1,0:T(8,128)(2,1)S(1)}, u32[]{:S(2)}) copy-start(bf16[128,512]{1,0:T(8,128)(2,1)S(1)} %collective-permute-done.11.refs_5_.refs_1_) | copy-start | bytes 393220
  34.3 8.5 %collective-permute-start.2 = (bf16[128,512]{1,0:T(8,128)(2,1)S(1)}, bf16[128,512]{1,0:T(8,128)(2,1)S(1)}, u32[]{:S(2)}, u32[]{:S(2)}) collective-permute-start(bf16[128,512]{1,0:T(8,128)(2,1)S(1)} %get-tuple-element.28), channel_id=1, source_target_pairs={{0,3},{1,2},{2,1},{3,0},{4,7},{5,6},{6,5},{7,4},{8,11},{9,10},{10,... | collective-permute-start | bytes 393224 | tf_op jit(solution)/shard_map/ppermute | solution.py:190
  37.4 18.8 %copy-start.8 = (bf16[4,128,256]{2,1,0:T(8,128)(2,1)}, bf16[4,128,256]{2,1,0:T(8,128)(2,1)S(1)}, u32[]{:S(2)}) copy-start(bf16[4,128,256]{2,1,0:T(8,128)(2,1)S(1)} %collective-permute-done.8.refs_6_) | copy-start | bytes 786436
  37.4 18.8 %collective-permute-start.9 = (bf16[4,128,256]{2,1,0:T(8,128)(2,1)S(1)}, bf16[4,128,256]{2,1,0:T(8,128)(2,1)S(1)}, u32[]{:S(2)}, u32[]{:S(2)}) collective-permute-start(bf16[4,128,256]{2,1,0:T(8,128)(2,1)S(1)} %collective-permute-done.8.refs_6_), channel_id=1, source_target_pairs={{0,8},{8,16},{16,24},{24,0},{1,9},{9,17},{17,25},{25,1},{2,10},{10... | collective-permute-start | bytes 786440 | tf_op jit(solution)/shard_map/ppermute | solution.py:222
  38.6 4.5 %copy-start.17 = (bf16[128,512]{1,0:T(8,128)(2,1)}, bf16[128,512]{1,0:T(8,128)(2,1)S(1)}, u32[]{:S(2)}) copy-start(bf16[128,512]{1,0:T(8,128)(2,1)S(1)} %collective-permute-done.12.refs_6_.refs_2_) | copy-start | bytes 393220
  41.0 2.1 %copy-start.18 = (bf16[128,512]{1,0:T(8,128)(2,1)}, bf16[128,512]{1,0:T(8,128)(2,1)S(1)}, u32[]{:S(2)}) copy-start(bf16[128,512]{1,0:T(8,128)(2,1)S(1)} %collective-permute-done.13.refs_7_.refs_3_) | copy-start | bytes 393220
  42.9 0.6 copy-start.16
  43.0 0.7 copy-start.10
  56.2 0.7 copy-start.11
  65.9 5.7 %copy-start.21 = (bf16[128,512]{1,0:T(8,128)(2,1)S(1)}, bf16[128,512]{1,0:T(8,128)(2,1)}, u32[]{:S(2)}) copy-start(bf16[128,512]{1,0:T(8,128)(2,1)} %get-tuple-element.22) | copy-start | bytes 393220
  65.9 12.6 %copy-start.20 = (bf16[128,512]{1,0:T(8,128)(2,1)S(1)}, bf16[128,512]{1,0:T(8,128)(2,1)}, u32[]{:S(2)}) copy-start(bf16[128,512]{1,0:T(8,128)(2,1)} %get-tuple-element.23) | copy-start | bytes 393220
  65.9 13.6 %copy-start.19 = (bf16[128,512]{1,0:T(8,128)(2,1)S(1)}, bf16[128,512]{1,0:T(8,128)(2,1)}, u32[]{:S(2)}) copy-start(bf16[128,512]{1,0:T(8,128)(2,1)} %get-tuple-element.24) | copy-start | bytes 393220
  66.0 16.0 %collective-permute-start.23 = (bf16[128,512]{1,0:T(8,128)(2,1)}, bf16[128,512]{1,0:T(8,128)(2,1)S(1)}, u32[]{:S(2)}, u32[]{:S(2)}) collective-permute-start(bf16[128,512]{1,0:T(8,128)(2,1)} %get-tuple-element.21), channel_id=1, source_target_pairs={{0,4},{1,5},{2,6},{3,7},{4,0},{5,1},{6,2},{7,3},{8,12},{9,13},{10,... | collective-permute-start | bytes 393224 | tf_op jit(solution)/shard_map/ppermute | solution.py:190
  69.6 8.9 %collective-permute-start.20 = (bf16[128,512]{1,0:T(8,128)(2,1)}, bf16[128,512]{1,0:T(8,128)(2,1)S(1)}, u32[]{:S(2)}, u32[]{:S(2)}) collective-permute-start(bf16[128,512]{1,0:T(8,128)(2,1)} %get-tuple-element.18), channel_id=1, source_target_pairs={{0,1},{1,0},{2,3},{3,2},{4,5},{5,4},{6,7},{7,6},{8,9},{9,8},{10,11... | collective-permute-start | bytes 393224 | tf_op jit(solution)/shard_map/ppermute | solution.py:190
  70.0 9.6 %collective-permute-start.21 = (bf16[128,512]{1,0:T(8,128)(2,1)}, bf16[128,512]{1,0:T(8,128)(2,1)S(1)}, u32[]{:S(2)}, u32[]{:S(2)}) collective-permute-start(bf16[128,512]{1,0:T(8,128)(2,1)} %get-tuple-element.19), channel_id=1, source_target_pairs={{0,2},{1,3},{2,0},{3,1},{4,6},{5,7},{6,4},{7,5},{8,10},{9,11},{10,... | collective-permute-start | bytes 393224 | tf_op jit(solution)/shard_map/ppermute | solution.py:190
  71.6 10.3 %collective-permute-start.22 = (bf16[128,512]{1,0:T(8,128)(2,1)}, bf16[128,512]{1,0:T(8,128)(2,1)S(1)}, u32[]{:S(2)}, u32[]{:S(2)}) collective-permute-start(bf16[128,512]{1,0:T(8,128)(2,1)} %get-tuple-element.20), channel_id=1, source_target_pairs={{0,3},{1,2},{2,1},{3,0},{4,7},{5,6},{6,5},{7,4},{8,11},{9,10},{10,... | collective-permute-start | bytes 393224 | tf_op jit(solution)/shard_map/ppermute | solution.py:190
  71.6 14.9 %collective-permute-start.24 = (bf16[128,512]{1,0:T(8,128)(2,1)S(1)}, bf16[128,512]{1,0:T(8,128)(2,1)S(1)}, u32[]{:S(2)}, u32[]{:S(2)}) collective-permute-start(bf16[128,512]{1,0:T(8,128)(2,1)S(1)} %copy-done.21), channel_id=1, source_target_pairs={{0,5},{1,4},{2,7},{3,6},{4,1},{5,0},{6,3},{7,2},{8,13},{9,12},{10,... | collective-permute-start | bytes 393224 | tf_op jit(solution)/shard_map/ppermute | solution.py:190
  78.5 8.9 %collective-permute-start.25 = (bf16[128,512]{1,0:T(8,128)(2,1)S(1)}, bf16[128,512]{1,0:T(8,128)(2,1)S(1)}, u32[]{:S(2)}, u32[]{:S(2)}) collective-permute-start(bf16[128,512]{1,0:T(8,128)(2,1)S(1)} %copy-done.20), channel_id=1, source_target_pairs={{0,6},{1,7},{2,4},{3,5},{4,2},{5,3},{6,0},{7,1},{8,14},{9,15},{10,... | collective-permute-start | bytes 393224 | tf_op jit(solution)/shard_map/ppermute | solution.py:190
  79.6 9.6 %collective-permute-start.26 = (bf16[128,512]{1,0:T(8,128)(2,1)S(1)}, bf16[128,512]{1,0:T(8,128)(2,1)S(1)}, u32[]{:S(2)}, u32[]{:S(2)}) collective-permute-start(bf16[128,512]{1,0:T(8,128)(2,1)S(1)} %copy-done.19), channel_id=1, source_target_pairs={{0,7},{1,6},{2,5},{3,4},{4,3},{5,2},{6,1},{7,0},{8,15},{9,14},{10,... | collective-permute-start | bytes 393224 | tf_op jit(solution)/shard_map/ppermute | solution.py:190
  89.4 1.0 %copy-start.4 = (bf16[128,4096]{1,0:T(8,128)(2,1)}, bf16[128,4096]{1,0:T(8,128)(2,1)S(1)}, u32[]{:S(2)}) copy-start(bf16[128,4096]{1,0:T(8,128)(2,1)S(1)} %bitcast_dynamic-update-slice_fusion.1) | copy-start | bytes 3145732

commit v2 on v1

v2 whole, which is shorter than its diff:
```python
import functools
import math

import jax
import jax.numpy as jnp
from jax import lax
from jax.experimental import pallas as pl
from jax.experimental.pallas import tpu as pltpu
from jax.sharding import PartitionSpec as P


KEY_VALUE_HEADS = 8
HEAD_SIZE = 128
NEGATIVE = -1e30
HALVES = 2


def attend_kernel(half, back, slots, opening, closing, parts, place_ref, bounds_ref, firsts_ref, *refs):
    width = KEY_VALUE_HEADS
    count = len(slots)
    q_refs, refs = refs[:count], refs[count:]
    units, refs = refs[:parts], refs[parts:]
    if not opening:
        acc_in, stat_in = refs[:2]
        refs = refs[2:]
    if closing:
        out_refs, refs = refs[:count], refs[count:]
    acc_ref, stat_ref, *refs = refs
    score_ref, peak_ref, q_ref, list_ref = refs
    rows, columns = q_refs[0].shape
    heads = columns // HEAD_SIZE
    lanes = heads * rows
    shard = parts * rows
    chunk = width // HALVES
    depth = place_ref[0]
    member = place_ref[1]
    group = place_ref[2]
    origin = group - back
    scale = math.log2(math.e) / math.sqrt(HEAD_SIZE)
    bottom = jnp.bitwise_xor(lax.div(member, chunk), half) * chunk

    visits = jnp.int32(0)
    for turn, slot in enumerate(slots):
        doc = jnp.bitwise_xor(member, slot) + back * width
        lowest = lax.div(bounds_ref[slot], shard) - origin * width
        start = jnp.maximum(lowest, bottom)
        stop = jnp.maximum(jnp.minimum(doc, bottom + chunk - 1) + 1, start)

        def note(key_doc, place, turn=turn):
            list_ref[0, place] = turn
            list_ref[1, place] = key_doc
            return place + 1

        visits = lax.fori_loop(start, stop, note, visits)

    for i in range(count):
        for h in range(heads):
            q_ref[i, h * rows : (h + 1) * rows, :] = q_refs[i][:, h * HEAD_SIZE : (h + 1) * HEAD_SIZE]
    if opening:
        acc_ref[...] = jnp.zeros_like(acc_ref)
        stat_ref[:, 0:1, :] = jnp.full((count, 1, lanes), NEGATIVE, jnp.float32)
        stat_ref[:, 1:2, :] = jnp.zeros((count, 1, lanes), jnp.float32)
    else:
        acc_ref[...] = acc_in[slots[0] : slots[0] + count]
        stat_ref[...] = stat_in[slots[0] : slots[0] + count]

    def multiply(i):
        turn, key_doc = list_ref[0, i], list_ref[1, i]
        where = jnp.bitwise_xor(member, key_doc) - half * chunk
        keys = jnp.concatenate([ref[where, :, 0:HEAD_SIZE] for ref in units], axis=0)
        return lax.dot_general(
            keys, q_ref[turn], (((1,), (1,)), ((), ())), preferred_element_type=jnp.float32
        )

    def settle(i, scores):
        turn, key_doc = list_ref[0, i], list_ref[1, i]
        slot = slots[0] + turn
        doc = jnp.bitwise_xor(member, slot)
        base = (origin * width + key_doc) * shard
        root = ((group * width + doc) * parts + depth) * rows
        at = root + lax.broadcasted_iota(jnp.int32, (1, rows), 1)
        firsts = firsts_ref[pl.ds(slot, 1), :]
        pieces = []
        for step in range(parts):
            behind = depth - step
            behind = jnp.where(behind < 0, behind + parts, behind)
            spot = lax.broadcasted_iota(jnp.int32, (rows, rows), 0)
            corner = base + behind * rows
            seen = (spot >= firsts - corner) & (spot <= at - corner)
            pieces.append(jnp.concatenate([seen] * heads, axis=1))
        scores = jnp.where(jnp.concatenate(pieces, axis=0), scores, NEGATIVE)
        score_ref[...] = scores
        peak_ref[0:1, :] = jnp.max(scores, axis=0, keepdims=True)

    @pl.when(visits > 0)
    def _():
        settle(0, multiply(0))

        def visit(i, _):
            turn, key_doc = list_ref[0, i], list_ref[1, i]
            where = jnp.bitwise_xor(member, key_doc) - half * chunk
            follow = jnp.minimum(i + 1, visits - 1)
            coming = multiply(follow)
            before = stat_ref[turn, 0:1, :]
            peak = jnp.maximum(before, peak_ref[0:1, :])
            weights = jnp.exp2((score_ref[...] - peak) * scale)
            total = jnp.sum(weights, axis=0, keepdims=True)
            values = jnp.concatenate([ref[where, :, HEAD_SIZE:] for ref in units], axis=0)
            gain = lax.dot_general(
                values,
                weights.astype(jnp.bfloat16),
                (((0,), (0,)), ((), ())),
                preferred_element_type=jnp.float32,
            )
            settle(follow, coming)
            shrink = jnp.exp2((before - peak) * scale)
            stat_ref[turn, 0:1, :] = peak
            stat_ref[turn, 1:2, :] = stat_ref[turn, 1:2, :] * shrink + total
            acc_ref[turn] = acc_ref[turn] * shrink + gain
            return 0

        lax.fori_loop(0, visits, visit, 0)

    if closing:
        for i in range(count):
            done = (acc_ref[i] / stat_ref[i, 1:2, :]).astype(out_refs[i].dtype)
            for h in range(heads):
                out_refs[i][:, h * HEAD_SIZE : (h + 1) * HEAD_SIZE] = done[:, h * rows : (h + 1) * rows].T


def attend(place, tables, queries, units, half, slots, state, closing, parts, back=0):
    width = KEY_VALUE_HEADS
    bounds, firsts = tables
    rows, columns = queries[0].shape
    lanes = columns // HEAD_SIZE * rows
    vmem = pl.BlockSpec(memory_space=pltpu.VMEM)
    smem = pl.BlockSpec(memory_space=pltpu.SMEM)
    opening = state is None
    held = () if opening else tuple(state)
    count = len(slots)
    kept = [
        pltpu.VMEM((width, HEAD_SIZE, lanes), jnp.float32),
        pltpu.VMEM((width, 8, lanes), jnp.float32),
    ]
    scratch = [
        pltpu.VMEM((parts * rows, lanes), jnp.float32),
        pltpu.VMEM((8, lanes), jnp.float32),
        pltpu.VMEM((count, lanes, HEAD_SIZE), queries[0].dtype),
        pltpu.SMEM((2, width * width), jnp.int32),
    ]
    aliases = {}
    if closing:
        out_shape = [pltpu.VMEM((rows, columns), queries[0].dtype) for _ in slots]
        scratch = [
            pltpu.VMEM((count, HEAD_SIZE, lanes), jnp.float32),
            pltpu.VMEM((count, 8, lanes), jnp.float32),
        ] + scratch
    else:
        out_shape = kept
        first = 3 + count + len(units)
        aliases = {} if opening else {first: 0, first + 1: 1}
    work = count * 2 * parts * rows * lanes * HEAD_SIZE * 4
    return pl.pallas_call(
        functools.partial(attend_kernel, half, back, tuple(slots), opening, closing, parts),
        out_shape=out_shape,
        in_specs=[smem, smem] + [vmem] * (1 + count + len(units) + len(held)),
        out_specs=[vmem] * len(out_shape),
        input_output_aliases=aliases,
        cost_estimate=pl.CostEstimate(
            flops=work, bytes_accessed=4 * width * HEAD_SIZE * lanes, transcendentals=0
        ),
        scratch_shapes=scratch,
    )(place, bounds, firsts, *[queries[slot] for slot in slots], *units, *held)


def doc_starts(doc_lengths, positions):
    closing = jnp.cumsum(doc_lengths)
    passed = closing[None, :] <= positions[:, None]
    return jnp.sum(jnp.where(passed, doc_lengths[None, :], 0), axis=1)


def swap(block, k):
    if k == 0:
        return block
    length = lax.axis_size("doc")
    return lax.ppermute(block, "doc", [(i, i ^ k) for i in range(length)])


def on_device(packed_query_rows, packed_key_rows, packed_value_rows, doc_lengths):
    width = KEY_VALUE_HEADS
    chunk = width // HALVES
    docs, parts = lax.axis_size("doc"), lax.axis_size("head")
    index = lax.axis_index("doc")
    member, group = index % width, index // width
    depth = lax.axis_index("head")
    place = jnp.stack([depth, member, group]).astype(jnp.int32)
    rows = packed_query_rows.shape[0]
    blocks = (group * width + jnp.bitwise_xor(member, jnp.arange(width))) * parts + depth
    spots = blocks[:, None] * rows + jnp.arange(rows)[None, :]
    firsts = doc_starts(doc_lengths, spots.reshape(-1)).reshape(width, rows).astype(jnp.int32)
    tables = (firsts[:, 0], firsts)

    def cut(value, k):
        size = value.shape[1] // width
        return lax.dynamic_slice_in_dim(value, jnp.bitwise_xor(member, k) * size, size, 1)

    ring = [(i, (i + 1) % parts) for i in range(parts)]
    pairs = [
        swap(jnp.concatenate([cut(packed_key_rows, k), cut(packed_value_rows, k)], axis=1), k)
        for k in range(width)
    ]
    units = []
    for half in range(HALVES):
        units.append([jnp.stack(pairs[half * chunk : (half + 1) * chunk])])
    queries = [swap(cut(packed_query_rows, k), k) for k in range(width)]
    for _ in range(1, parts):
        for half in range(HALVES):
            units[half].append(lax.ppermute(units[half][-1], "head", ring))

    attends = functools.partial(attend, place, tables, queries)
    everyone = list(range(width))
    state = None
    if docs > width:
        over = [(i, i + width) for i in range(docs - width)]
        for half in range(HALVES):
            far = [lax.ppermute(piece, "doc", over) for piece in units[half]]
            state = attends(far, half, everyone, state, False, parts, back=1)
    for half in range(HALVES - 1):
        state = attends(units[half], half, everyone, state, False, parts)
    results = {}
    for turn in reversed(range(HALVES)):
        slots = list(range(turn * chunk, (turn + 1) * chunk))
        outs = attends(units[HALVES - 1], HALVES - 1, slots, state, True, parts)
        for slot, out in zip(slots, outs):
            results[slot] = swap(out, slot)
    stacked = jnp.stack([results[k] for k in range(width)])
    order = [jnp.bitwise_xor(member, k) for k in range(width)]
    return jnp.concatenate(
        [lax.dynamic_index_in_dim(stacked, order[k], 0, keepdims=False) for k in range(width)],
        axis=1,
    )


def solution(mesh):
    in_specs = (P(("doc", "head"), None), P(("doc", "head"), None), P(("doc", "head"), None), P())
    out_specs = P(("doc", "head"), None)

    return jax.shard_map(
        on_device, mesh=mesh, in_specs=in_specs, out_specs=out_specs, check_vma=False
    )
```

time: 91.3 us -> 83.4 us (0.913)
  Pallas kernels: 25.1 us -> 16.8 us
  local copies, waits for them, and re-layouts: 6.16 us -> 7.76 us
  starting transfers between devices: 30.9 us -> 29.4 us
    pallas_call x3, Pallas kernels: 25.1 us -> 16.8 us  [attend(): pl.pallas_call(functools.partial(attend_kernel, half, back, tuple(slots),...]
    ppermute x21, waiting for transfers between devices: 11.5 us -> 14.6 us  [swap(): return lax.ppermute(block, 'doc', [(i, i ^ k) for i in range(length)])]
    ppermute x6, waiting for transfers between devices: 15.1 us -> 12.8 us  [on_device(): units[half].append(lax.ppermute(units[half][-1], 'head', ring))]
    ppermute x21, starting transfers between devices: 26.9 us -> 25.1 us  [swap(): return lax.ppermute(block, 'doc', [(i, i ^ k) for i in range(length)])]
    unnamed x58 -> x54, local copies, waits for them, and re-layouts: 3.44 us -> 4.5 us
  transfers between devices with their start and end apart: 27 -> 27, of which waited for: 10 -> 11; matrix products, arithmetic and copies ran while one was open for 4% -> 3% of each run, Pallas kernels for 18% -> 13%
where the time goes in v2:
time: 83.4 us; the launch traced here: 83 us
  starting transfers between devices  29.4 us (35%)
  waiting for transfers between devices  27.4 us (33%)
  Pallas kernels  16.8 us (20%)
  local copies, waits for them, and re-layouts  7.76 us (9%)
  other arithmetic  1.11 us (1%)
    ppermute x21, starting transfers between devices, swap(): return lax.ppermute(block, 'doc', [(i, i ^ k) for i in range(length)])  25.1 us
    pallas_call x3, Pallas kernels, attend(): pl.pallas_call(functools.partial(attend_kernel, half, back, tuple(slots),...  16.8 us
    ppermute x21, waiting for transfers between devices, swap(): return lax.ppermute(block, 'doc', [(i, i ^ k) for i in range(length)])  14.6 us
    ppermute x6, waiting for transfers between devices, on_device(): units[half].append(lax.ppermute(units[half][-1], 'head', ring))  12.8 us
    unnamed x54, local copies, waits for them, and re-layouts  4.5 us
    ppermute x6, starting transfers between devices, on_device(): units[half].append(lax.ppermute(units[half][-1], 'head', ring))  4.29 us
    dynamic_slice x2, local copies, waits for them, and re-layouts, cut(): lax.dynamic_slice_in_dim(value, jnp.bitwise_xor(member, k) * size, size, 1)  1.89 us
  transfers between devices with their start and end apart: 27, of which 11 were waited for; matrix products, arithmetic and copies ran while one was open for 3% of the time, Pallas kernels for 13%

profile of v2, /device:TPU:0, one launch (start us, length us, event | category | flops | bytes accessed | tf_op | source)
XLA Modules:
  0.0 83.0 jit_solution(18337670363604336848)
XLA Ops:
  0.0 1.1 %constant_dynamic-slice_fusion.6 = (bf16[128,128]{1,0:T(8,128)(2,1)S(1)}, bf16[128,128]{1,0:T(8,128)(2,1)S(1)}, bf16[128,128]{1,0:T(8,128)(2,1)S(1)}, bf16[128,1...) fusion(bf16[128,1024]{1,0:T(8,128)(2,1)} %param.6, ...), kind=kLoop, calls=%fused_computation.33 | loop fusion | bytes 1048608 | tf_op jit(solution)/shard_map/dynamic_slice | solution.py:205
  1.2 0.6 collective-permute-start.14
  1.7 2.6 %collective-permute-start.15 = (bf16[128,256]{1,0:T(8,128)(2,1)S(1)}, bf16[128,256]{1,0:T(8,128)(2,1)S(1)}, u32[]{:S(2)}, u32[]{:S(2)}) collective-permute-start(bf16[128,256]{1,0:T(8,128)(2,1)S(1)} %pad_maximum_fusion.7), channel_id=1, source_target_pairs={{0,2},{1,3},{2,0},{3,1},{4,6},{5,7},{6,4},{7,5},{8,10},{9,11},{10,... | collective-permute-start | bytes 196616 | tf_op jit(solution)/shard_map/ppermute | solution.py:186
  4.3 0.2 collective-permute-start.16
  4.5 1.8 %collective-permute-start.3 = (bf16[128,256]{1,0:T(8,128)(2,1)S(1)}, bf16[128,256]{1,0:T(8,128)(2,1)S(1)}, u32[]{:S(2)}, u32[]{:S(2)}) collective-permute-start(bf16[128,256]{1,0:T(8,128)(2,1)S(1)} %pad_maximum_fusion.2), channel_id=1, source_target_pairs={{0,4},{1,5},{2,6},{3,7},{4,0},{5,1},{6,2},{7,3},{8,12},{9,13},{10,... | collective-permute-start | bytes 196616 | tf_op jit(solution)/shard_map/ppermute | solution.py:186
  6.3 0.1 collective-permute-start.4
  6.6 2.6 %collective-permute-start.5 = (bf16[128,256]{1,0:T(8,128)(2,1)S(1)}, bf16[128,256]{1,0:T(8,128)(2,1)S(1)}, u32[]{:S(2)}, u32[]{:S(2)}) collective-permute-start(bf16[128,256]{1,0:T(8,128)(2,1)S(1)} %pad_maximum_fusion.4), channel_id=1, source_target_pairs={{0,6},{1,7},{2,4},{3,5},{4,2},{5,3},{6,0},{7,1},{8,14},{9,15},{10,... | collective-permute-start | bytes 196616 | tf_op jit(solution)/shard_map/ppermute | solution.py:186
  9.2 0.0 collective-permute-done.15
  9.2 0.2 collective-permute-start.6
  9.3 0.0 collective-permute-done.16
  9.4 1.7 %collective-permute-start.17 = (bf16[4,128,256]{2,1,0:T(8,128)(2,1)S(1)}, bf16[4,128,256]{2,1,0:T(8,128)(2,1)S(1)}, u32[]{:S(2)}, u32[]{:S(2)}) collective-permute-start(bf16[4,128,256]{2,1,0:T(8,128)(2,1)S(1)} %pad_maximum_fusion.1.refs_8_), channel_id=1, source_target_pairs={{0,8},{8,16},{16,24},{24,0},{1,9},{9,17},{17,25},{25,1},{2,10},{10... | collective-permute-start | bytes 786440 | tf_op jit(solution)/shard_map/ppermute | solution.py:218
  11.1 0.0 collective-permute-done.3
  11.1 0.0 collective-permute-done.4
  11.1 0.9 %collective-permute-done.5 = bf16[128,256]{1,0:T(8,128)(2,1)S(1)} collective-permute-done((bf16[128,256]{1,0:T(8,128)(2,1)S(1)}, bf16[128,256]{1,0:T(8,128)(2,1)S(1)}, u32[]{:S(2)}, u32[]{:S(2)}) %collective-permute-start.5) | collective-permute-done | bytes 65568 | tf_op jit(solution)/shard_map/ppermute | solution.py:186
  12.0 2.1 %collective-permute-done.6 = bf16[128,256]{1,0:T(8,128)(2,1)S(1)} collective-permute-done((bf16[128,256]{1,0:T(8,128)(2,1)S(1)}, bf16[128,256]{1,0:T(8,128)(2,1)S(1)}, u32[]{:S(2)}, u32[]{:S(2)}) %collective-permute-start.6) | collective-permute-done | bytes 65568 | tf_op jit(solution)/shard_map/ppermute | solution.py:186
  14.1 0.0 copy-start.3
  14.1 1.6 %collective-permute-start.7 = (bf16[4,128,256]{2,1,0:T(8,128)(2,1)S(1)}, bf16[4,128,256]{2,1,0:T(8,128)(2,1)S(1)}, u32[]{:S(2)}, u32[]{:S(2)}) collective-permute-start(bf16[4,128,256]{2,1,0:T(8,128)(2,1)S(1)} %pad_maximum_fusion.refs_4_), channel_id=1, source_target_pairs={{0,8},{8,16},{16,24},{24,0},{1,9},{9,17},{17,25},{25,1},{2,10},{10... | collective-permute-start | bytes 786440 | tf_op jit(solution)/shard_map/ppermute | solution.py:218
  15.7 0.8 constant_dynamic-slice_fusion.8
  16.5 0.0 collective-permute-start
  16.5 0.9 %collective-permute-start.1 = (bf16[128,512]{1,0:T(8,128)(2,1)S(1)}, bf16[128,512]{1,0:T(8,128)(2,1)S(1)}, u32[]{:S(2)}, u32[]{:S(2)}) collective-permute-start(bf16[128,512]{1,0:T(8,128)(2,1)S(1)} %get-tuple-element.29), channel_id=1, source_target_pairs={{0,2},{1,3},{2,0},{3,1},{4,6},{5,7},{6,4},{7,5},{8,10},{9,11},{10,... | collective-permute-start | bytes 393224 | tf_op jit(solution)/shard_map/ppermute | solution.py:186
  17.4 1.2 %collective-permute-start.10 = (bf16[128,512]{1,0:T(8,128)(2,1)S(1)}, bf16[128,512]{1,0:T(8,128)(2,1)S(1)}, u32[]{:S(2)}, u32[]{:S(2)}) collective-permute-start(bf16[128,512]{1,0:T(8,128)(2,1)S(1)} %get-tuple-element.27), channel_id=1, source_target_pairs={{0,4},{1,5},{2,6},{3,7},{4,0},{5,1},{6,2},{7,3},{8,12},{9,13},{10,... | collective-permute-start | bytes 393224 | tf_op jit(solution)/shard_map/ppermute | solution.py:186
  18.5 1.8 %collective-permute-done.17.refs_9_ = bf16[4,128,256]{2,1,0:T(8,128)(2,1)S(1)} collective-permute-done((bf16[4,128,256]{2,1,0:T(8,128)(2,1)S(1)}, bf16[4,128,256]{2,1,0:T(8,128)(2,1)S(1)}, u32[]{:S(2)}, u32[]{:S(2)}) %collective-permute-start.17) | collective-permute-done | bytes 262176 | tf_op jit(solution)/shard_map/ppermute | solution.py:218
  20.3 0.3 collective-permute-start.11
  20.7 5.2 %collective-permute-done.7.refs_5_ = bf16[4,128,256]{2,1,0:T(8,128)(2,1)S(1)} collective-permute-done((bf16[4,128,256]{2,1,0:T(8,128)(2,1)S(1)}, bf16[4,128,256]{2,1,0:T(8,128)(2,1)S(1)}, u32[]{:S(2)}, u32[]{:S(2)}) %collective-permute-start.7) | collective-permute-done | bytes 262176 | tf_op jit(solution)/shard_map/ppermute | solution.py:218
  25.9 0.0 collective-permute-start.8
  25.9 0.1 add_bitcast_fusion
  26.0 0.1 copy.7
  26.1 0.1 reduce
  26.2 5.3 %collective-permute-done.18.refs_10_ = bf16[4,128,256]{2,1,0:T(8,128)(2,1)S(1)} collective-permute-done((bf16[4,128,256]{2,1,0:T(8,128)(2,1)S(1)}, bf16[4,128,256]{2,1,0:T(8,128)(2,1)S(1)}, u32[]{:S(2)}, u32[]{:S(2)}) %collective-permute-start.18) | collective-permute-done | bytes 262176 | tf_op jit(solution)/shard_map/ppermute | solution.py:218
  31.5 0.1 select_reduce_fusion
  31.7 2.7 %collective-permute-start.12 = (bf16[128,512]{1,0:T(8,128)(2,1)S(1)}, bf16[128,512]{1,0:T(8,128)(2,1)S(1)}, u32[]{:S(2)}, u32[]{:S(2)}) collective-permute-start(bf16[128,512]{1,0:T(8,128)(2,1)S(1)} %get-tuple-element.32), channel_id=1, source_target_pairs={{0,6},{1,7},{2,4},{3,5},{4,2},{5,3},{6,0},{7,1},{8,14},{9,15},{10,... | collective-permute-start | bytes 393224 | tf_op jit(solution)/shard_map/ppermute | solution.py:186
  34.4 0.0 collective-permute-done.10.refs_4_.refs_0_
  34.4 0.0 collective-permute-done.11.refs_5_.refs_1_
  34.4 1.7 %collective-permute-start.2 = (bf16[128,512]{1,0:T(8,128)(2,1)S(1)}, bf16[128,512]{1,0:T(8,128)(2,1)S(1)}, u32[]{:S(2)}, u32[]{:S(2)}) collective-permute-start(bf16[128,512]{1,0:T(8,128)(2,1)S(1)} %get-tuple-element.28), channel_id=1, source_target_pairs={{0,3},{1,2},{2,1},{3,0},{4,7},{5,6},{6,5},{7,4},{8,11},{9,10},{10,... | collective-permute-start | bytes 393224 | tf_op jit(solution)/shard_map/ppermute | solution.py:186
  36.1 0.6 slice_reduce_fusion.bounds_ref
  36.7 0.4 collective-permute-done.8.refs_6_
  37.2 0.9 %collective-permute-start.9 = (bf16[4,128,256]{2,1,0:T(8,128)(2,1)S(1)}, bf16[4,128,256]{2,1,0:T(8,128)(2,1)}, u32[]{:S(2)}, u32[]{:S(2)}) collective-permute-start(bf16[4,128,256]{2,1,0:T(8,128)(2,1)S(1)} %collective-permute-done.8.refs_6_), channel_id=1, source_target_pairs={{0,8},{8,16},{16,24},{24,0},{1,9},{9,17},{17,25},{25,1},{2,10},{10... | collective-permute-start | bytes 786440 | tf_op jit(solution)/shard_map/ppermute | solution.py:218
  38.1 0.6 pad_add_fusion.place_ref
  38.7 0.0 collective-permute-done.12.refs_6_.refs_2_
  38.7 2.4 %collective-permute-done.13.refs_7_.refs_3_ = bf16[128,512]{1,0:T(8,128)(2,1)S(1)} collective-permute-done((bf16[128,512]{1,0:T(8,128)(2,1)S(1)}, bf16[128,512]{1,0:T(8,128)(2,1)S(1)}, u32[]{:S(2)}, u32[]{:S(2)}) %collective-permute-start.13) | collective-permute-done | bytes 131104 | tf_op jit(solution)/shard_map/ppermute | solution.py:186
  41.1 1.8 %collective-permute-done.2.refs_3_ = bf16[128,512]{1,0:T(8,128)(2,1)S(1)} collective-permute-done((bf16[128,512]{1,0:T(8,128)(2,1)S(1)}, bf16[128,512]{1,0:T(8,128)(2,1)S(1)}, u32[]{:S(2)}, u32[]{:S(2)}) %collective-permute-start.2) | collective-permute-done | bytes 131104 | tf_op jit(solution)/shard_map/ppermute | solution.py:186
  42.9 0.0 collective-permute-done.19.refs_11_
  43.0 0.6 copy-done.17
  43.6 0.7 copy-done.12
  44.3 8.0 %shard_map.46 = (f32[8,128,512]{2,1,0:T(8,128)S(1)}, f32[8,8,512]{2,1,0:T(8,128)S(1)}) custom-call(s32[3]{0:T(128)} %pad_add_fusion.place_ref, s32[8]{0:T(128)} %slice_reduce_fusion.bounds_ref, s32[8,128]{1,0:T(8,128)} %bitcast.56, bf16[128,512]{1,0:T(8,128)(2,1)} %get-tuple-element.31.refs_0_, bf16[128,512]{1,0:T(8,128)(2,1)} %copy-done.13, ...), custom_call_target="tpu_custom_call" | custom-call | flops 2147483648 | bytes 2097152 | tf_op jit(solution)/shard_map/pallas_call | solution.py:163
  52.4 1.3 %copy-done = f32[8,128,512]{2,1,0:T(8,128)} copy-done((f32[8,128,512]{2,1,0:T(8,128)}, f32[8,128,512]{2,1,0:T(8,128)S(1)}, u32[]{:S(2)}) %copy-start) | copy-done | bytes 2097176
  53.7 0.6 copy-done.1
  54.4 0.0 collective-permute-done.9.refs_7_
  54.4 6.3 %shard_map.48 = (bf16[128,512]{1,0:T(8,128)(2,1)S(1)}, bf16[128,512]{1,0:T(8,128)(2,1)S(1)}, bf16[128,512]{1,0:T(8,128)(2,1)S(1)}, bf16[128,512]{1,0:T(8,128)(2,1)S(1)}) custom-call(s32[3]{0:T(128)} %pad_add_fusion.place_ref, s32[8]{0:T(128)} %slice_reduce_fusion.bounds_ref, s32[8,128]{1,0:T(8,128)} %bitcast.57, bf16[128,512]{1,0:T(8,128)(2,1)} %copy-done.15, ...), custom_call_target="tpu_custom_call" | custom-call | flops 1073741824 | bytes 2097152 | tf_op jit(solution)/shard_map/pallas_call | solution.py:163
  60.7 0.1 collective-permute-start.23
  60.7 2.5 %shard_map.47 = (bf16[128,512]{1,0:T(8,128)(2,1)S(1)}, bf16[128,512]{1,0:T(8,128)(2,1)S(1)}, bf16[128,512]{1,0:T(8,128)(2,1)S(1)}, bf16[128,512]{1,0:T(8,128)(2,1)S(1)}) custom-call(s32[3]{0:T(128)} %pad_add_fusion.place_ref, s32[8]{0:T(128)} %slice_reduce_fusion.bounds_ref, s32[8,128]{1,0:T(8,128)} %bitcast.58, bf16[128,512]{1,0:T(8,128)(2,1)} %get-tuple-element.31.refs_0_, ...), custom_call_target="tpu_custom_call" | custom-call | flops 1073741824 | bytes 2097152 | tf_op jit(solution)/shard_map/pallas_call | solution.py:163
  63.3 0.8 collective-permute-start.20
  64.1 1.2 %collective-permute-start.21 = (bf16[128,512]{1,0:T(8,128)(2,1)S(1)}, bf16[128,512]{1,0:T(8,128)(2,1)S(1)}, u32[]{:S(2)}, u32[]{:S(2)}) collective-permute-start(bf16[128,512]{1,0:T(8,128)(2,1)S(1)} %get-tuple-element.19), channel_id=1, source_target_pairs={{0,2},{1,3},{2,0},{3,1},{4,6},{5,7},{6,4},{7,5},{8,10},{9,11},{10,... | collective-permute-start | bytes 393224 | tf_op jit(solution)/shard_map/ppermute | solution.py:186
  65.3 0.2 collective-permute-start.22
  65.5 5.0 %collective-permute-start.24 = (bf16[128,512]{1,0:T(8,128)(2,1)S(1)}, bf16[128,512]{1,0:T(8,128)(2,1)S(1)}, u32[]{:S(2)}, u32[]{:S(2)}) collective-permute-start(bf16[128,512]{1,0:T(8,128)(2,1)S(1)} %get-tuple-element.22), channel_id=1, source_target_pairs={{0,5},{1,4},{2,7},{3,6},{4,1},{5,0},{6,3},{7,2},{8,13},{9,12},{10,... | collective-permute-start | bytes 393224 | tf_op jit(solution)/shard_map/ppermute | solution.py:186
  70.5 0.4 collective-permute-start.25
  70.9 2.8 %collective-permute-start.26 = (bf16[128,512]{1,0:T(8,128)(2,1)S(1)}, bf16[128,512]{1,0:T(8,128)(2,1)S(1)}, u32[]{:S(2)}, u32[]{:S(2)}) collective-permute-start(bf16[128,512]{1,0:T(8,128)(2,1)S(1)} %get-tuple-element.24), channel_id=1, source_target_pairs={{0,7},{1,6},{2,5},{3,4},{4,3},{5,2},{6,1},{7,0},{8,15},{9,14},{10,... | collective-permute-start | bytes 393224 | tf_op jit(solution)/shard_map/ppermute | solution.py:186
  73.7 0.0 collective-permute-done.23
  73.7 5.4 %collective-permute-done.24 = bf16[128,512]{1,0:T(8,128)(2,1)S(1)} collective-permute-done((bf16[128,512]{1,0:T(8,128)(2,1)S(1)}, bf16[128,512]{1,0:T(8,128)(2,1)S(1)}, u32[]{:S(2)}, u32[]{:S(2)}) %collective-permute-start.24) | collective-permute-done | bytes 131104 | tf_op jit(solution)/shard_map/ppermute | solution.py:186
  79.1 1.0 %collective-permute-done.25 = bf16[128,512]{1,0:T(8,128)(2,1)S(1)} collective-permute-done((bf16[128,512]{1,0:T(8,128)(2,1)S(1)}, bf16[128,512]{1,0:T(8,128)(2,1)S(1)}, u32[]{:S(2)}, u32[]{:S(2)}) %collective-permute-start.25) | collective-permute-done | bytes 131104 | tf_op jit(solution)/shard_map/ppermute | solution.py:186
  80.2 1.0 %collective-permute-done.26 = bf16[128,512]{1,0:T(8,128)(2,1)S(1)} collective-permute-done((bf16[128,512]{1,0:T(8,128)(2,1)S(1)}, bf16[128,512]{1,0:T(8,128)(2,1)S(1)}, u32[]{:S(2)}, u32[]{:S(2)}) %collective-permute-start.26) | collective-permute-done | bytes 131104 | tf_op jit(solution)/shard_map/ppermute | solution.py:186
  81.4 0.0 copy-start.5
  81.4 1.0 %copy-done.5 = bf16[128,4096]{1,0:T(8,128)(2,1)} copy-done((bf16[128,4096]{1,0:T(8,128)(2,1)}, bf16[128,4096]{1,0:T(8,128)(2,1)S(1)}, u32[]{:S(2)}) %copy-start.5) | copy-done | bytes 1048600
  82.3 0.7 bitcast_dynamic-update-slice_fusion
  (69 shorter events, 0.5 us)
Async XLA Ops:
  0.0 15.7 %copy-start.2 = (bf16[128,4096]{1,0:T(8,128)(2,1)S(1)}, bf16[128,4096]{1,0:T(8,128)(2,1)}, u32[]{:S(2)}) copy-start(bf16[128,4096]{1,0:T(8,128)(2,1)} %param.4) | copy-start | bytes 3145732
  1.2 5.4 %collective-permute-start.14 = (bf16[128,256]{1,0:T(8,128)(2,1)S(1)}, bf16[128,256]{1,0:T(8,128)(2,1)S(1)}, u32[]{:S(2)}, u32[]{:S(2)}) collective-permute-start(bf16[128,256]{1,0:T(8,128)(2,1)S(1)} %pad_maximum_fusion.6), channel_id=1, source_target_pairs={{0,1},{1,0},{2,3},{3,2},{4,5},{5,4},{6,7},{7,6},{8,9},{9,8},{10,11... | collective-permute-start | bytes 196616 | tf_op jit(solution)/shard_map/ppermute | solution.py:186
  1.7 24.3 %copy-start.7 = (s32[16]{0:T(128)S(1)}, s32[16]{0:T(128)}, u32[]{:S(2)}) copy-start(s32[16]{0:T(128)} %param.7) | copy-start | bytes 196
  1.7 7.4 %collective-permute-start.15 = (bf16[128,256]{1,0:T(8,128)(2,1)S(1)}, bf16[128,256]{1,0:T(8,128)(2,1)S(1)}, u32[]{:S(2)}, u32[]{:S(2)}) collective-permute-start(bf16[128,256]{1,0:T(8,128)(2,1)S(1)} %pad_maximum_fusion.7), channel_id=1, source_target_pairs={{0,2},{1,3},{2,0},{3,1},{4,6},{5,7},{6,4},{7,5},{8,10},{9,11},{10,... | collective-permute-start | bytes 196616 | tf_op jit(solution)/shard_map/ppermute | solution.py:186
  4.3 5.0 %collective-permute-start.16 = (bf16[128,256]{1,0:T(8,128)(2,1)S(1)}, bf16[128,256]{1,0:T(8,128)(2,1)S(1)}, u32[]{:S(2)}, u32[]{:S(2)}) collective-permute-start(bf16[128,256]{1,0:T(8,128)(2,1)S(1)} %pad_maximum_fusion.8), channel_id=1, source_target_pairs={{0,3},{1,2},{2,1},{3,0},{4,7},{5,6},{6,5},{7,4},{8,11},{9,10},{10,... | collective-permute-start | bytes 196616 | tf_op jit(solution)/shard_map/ppermute | solution.py:186
  4.5 6.6 %collective-permute-start.3 = (bf16[128,256]{1,0:T(8,128)(2,1)S(1)}, bf16[128,256]{1,0:T(8,128)(2,1)S(1)}, u32[]{:S(2)}, u32[]{:S(2)}) collective-permute-start(bf16[128,256]{1,0:T(8,128)(2,1)S(1)} %pad_maximum_fusion.2), channel_id=1, source_target_pairs={{0,4},{1,5},{2,6},{3,7},{4,0},{5,1},{6,2},{7,3},{8,12},{9,13},{10,... | collective-permute-start | bytes 196616 | tf_op jit(solution)/shard_map/ppermute | solution.py:186
  6.3 4.8 %collective-permute-start.4 = (bf16[128,256]{1,0:T(8,128)(2,1)S(1)}, bf16[128,256]{1,0:T(8,128)(2,1)S(1)}, u32[]{:S(2)}, u32[]{:S(2)}) collective-permute-start(bf16[128,256]{1,0:T(8,128)(2,1)S(1)} %pad_maximum_fusion.3), channel_id=1, source_target_pairs={{0,5},{1,4},{2,7},{3,6},{4,1},{5,0},{6,3},{7,2},{8,13},{9,12},{10,... | collective-permute-start | bytes 196616 | tf_op jit(solution)/shard_map/ppermute | solution.py:186
  6.6 5.4 %collective-permute-start.5 = (bf16[128,256]{1,0:T(8,128)(2,1)S(1)}, bf16[128,256]{1,0:T(8,128)(2,1)S(1)}, u32[]{:S(2)}, u32[]{:S(2)}) collective-permute-start(bf16[128,256]{1,0:T(8,128)(2,1)S(1)} %pad_maximum_fusion.4), channel_id=1, source_target_pairs={{0,6},{1,7},{2,4},{3,5},{4,2},{5,3},{6,0},{7,1},{8,14},{9,15},{10,... | collective-permute-start | bytes 196616 | tf_op jit(solution)/shard_map/ppermute | solution.py:186
  9.2 4.9 %collective-permute-start.6 = (bf16[128,256]{1,0:T(8,128)(2,1)S(1)}, bf16[128,256]{1,0:T(8,128)(2,1)S(1)}, u32[]{:S(2)}, u32[]{:S(2)}) collective-permute-start(bf16[128,256]{1,0:T(8,128)(2,1)S(1)} %pad_maximum_fusion.5), channel_id=1, source_target_pairs={{0,7},{1,6},{2,5},{3,4},{4,3},{5,2},{6,1},{7,0},{8,15},{9,14},{10,... | collective-permute-start | bytes 196616 | tf_op jit(solution)/shard_map/ppermute | solution.py:186
  9.4 34.9 %copy-start.4 = (bf16[4,128,256]{2,1,0:T(8,128)(2,1)}, bf16[4,128,256]{2,1,0:T(8,128)(2,1)S(1)}, u32[]{:S(2)}) copy-start(bf16[4,128,256]{2,1,0:T(8,128)(2,1)S(1)} %pad_maximum_fusion.1.refs_8_) | copy-start | bytes 786436
  9.4 10.9 %collective-permute-start.17 = (bf16[4,128,256]{2,1,0:T(8,128)(2,1)S(1)}, bf16[4,128,256]{2,1,0:T(8,128)(2,1)S(1)}, u32[]{:S(2)}, u32[]{:S(2)}) collective-permute-start(bf16[4,128,256]{2,1,0:T(8,128)(2,1)S(1)} %pad_maximum_fusion.1.refs_8_), channel_id=1, source_target_pairs={{0,8},{8,16},{16,24},{24,0},{1,9},{9,17},{17,25},{25,1},{2,10},{10... | collective-permute-start | bytes 786440 | tf_op jit(solution)/shard_map/ppermute | solution.py:218
  14.1 38.2 %copy-start.3 = (bf16[4,128,256]{2,1,0:T(8,128)(2,1)}, bf16[4,128,256]{2,1,0:T(8,128)(2,1)S(1)}, u32[]{:S(2)}) copy-start(bf16[4,128,256]{2,1,0:T(8,128)(2,1)S(1)} %pad_maximum_fusion.refs_4_) | copy-start | bytes 786436
  14.1 11.8 %collective-permute-start.7 = (bf16[4,128,256]{2,1,0:T(8,128)(2,1)S(1)}, bf16[4,128,256]{2,1,0:T(8,128)(2,1)S(1)}, u32[]{:S(2)}, u32[]{:S(2)}) collective-permute-start(bf16[4,128,256]{2,1,0:T(8,128)(2,1)S(1)} %pad_maximum_fusion.refs_4_), channel_id=1, source_target_pairs={{0,8},{8,16},{16,24},{24,0},{1,9},{9,17},{17,25},{25,1},{2,10},{10... | collective-permute-start | bytes 786440 | tf_op jit(solution)/shard_map/ppermute | solution.py:218
  16.5 3.8 %collective-permute-start = (bf16[128,512]{1,0:T(8,128)(2,1)S(1)}, bf16[128,512]{1,0:T(8,128)(2,1)S(1)}, u32[]{:S(2)}, u32[]{:S(2)}) collective-permute-start(bf16[128,512]{1,0:T(8,128)(2,1)S(1)} %get-tuple-element.30), channel_id=1, source_target_pairs={{0,1},{1,0},{2,3},{3,2},{4,5},{5,4},{6,7},{7,6},{8,9},{9,8},{10,11... | collective-permute-start | bytes 393224 | tf_op jit(solution)/shard_map/ppermute | solution.py:186
  16.5 15.1 %collective-permute-start.1 = (bf16[128,512]{1,0:T(8,128)(2,1)S(1)}, bf16[128,512]{1,0:T(8,128)(2,1)S(1)}, u32[]{:S(2)}, u32[]{:S(2)}) collective-permute-start(bf16[128,512]{1,0:T(8,128)(2,1)S(1)} %get-tuple-element.29), channel_id=1, source_target_pairs={{0,2},{1,3},{2,0},{3,1},{4,6},{5,7},{6,4},{7,5},{8,10},{9,11},{10,... | collective-permute-start | bytes 393224 | tf_op jit(solution)/shard_map/ppermute | solution.py:186
  17.4 17.0 %collective-permute-start.10 = (bf16[128,512]{1,0:T(8,128)(2,1)S(1)}, bf16[128,512]{1,0:T(8,128)(2,1)S(1)}, u32[]{:S(2)}, u32[]{:S(2)}) collective-permute-start(bf16[128,512]{1,0:T(8,128)(2,1)S(1)} %get-tuple-element.27), channel_id=1, source_target_pairs={{0,4},{1,5},{2,6},{3,7},{4,0},{5,1},{6,2},{7,3},{8,12},{9,13},{10,... | collective-permute-start | bytes 393224 | tf_op jit(solution)/shard_map/ppermute | solution.py:186
  20.3 24.0 %copy-start.9 = (bf16[4,128,256]{2,1,0:T(8,128)(2,1)}, bf16[4,128,256]{2,1,0:T(8,128)(2,1)S(1)}, u32[]{:S(2)}) copy-start(bf16[4,128,256]{2,1,0:T(8,128)(2,1)S(1)} %collective-permute-done.17.refs_9_) | copy-start | bytes 786436
  20.3 11.2 %collective-permute-start.18 = (bf16[4,128,256]{2,1,0:T(8,128)(2,1)S(1)}, bf16[4,128,256]{2,1,0:T(8,128)(2,1)S(1)}, u32[]{:S(2)}, u32[]{:S(2)}) collective-permute-start(bf16[4,128,256]{2,1,0:T(8,128)(2,1)S(1)} %collective-permute-done.17.refs_9_), channel_id=1, source_target_pairs={{0,8},{8,16},{16,24},{24,0},{1,9},{9,17},{17,25},{25,1},{2,10},{10... | collective-permute-start | bytes 786440 | tf_op jit(solution)/shard_map/ppermute | solution.py:218
  20.3 22.6 %copy-start.13 = (bf16[128,512]{1,0:T(8,128)(2,1)}, bf16[128,512]{1,0:T(8,128)(2,1)S(1)}, u32[]{:S(2)}) copy-start(bf16[128,512]{1,0:T(8,128)(2,1)S(1)} %collective-permute-done.refs_1_) | copy-start | bytes 393220
  20.3 14.1 %collective-permute-start.11 = (bf16[128,512]{1,0:T(8,128)(2,1)S(1)}, bf16[128,512]{1,0:T(8,128)(2,1)S(1)}, u32[]{:S(2)}, u32[]{:S(2)}) collective-permute-start(bf16[128,512]{1,0:T(8,128)(2,1)S(1)} %get-tuple-element.26), channel_id=1, source_target_pairs={{0,5},{1,4},{2,7},{3,6},{4,1},{5,0},{6,3},{7,2},{8,13},{9,12},{10,... | collective-permute-start | bytes 393224 | tf_op jit(solution)/shard_map/ppermute | solution.py:186
  25.9 28.5 %copy-start.8 = (bf16[4,128,256]{2,1,0:T(8,128)(2,1)}, bf16[4,128,256]{2,1,0:T(8,128)(2,1)S(1)}, u32[]{:S(2)}) copy-start(bf16[4,128,256]{2,1,0:T(8,128)(2,1)S(1)} %collective-permute-done.7.refs_5_) | copy-start | bytes 786436
  25.9 11.2 %collective-permute-start.8 = (bf16[4,128,256]{2,1,0:T(8,128)(2,1)S(1)}, bf16[4,128,256]{2,1,0:T(8,128)(2,1)S(1)}, u32[]{:S(2)}, u32[]{:S(2)}) collective-permute-start(bf16[4,128,256]{2,1,0:T(8,128)(2,1)S(1)} %collective-permute-done.7.refs_5_), channel_id=1, source_target_pairs={{0,8},{8,16},{16,24},{24,0},{1,9},{9,17},{17,25},{25,1},{2,10},{10... | collective-permute-start | bytes 786440 | tf_op jit(solution)/shard_map/ppermute | solution.py:218
  31.5 11.4 %copy-start.11 = (bf16[4,128,256]{2,1,0:T(8,128)(2,1)}, bf16[4,128,256]{2,1,0:T(8,128)(2,1)S(1)}, u32[]{:S(2)}) copy-start(bf16[4,128,256]{2,1,0:T(8,128)(2,1)S(1)} %collective-permute-done.18.refs_10_) | copy-start | bytes 786436
  31.5 11.4 %collective-permute-start.19 = (bf16[4,128,256]{2,1,0:T(8,128)(2,1)S(1)}, bf16[4,128,256]{2,1,0:T(8,128)(2,1)S(1)}, u32[]{:S(2)}, u32[]{:S(2)}) collective-permute-start(bf16[4,128,256]{2,1,0:T(8,128)(2,1)S(1)} %collective-permute-done.18.refs_10_), channel_id=1, source_target_pairs={{0,8},{8,16},{16,24},{24,0},{1,9},{9,17},{17,25},{25,1},{2,10},{10... | collective-permute-start | bytes 786440 | tf_op jit(solution)/shard_map/ppermute | solution.py:218
  31.6 12.7 %copy-start.6 = (s32[1024]{0:T(1024)}, s32[1024]{0:T(1024)S(1)}, u32[]{:S(2)}) copy-start(s32[1024]{0:T(1024)S(1)} %select_reduce_fusion) | copy-start | bytes 12292
  31.6 11.3 %copy-start.14 = (bf16[128,512]{1,0:T(8,128)(2,1)}, bf16[128,512]{1,0:T(8,128)(2,1)S(1)}, u32[]{:S(2)}) copy-start(bf16[128,512]{1,0:T(8,128)(2,1)S(1)} %collective-permute-done.1.refs_2_) | copy-start | bytes 393220
  31.7 7.1 %collective-permute-start.12 = (bf16[128,512]{1,0:T(8,128)(2,1)S(1)}, bf16[128,512]{1,0:T(8,128)(2,1)S(1)}, u32[]{:S(2)}, u32[]{:S(2)}) collective-permute-start(bf16[128,512]{1,0:T(8,128)(2,1)S(1)} %get-tuple-element.32), channel_id=1, source_target_pairs={{0,6},{1,7},{2,4},{3,5},{4,2},{5,3},{6,0},{7,1},{8,14},{9,15},{10,... | collective-permute-start | bytes 393224 | tf_op jit(solution)/shard_map/ppermute | solution.py:186
  34.4 8.6 %copy-start.15 = (bf16[128,512]{1,0:T(8,128)(2,1)}, bf16[128,512]{1,0:T(8,128)(2,1)S(1)}, u32[]{:S(2)}) copy-start(bf16[128,512]{1,0:T(8,128)(2,1)S(1)} %collective-permute-done.10.refs_4_.refs_0_) | copy-start | bytes 393220
  34.4 6.7 %collective-permute-start.13 = (bf16[128,512]{1,0:T(8,128)(2,1)S(1)}, bf16[128,512]{1,0:T(8,128)(2,1)S(1)}, u32[]{:S(2)}, u32[]{:S(2)}) collective-permute-start(bf16[128,512]{1,0:T(8,128)(2,1)S(1)} %get-tuple-element.25), channel_id=1, source_target_pairs={{0,7},{1,6},{2,5},{3,4},{4,3},{5,2},{6,1},{7,0},{8,15},{9,14},{10,... | collective-permute-start | bytes 393224 | tf_op jit(solution)/shard_map/ppermute | solution.py:186
  34.4 8.6 %copy-start.16 = (bf16[128,512]{1,0:T(8,128)(2,1)}, bf16[128,512]{1,0:T(8,128)(2,1)S(1)}, u32[]{:S(2)}) copy-start(bf16[128,512]{1,0:T(8,128)(2,1)S(1)} %collective-permute-done.11.refs_5_.refs_1_) | copy-start | bytes 393220
  34.4 8.5 %collective-permute-start.2 = (bf16[128,512]{1,0:T(8,128)(2,1)S(1)}, bf16[128,512]{1,0:T(8,128)(2,1)S(1)}, u32[]{:S(2)}, u32[]{:S(2)}) collective-permute-start(bf16[128,512]{1,0:T(8,128)(2,1)S(1)} %get-tuple-element.28), channel_id=1, source_target_pairs={{0,3},{1,2},{2,1},{3,0},{4,7},{5,6},{6,5},{7,4},{8,11},{9,10},{10,... | collective-permute-start | bytes 393224 | tf_op jit(solution)/shard_map/ppermute | solution.py:186
  37.2 15.2 %copy-start.10 = (bf16[4,128,256]{2,1,0:T(8,128)(2,1)}, bf16[4,128,256]{2,1,0:T(8,128)(2,1)S(1)}, u32[]{:S(2)}) copy-start(bf16[4,128,256]{2,1,0:T(8,128)(2,1)S(1)} %collective-permute-done.8.refs_6_) | copy-start | bytes 786436
  37.2 17.2 %collective-permute-start.9 = (bf16[4,128,256]{2,1,0:T(8,128)(2,1)S(1)}, bf16[4,128,256]{2,1,0:T(8,128)(2,1)}, u32[]{:S(2)}, u32[]{:S(2)}) collective-permute-start(bf16[4,128,256]{2,1,0:T(8,128)(2,1)S(1)} %collective-permute-done.8.refs_6_), channel_id=1, source_target_pairs={{0,8},{8,16},{16,24},{24,0},{1,9},{9,17},{17,25},{25,1},{2,10},{10... | collective-permute-start | bytes 786440 | tf_op jit(solution)/shard_map/ppermute | solution.py:218
  38.7 4.3 %copy-start.18 = (bf16[128,512]{1,0:T(8,128)(2,1)}, bf16[128,512]{1,0:T(8,128)(2,1)S(1)}, u32[]{:S(2)}) copy-start(bf16[128,512]{1,0:T(8,128)(2,1)S(1)} %collective-permute-done.12.refs_6_.refs_2_) | copy-start | bytes 393220
  41.1 1.9 %copy-start.19 = (bf16[128,512]{1,0:T(8,128)(2,1)}, bf16[128,512]{1,0:T(8,128)(2,1)S(1)}, u32[]{:S(2)}) copy-start(bf16[128,512]{1,0:T(8,128)(2,1)S(1)} %collective-permute-done.13.refs_7_.refs_3_) | copy-start | bytes 393220
  42.9 0.6 copy-start.17
  43.6 0.7 copy-start.12
  52.4 1.4 %copy-start = (f32[8,128,512]{2,1,0:T(8,128)}, f32[8,128,512]{2,1,0:T(8,128)S(1)}, u32[]{:S(2)}) copy-start(f32[8,128,512]{2,1,0:T(8,128)S(1)} %get-tuple-element.15.refs_8_) | copy-start | bytes 6291460
  53.7 0.6 copy-start.1
  60.7 13.0 %collective-permute-start.23 = (bf16[128,512]{1,0:T(8,128)(2,1)S(1)}, bf16[128,512]{1,0:T(8,128)(2,1)S(1)}, u32[]{:S(2)}, u32[]{:S(2)}) collective-permute-start(bf16[128,512]{1,0:T(8,128)(2,1)S(1)} %get-tuple-element.21), channel_id=1, source_target_pairs={{0,4},{1,5},{2,6},{3,7},{4,0},{5,1},{6,2},{7,3},{8,12},{9,13},{10,... | collective-permute-start | bytes 393224 | tf_op jit(solution)/shard_map/ppermute | solution.py:186
  63.3 7.2 %collective-permute-start.20 = (bf16[128,512]{1,0:T(8,128)(2,1)S(1)}, bf16[128,512]{1,0:T(8,128)(2,1)S(1)}, u32[]{:S(2)}, u32[]{:S(2)}) collective-permute-start(bf16[128,512]{1,0:T(8,128)(2,1)S(1)} %get-tuple-element.18), channel_id=1, source_target_pairs={{0,1},{1,0},{2,3},{3,2},{4,5},{5,4},{6,7},{7,6},{8,9},{9,8},{10,11... | collective-permute-start | bytes 393224 | tf_op jit(solution)/shard_map/ppermute | solution.py:186
  64.1 6.8 %collective-permute-start.21 = (bf16[128,512]{1,0:T(8,128)(2,1)S(1)}, bf16[128,512]{1,0:T(8,128)(2,1)S(1)}, u32[]{:S(2)}, u32[]{:S(2)}) collective-permute-start(bf16[128,512]{1,0:T(8,128)(2,1)S(1)} %get-tuple-element.19), channel_id=1, source_target_pairs={{0,2},{1,3},{2,0},{3,1},{4,6},{5,7},{6,4},{7,5},{8,10},{9,11},{10,... | collective-permute-start | bytes 393224 | tf_op jit(solution)/shard_map/ppermute | solution.py:186
  65.3 8.4 %collective-permute-start.22 = (bf16[128,512]{1,0:T(8,128)(2,1)S(1)}, bf16[128,512]{1,0:T(8,128)(2,1)S(1)}, u32[]{:S(2)}, u32[]{:S(2)}) collective-permute-start(bf16[128,512]{1,0:T(8,128)(2,1)S(1)} %get-tuple-element.20), channel_id=1, source_target_pairs={{0,3},{1,2},{2,1},{3,0},{4,7},{5,6},{6,5},{7,4},{8,11},{9,10},{10,... | collective-permute-start | bytes 393224 | tf_op jit(solution)/shard_map/ppermute | solution.py:186
  65.5 13.6 %collective-permute-start.24 = (bf16[128,512]{1,0:T(8,128)(2,1)S(1)}, bf16[128,512]{1,0:T(8,128)(2,1)S(1)}, u32[]{:S(2)}, u32[]{:S(2)}) collective-permute-start(bf16[128,512]{1,0:T(8,128)(2,1)S(1)} %get-tuple-element.22), channel_id=1, source_target_pairs={{0,5},{1,4},{2,7},{3,6},{4,1},{5,0},{6,3},{7,2},{8,13},{9,12},{10,... | collective-permute-start | bytes 393224 | tf_op jit(solution)/shard_map/ppermute | solution.py:186
  70.5 9.7 %collective-permute-start.25 = (bf16[128,512]{1,0:T(8,128)(2,1)S(1)}, bf16[128,512]{1,0:T(8,128)(2,1)S(1)}, u32[]{:S(2)}, u32[]{:S(2)}) collective-permute-start(bf16[128,512]{1,0:T(8,128)(2,1)S(1)} %get-tuple-element.23), channel_id=1, source_target_pairs={{0,6},{1,7},{2,4},{3,5},{4,2},{5,3},{6,0},{7,1},{8,14},{9,15},{10,... | collective-permute-start | bytes 393224 | tf_op jit(solution)/shard_map/ppermute | solution.py:186
  70.9 10.3 %collective-permute-start.26 = (bf16[128,512]{1,0:T(8,128)(2,1)S(1)}, bf16[128,512]{1,0:T(8,128)(2,1)S(1)}, u32[]{:S(2)}, u32[]{:S(2)}) collective-permute-start(bf16[128,512]{1,0:T(8,128)(2,1)S(1)} %get-tuple-element.24), channel_id=1, source_target_pairs={{0,7},{1,6},{2,5},{3,4},{4,3},{5,2},{6,1},{7,0},{8,15},{9,14},{10,... | collective-permute-start | bytes 393224 | tf_op jit(solution)/shard_map/ppermute | solution.py:186
  81.4 1.0 %copy-start.5 = (bf16[128,4096]{1,0:T(8,128)(2,1)}, bf16[128,4096]{1,0:T(8,128)(2,1)S(1)}, u32[]{:S(2)}) copy-start(bf16[128,4096]{1,0:T(8,128)(2,1)S(1)} %bitcast_dynamic-update-slice_fusion.1) | copy-start | bytes 3145732

commit v3 on v2

v3 whole, which is shorter than its diff:
```python
import functools
import math

import jax
import jax.numpy as jnp
from jax import lax
from jax.experimental import pallas as pl
from jax.experimental.pallas import tpu as pltpu
from jax.sharding import PartitionSpec as P


KEY_VALUE_HEADS = 8
HEAD_SIZE = 128
NEGATIVE = -1e30
HALVES = 2


def attend_kernel(
    pieces, half, back, slots, opening, closing, parts, place_ref, bounds_ref, firsts_ref, *refs
):
    width = KEY_VALUE_HEADS
    count = len(slots)
    steps = sorted({step for step, _ in pieces})
    q_refs, refs = refs[:count], refs[count:]
    units, refs = refs[: len(pieces)], refs[len(pieces) :]
    if not opening:
        acc_in, stat_in = refs[:2]
        refs = refs[2:]
    if closing:
        out_refs, refs = refs[:count], refs[count:]
    acc_ref, stat_ref, score_ref, peak_ref, q_ref, kv_ref, list_ref = refs
    rows, columns = q_refs[0].shape
    heads = columns // HEAD_SIZE
    lanes = heads * rows
    shard = parts * rows
    depth = place_ref[0]
    member = place_ref[1]
    group = place_ref[2]
    origin = group - back
    scale = math.log2(math.e) / math.sqrt(HEAD_SIZE)
    if half is None:
        bottom, chunk = 0, width
    else:
        chunk = width // HALVES
        bottom = jnp.bitwise_xor(lax.div(member, chunk), half) * chunk

    visits = jnp.int32(0)
    for turn, slot in enumerate(slots):
        doc = jnp.bitwise_xor(member, slot) + back * width
        lowest = lax.div(bounds_ref[slot], shard) - origin * width
        start = jnp.maximum(lowest, bottom)
        stop = jnp.maximum(jnp.minimum(doc, bottom + chunk - 1) + 1, start)

        def note(key_doc, spot, turn=turn):
            list_ref[0, spot] = turn
            list_ref[1, spot] = key_doc
            return spot + 1

        visits = lax.fori_loop(start, stop, note, visits)

    for (step, first), unit in zip(pieces, units):
        at = steps.index(step) * rows
        kv_ref[first : first + unit.shape[0], at : at + rows, :] = unit[...]
    for i in range(count):
        for h in range(heads):
            q_ref[i, h * rows : (h + 1) * rows, :] = q_refs[i][:, h * HEAD_SIZE : (h + 1) * HEAD_SIZE]
    if opening:
        acc_ref[...] = jnp.zeros_like(acc_ref)
        stat_ref[:, 0:1, :] = jnp.full((count, 1, lanes), NEGATIVE, jnp.float32)
        stat_ref[:, 1:2, :] = jnp.zeros((count, 1, lanes), jnp.float32)
    else:
        acc_ref[...] = acc_in[slots[0] : slots[0] + count]
        stat_ref[...] = stat_in[slots[0] : slots[0] + count]

    def multiply(i):
        turn, key_doc = list_ref[0, i], list_ref[1, i]
        keys = kv_ref[jnp.bitwise_xor(member, key_doc), :, 0:HEAD_SIZE]
        return lax.dot_general(
            keys, q_ref[turn], (((1,), (1,)), ((), ())), preferred_element_type=jnp.float32
        )

    def settle(i, scores):
        turn, key_doc = list_ref[0, i], list_ref[1, i]
        slot = slots[0] + turn
        doc = jnp.bitwise_xor(member, slot)
        base = (origin * width + key_doc) * shard
        root = ((group * width + doc) * parts + depth) * rows
        at = root + lax.broadcasted_iota(jnp.int32, (1, rows), 1)
        firsts = firsts_ref[pl.ds(slot, 1), :]
        seen = []
        for step in steps:
            behind = depth - step
            behind = jnp.where(behind < 0, behind + parts, behind)
            spot = lax.broadcasted_iota(jnp.int32, (rows, rows), 0)
            corner = base + behind * rows
            here = (spot >= firsts - corner) & (spot <= at - corner)
            seen.append(jnp.concatenate([here] * heads, axis=1))
        scores = jnp.where(jnp.concatenate(seen, axis=0), scores, NEGATIVE)
        score_ref[...] = scores
        peak_ref[0:1, :] = jnp.max(scores, axis=0, keepdims=True)

    @pl.when(visits > 0)
    def _():
        settle(0, multiply(0))

        def visit(i, _):
            turn, key_doc = list_ref[0, i], list_ref[1, i]
            follow = jnp.minimum(i + 1, visits - 1)
            coming = multiply(follow)
            before = stat_ref[turn, 0:1, :]
            peak = jnp.maximum(before, peak_ref[0:1, :])
            weights = jnp.exp2((score_ref[...] - peak) * scale)
            total = jnp.sum(weights, axis=0, keepdims=True)
            values = kv_ref[jnp.bitwise_xor(member, key_doc), :, HEAD_SIZE:]
            gain = lax.dot_general(
                values,
                weights.astype(jnp.bfloat16),
                (((0,), (0,)), ((), ())),
                preferred_element_type=jnp.float32,
            )
            settle(follow, coming)
            shrink = jnp.exp2((before - peak) * scale)
            stat_ref[turn, 0:1, :] = peak
            stat_ref[turn, 1:2, :] = stat_ref[turn, 1:2, :] * shrink + total
            acc_ref[turn] = acc_ref[turn] * shrink + gain
            return 0

        lax.fori_loop(0, visits, visit, 0)

    if closing:
        for i in range(count):
            done = (acc_ref[i] / stat_ref[i, 1:2, :]).astype(out_refs[i].dtype)
            for h in range(heads):
                out_refs[i][:, h * HEAD_SIZE : (h + 1) * HEAD_SIZE] = done[:, h * rows : (h + 1) * rows].T


def attend(place, tables, queries, pieces, half, slots, state, closing, parts, back=0):
    width = KEY_VALUE_HEADS
    bounds, firsts = tables
    rows, columns = queries[0].shape
    lanes = columns // HEAD_SIZE * rows
    vmem = pl.BlockSpec(memory_space=pltpu.VMEM)
    smem = pl.BlockSpec(memory_space=pltpu.SMEM)
    opening = state is None
    held = () if opening else [pltpu.with_memory_space_constraint(x, pltpu.VMEM) for x in state]
    count = len(slots)
    tokens = len({step for step, _, _ in pieces}) * rows
    kept = [
        pltpu.VMEM((count, HEAD_SIZE, lanes), jnp.float32),
        pltpu.VMEM((count, 8, lanes), jnp.float32),
    ]
    scratch = [
        pltpu.VMEM((tokens, lanes), jnp.float32),
        pltpu.VMEM((8, lanes), jnp.float32),
        pltpu.VMEM((count, lanes, HEAD_SIZE), queries[0].dtype),
        pltpu.VMEM((width, tokens, 2 * HEAD_SIZE), queries[0].dtype),
        pltpu.SMEM((2, width * width), jnp.int32),
    ]
    aliases = {}
    if closing:
        out_shape = [pltpu.VMEM((rows, columns), queries[0].dtype) for _ in slots]
        scratch = kept + scratch
    else:
        out_shape = kept
        first = 3 + count + len(pieces)
        aliases = {} if opening else {first: 0, first + 1: 1}
    work = count * 2 * tokens * lanes * HEAD_SIZE * 4
    return pl.pallas_call(
        functools.partial(
            attend_kernel,
            tuple((step, first) for step, first, _ in pieces),
            half,
            back,
            tuple(slots),
            opening,
            closing,
            parts,
        ),
        out_shape=out_shape,
        in_specs=[smem, smem] + [vmem] * (1 + count + len(pieces) + len(held)),
        out_specs=[vmem] * len(out_shape),
        input_output_aliases=aliases,
        cost_estimate=pl.CostEstimate(
            flops=work, bytes_accessed=4 * width * HEAD_SIZE * lanes, transcendentals=0
        ),
        scratch_shapes=scratch,
    )(
        place,
        bounds,
        firsts,
        *[queries[slot] for slot in slots],
        *[unit for _, _, unit in pieces],
        *held,
    )


def collect_kernel(place_ref, *refs):
    sem = refs[-1]
    out_ref = refs[-2]
    copies = []
    for k, ref in enumerate(refs[:-2]):
        columns = ref.shape[1]
        at = pl.multiple_of(jnp.bitwise_xor(place_ref[1], k) * columns, columns)
        copies.append(pltpu.make_async_copy(ref, out_ref.at[:, pl.ds(at, columns)], sem.at[k]))
    for copy in copies:
        copy.start()
    for copy in copies:
        copy.wait()


def collect(place, blocks):
    rows, columns = blocks[0].shape
    count = len(blocks)
    return pl.pallas_call(
        collect_kernel,
        out_shape=jax.ShapeDtypeStruct((rows, count * columns), blocks[0].dtype),
        in_specs=[pl.BlockSpec(memory_space=pltpu.SMEM)]
        + [pl.BlockSpec(memory_space=pltpu.VMEM)] * count,
        out_specs=pl.BlockSpec(memory_space=pltpu.HBM),
        scratch_shapes=[pltpu.SemaphoreType.DMA((count,))],
    )(place, *blocks)


def doc_starts(doc_lengths, positions):
    closing = jnp.cumsum(doc_lengths)
    passed = closing[None, :] <= positions[:, None]
    return jnp.sum(jnp.where(passed, doc_lengths[None, :], 0), axis=1)


def swap(block, k):
    if k == 0:
        return block
    length = lax.axis_size("doc")
    return lax.ppermute(block, "doc", [(i, i ^ k) for i in range(length)])


def on_device(packed_query_rows, packed_key_rows, packed_value_rows, doc_lengths):
    width = KEY_VALUE_HEADS
    chunk = width // HALVES
    docs, parts = lax.axis_size("doc"), lax.axis_size("head")
    index = lax.axis_index("doc")
    member, group = index % width, index // width
    depth = lax.axis_index("head")
    place = jnp.stack([depth, member, group]).astype(jnp.int32)
    rows = packed_query_rows.shape[0]
    blocks = (group * width + jnp.bitwise_xor(member, jnp.arange(width))) * parts + depth
    spots = blocks[:, None] * rows + jnp.arange(rows)[None, :]
    firsts = doc_starts(doc_lengths, spots.reshape(-1)).reshape(width, rows).astype(jnp.int32)
    tables = (firsts[:, 0], firsts)

    def cut(value, k):
        size = value.shape[1] // width
        return lax.dynamic_slice_in_dim(value, jnp.bitwise_xor(member, k) * size, size, 1)

    ring = [(i, (i + 1) % parts) for i in range(parts)]
    pairs = [
        swap(jnp.concatenate([cut(packed_key_rows, k), cut(packed_value_rows, k)], axis=1), k)
        for k in range(width)
    ]
    opens = [(0, chunk // 2), (chunk // 2, chunk), (chunk, width)]
    queries = [swap(cut(packed_query_rows, k), k) for k in range(width)]

    def move(piece):
        return lax.ppermute(piece, "head", ring)

    held = [(low, jnp.stack(pairs[low:high])) for low, high in opens]
    pieces = [(0, low, piece) for low, piece in held]
    held = [(low, move(piece)) for low, piece in held]
    pieces += [(1, low, piece) for low, piece in held]
    held = [(0, jnp.concatenate([held[0][1], held[1][1]], axis=0)), held[2]]
    for step in range(2, parts):
        held = [(low, move(piece)) for low, piece in held]
        pieces += [(step, low, piece) for low, piece in held]

    attends = functools.partial(attend, place, tables, queries)
    everyone = list(range(width))
    soon = parts // 2
    first = [piece for piece in pieces if piece[0] < soon]
    state = attends(first, None, everyone, None, False, parts)
    late = [piece for piece in pieces if piece[0] >= soon]
    if docs > width:
        over = [(i, i + width) for i in range(docs - width)]
        far = [(step, low, lax.ppermute(piece, "doc", over)) for step, low, piece in pieces]
        state = attends(far, None, everyone, state, False, parts, back=1)
    near = [piece for piece in late if piece[1] < chunk]
    state = attends(near, 0, everyone, state, False, parts)
    results = {}
    for turn in reversed(range(HALVES)):
        slots = list(range(turn * chunk, (turn + 1) * chunk))
        rest = [piece for piece in late if piece[1] >= chunk]
        outs = attends(rest, 1, slots, state, True, parts)
        for slot, out in zip(slots, outs):
            results[slot] = swap(out, slot)
    return collect(place, [results[k] for k in range(width)])


def solution(mesh):
    in_specs = (P(("doc", "head"), None), P(("doc", "head"), None), P(("doc", "head"), None), P())
    out_specs = P(("doc", "head"), None)

    return jax.shard_map(
        on_device, mesh=mesh, in_specs=in_specs, out_specs=out_specs, check_vma=False
    )
```

time: 83.4 us -> 82.2 us (0.986)
  Pallas kernels: 16.8 us -> 22.6 us
  waiting for transfers between devices: 27.4 us -> 24.5 us
  starting transfers between devices: 29.4 us -> 27.2 us
  local copies, waits for them, and re-layouts: 7.76 us -> 5.91 us
    pallas_call x3 -> x5, Pallas kernels: 16.8 us -> 22.6 us  [the longest x4 20.3 us: attend(): pl.pallas_call(functools.partial(attend_kernel, tuple(((step, first) for...]
    ppermute x21, waiting for transfers between devices: 14.6 us -> 11.1 us  [swap(): return lax.ppermute(block, 'doc', [(i, i ^ k) for i in range(length)])]
    ppermute x21, starting transfers between devices: 25.1 us -> 22.2 us  [swap(): return lax.ppermute(block, 'doc', [(i, i ^ k) for i in range(length)])]
    unnamed x54 -> x46, local copies, waits for them, and re-layouts: 4.5 us -> 3.32 us
    ppermute x6 -> x7, starting transfers between devices: 4.29 us -> 5.01 us  [move(): return lax.ppermute(piece, 'head', ring)]
    ppermute x6 -> x7, waiting for transfers between devices: 12.8 us -> 13.5 us  [move(): return lax.ppermute(piece, 'head', ring)]
  transfers between devices with their start and end apart: 27 -> 28, of which waited for: 11 -> 9; matrix products, arithmetic and copies ran while one was open for 3% -> 3% of each run, Pallas kernels for 13% -> 20%
where the time goes in v3:
time: 82.2 us; the launch traced here: 81.9 us
  starting transfers between devices  27.2 us (33%)
  waiting for transfers between devices  24.5 us (30%)
  Pallas kernels  22.6 us (27%)
  local copies, waits for them, and re-layouts  5.91 us (7%)
  other arithmetic  1.13 us (1%)
    ppermute x21, starting transfers between devices, swap(): return lax.ppermute(block, 'doc', [(i, i ^ k) for i in range(length)])  22.2 us
    pallas_call x4, Pallas kernels, attend(): pl.pallas_call(functools.partial(attend_kernel, tuple(((step, first) for...  20.3 us
    ppermute x7, waiting for transfers between devices, move(): return lax.ppermute(piece, 'head', ring)  13.5 us
    ppermute x21, waiting for transfers between devices, swap(): return lax.ppermute(block, 'doc', [(i, i ^ k) for i in range(length)])  11.1 us
    ppermute x7, starting transfers between devices, move(): return lax.ppermute(piece, 'head', ring)  5.01 us
    unnamed x46, local copies, waits for them, and re-layouts  3.32 us
    pallas_call x1, Pallas kernels, collect(): pl.pallas_call(collect_kernel, out_shape=jax.ShapeDtypeStruct((rows, coun...  2.32 us
    dynamic_slice x2, local copies, waits for them, and re-layouts, cut(): lax.dynamic_slice_in_dim(value, jnp.bitwise_xor(member, k) * size, size, 1)  1.88 us
  transfers between devices with their start and end apart: 28, of which 9 were waited for; matrix products, arithmetic and copies ran while one was open for 3% of the time, Pallas kernels for 20%

profile of v3, /device:TPU:0, one launch (start us, length us, event | category | flops | bytes accessed | tf_op | source)
XLA Modules:
  0.0 81.9 jit_solution(9218094219854356806)
XLA Ops:
  0.0 1.1 %constant_dynamic-slice_fusion.6 = (bf16[128,128]{1,0:T(8,128)(2,1)S(1)}, bf16[128,128]{1,0:T(8,128)(2,1)S(1)}, bf16[128,128]{1,0:T(8,128)(2,1)S(1)}, bf16[128,1...) fusion(bf16[128,1024]{1,0:T(8,128)(2,1)} %param.6, ...), kind=kLoop, calls=%fused_computation.19 | loop fusion | bytes 1048608 | tf_op jit(solution)/shard_map/dynamic_slice | solution.py:253
  1.2 3.0 %collective-permute-start.16 = (bf16[128,256]{1,0:T(8,128)(2,1)S(1)}, bf16[128,256]{1,0:T(8,128)(2,1)S(1)}, u32[]{:S(2)}, u32[]{:S(2)}) collective-permute-start(bf16[128,256]{1,0:T(8,128)(2,1)S(1)} %pad_maximum_fusion.9), channel_id=1, source_target_pairs={{0,2},{1,3},{2,0},{3,1},{4,6},{5,7},{6,4},{7,5},{8,10},{9,11},{10,... | collective-permute-start | bytes 196616 | tf_op jit(solution)/shard_map/ppermute | solution.py:234
  4.2 0.1 collective-permute-start.17
  4.3 0.2 collective-permute-start.14
  4.5 2.1 %collective-permute-start.3 = (bf16[128,256]{1,0:T(8,128)(2,1)S(1)}, bf16[128,256]{1,0:T(8,128)(2,1)S(1)}, u32[]{:S(2)}, u32[]{:S(2)}) collective-permute-start(bf16[128,256]{1,0:T(8,128)(2,1)S(1)} %pad_maximum_fusion.4), channel_id=1, source_target_pairs={{0,4},{1,5},{2,6},{3,7},{4,0},{5,1},{6,2},{7,3},{8,12},{9,13},{10,... | collective-permute-start | bytes 196616 | tf_op jit(solution)/shard_map/ppermute | solution.py:234
  6.6 0.1 collective-permute-start.4
  6.7 0.0 copy-start.22
  6.8 3.2 %collective-permute-start.5 = (bf16[128,256]{1,0:T(8,128)(2,1)S(1)}, bf16[128,256]{1,0:T(8,128)(2,1)S(1)}, u32[]{:S(2)}, u32[]{:S(2)}) collective-permute-start(bf16[128,256]{1,0:T(8,128)(2,1)S(1)} %pad_maximum_fusion.6), channel_id=1, source_target_pairs={{0,6},{1,7},{2,4},{3,5},{4,2},{5,3},{6,0},{7,1},{8,14},{9,15},{10,... | collective-permute-start | bytes 196616 | tf_op jit(solution)/shard_map/ppermute | solution.py:234
  10.1 0.2 collective-permute-start.6
  10.3 0.0 collective-permute-done.14
  10.3 1.6 %collective-permute-start.18 = (bf16[2,128,256]{2,1,0:T(8,128)(2,1)S(1)}, bf16[2,128,256]{2,1,0:T(8,128)(2,1)S(1)}, u32[]{:S(2)}, u32[]{:S(2)}) collective-permute-start(bf16[2,128,256]{2,1,0:T(8,128)(2,1)S(1)} %pad_maximum_fusion.3.refs_9_), channel_id=1, source_target_pairs={{0,8},{8,16},{16,24},{24,0},{1,9},{9,17},{17,25},{25,1},{2,10},{10... | collective-permute-start | bytes 393224 | tf_op jit(solution)/shard_map/ppermute | solution.py:264
  11.9 1.6 %collective-permute-start.15 = (bf16[2,128,256]{2,1,0:T(8,128)(2,1)S(1)}, bf16[2,128,256]{2,1,0:T(8,128)(2,1)S(1)}, u32[]{:S(2)}, u32[]{:S(2)}) collective-permute-start(bf16[2,128,256]{2,1,0:T(8,128)(2,1)S(1)} %pad_maximum_fusion.2.refs_8_), channel_id=1, source_target_pairs={{0,8},{8,16},{16,24},{24,0},{1,9},{9,17},{17,25},{25,1},{2,10},{10... | collective-permute-start | bytes 393224 | tf_op jit(solution)/shard_map/ppermute | solution.py:264
  13.6 0.0 collective-permute-done.5
  13.6 1.5 %collective-permute-done.6 = bf16[128,256]{1,0:T(8,128)(2,1)S(1)} collective-permute-done((bf16[128,256]{1,0:T(8,128)(2,1)S(1)}, bf16[128,256]{1,0:T(8,128)(2,1)S(1)}, u32[]{:S(2)}, u32[]{:S(2)}) %collective-permute-start.6) | collective-permute-done | bytes 65568 | tf_op jit(solution)/shard_map/ppermute | solution.py:234
  15.2 1.6 %collective-permute-start.7 = (bf16[4,128,256]{2,1,0:T(8,128)(2,1)S(1)}, bf16[4,128,256]{2,1,0:T(8,128)(2,1)}, u32[]{:S(2)}, u32[]{:S(2)}) collective-permute-start(bf16[4,128,256]{2,1,0:T(8,128)(2,1)S(1)} %pad_maximum_fusion.refs_10_), channel_id=1, source_target_pairs={{0,8},{8,16},{16,24},{24,0},{1,9},{9,17},{17,25},{25,1},{2,10},{10... | collective-permute-start | bytes 786440 | tf_op jit(solution)/shard_map/ppermute | solution.py:264
  16.8 0.7 constant_dynamic-slice_fusion.8
  17.5 0.0 collective-permute-start
  17.5 0.1 collective-permute-start.1
  17.7 0.8 %collective-permute-done.18.refs_12_ = bf16[2,128,256]{2,1,0:T(8,128)(2,1)S(1)} collective-permute-done((bf16[2,128,256]{2,1,0:T(8,128)(2,1)S(1)}, bf16[2,128,256]{2,1,0:T(8,128)(2,1)S(1)}, u32[]{:S(2)}, u32[]{:S(2)}) %collective-permute-start.18) | collective-permute-done | bytes 131104 | tf_op jit(solution)/shard_map/ppermute | solution.py:264
  18.5 1.0 %collective-permute-start.10 = (bf16[128,512]{1,0:T(8,128)(2,1)S(1)}, bf16[128,512]{1,0:T(8,128)(2,1)S(1)}, u32[]{:S(2)}, u32[]{:S(2)}) collective-permute-start(bf16[128,512]{1,0:T(8,128)(2,1)S(1)} %get-tuple-element.31), channel_id=1, source_target_pairs={{0,4},{1,5},{2,6},{3,7},{4,0},{5,1},{6,2},{7,3},{8,12},{9,13},{10,... | collective-permute-start | bytes 393224 | tf_op jit(solution)/shard_map/ppermute | solution.py:234
  19.5 1.8 %collective-permute-done.15.refs_11_ = bf16[2,128,256]{2,1,0:T(8,128)(2,1)S(1)} collective-permute-done((bf16[2,128,256]{2,1,0:T(8,128)(2,1)S(1)}, bf16[2,128,256]{2,1,0:T(8,128)(2,1)S(1)}, u32[]{:S(2)}, u32[]{:S(2)}) %collective-permute-start.15) | collective-permute-done | bytes 131104 | tf_op jit(solution)/shard_map/ppermute | solution.py:264
  21.3 0.1 collective-permute-start.11
  21.4 0.0 collective-permute-done.refs_1_
  21.4 0.1 collective-permute-start.19
  21.5 4.6 %collective-permute-done.7.refs_13_ = bf16[4,128,256]{2,1,0:T(8,128)(2,1)} collective-permute-done((bf16[4,128,256]{2,1,0:T(8,128)(2,1)S(1)}, bf16[4,128,256]{2,1,0:T(8,128)(2,1)}, u32[]{:S(2)}, u32[]{:S(2)}) %collective-permute-start.7) | collective-permute-done | bytes 262176 | tf_op jit(solution)/shard_map/ppermute | solution.py:264
  26.2 0.0 collective-permute-start.8
  26.2 0.1 add_bitcast_fusion
  26.2 0.1 copy.9
  26.4 0.1 reduce
  26.5 0.1 select_reduce_fusion
  26.6 0.0 collective-permute-done.1.refs_2_
  26.6 2.8 %collective-permute-start.12 = (bf16[128,512]{1,0:T(8,128)(2,1)S(1)}, bf16[128,512]{1,0:T(8,128)(2,1)S(1)}, u32[]{:S(2)}, u32[]{:S(2)}) collective-permute-start(bf16[128,512]{1,0:T(8,128)(2,1)S(1)} %get-tuple-element.36), channel_id=1, source_target_pairs={{0,6},{1,7},{2,4},{3,5},{4,2},{5,3},{6,0},{7,1},{8,14},{9,15},{10,... | collective-permute-start | bytes 393224 | tf_op jit(solution)/shard_map/ppermute | solution.py:234
  29.4 0.0 collective-permute-done.10.refs_4_.refs_0_
  29.4 0.0 collective-permute-start.13
  29.4 1.7 %collective-permute-start.2 = (bf16[128,512]{1,0:T(8,128)(2,1)S(1)}, bf16[128,512]{1,0:T(8,128)(2,1)S(1)}, u32[]{:S(2)}, u32[]{:S(2)}) collective-permute-start(bf16[128,512]{1,0:T(8,128)(2,1)S(1)} %get-tuple-element.32), channel_id=1, source_target_pairs={{0,3},{1,2},{2,1},{3,0},{4,7},{5,6},{6,5},{7,4},{8,11},{9,10},{10,... | collective-permute-start | bytes 393224 | tf_op jit(solution)/shard_map/ppermute | solution.py:234
  31.1 1.4 %collective-permute-done.19.refs_8_ = bf16[4,128,256]{2,1,0:T(8,128)(2,1)} collective-permute-done((bf16[4,128,256]{2,1,0:T(8,128)(2,1)S(1)}, bf16[4,128,256]{2,1,0:T(8,128)(2,1)}, u32[]{:S(2)}, u32[]{:S(2)}) %collective-permute-start.19) | collective-permute-done | bytes 262176 | tf_op jit(solution)/shard_map/ppermute | solution.py:264
  32.5 0.1 collective-permute-start.20
  32.5 0.6 slice_reduce_fusion.bounds_ref
  33.1 4.8 %collective-permute-done.8.refs_4_ = bf16[4,128,256]{2,1,0:T(8,128)(2,1)S(1)} collective-permute-done((bf16[4,128,256]{2,1,0:T(8,128)(2,1)}, bf16[4,128,256]{2,1,0:T(8,128)(2,1)S(1)}, u32[]{:S(2)}, u32[]{:S(2)}) %collective-permute-start.8) | collective-permute-done | bytes 262176 | tf_op jit(solution)/shard_map/ppermute | solution.py:264
  38.0 0.6 pad_add_fusion.place_ref
  38.6 0.0 collective-permute-done.12.refs_6_.refs_2_
  38.6 0.0 collective-permute-done.13.refs_7_.refs_3_
  38.7 0.6 copy-done.10
  39.3 0.1 copy-done.11
  39.4 0.6 copy-done.9
  40.0 8.3 %shard_map.46 = (f32[8,128,512]{2,1,0:T(8,128)S(1)}, f32[8,8,512]{2,1,0:T(8,128)S(1)}) custom-call(s32[3]{0:T(128)} %pad_add_fusion.place_ref, s32[8]{0:T(128)} %slice_reduce_fusion.bounds_ref, s32[8,128]{1,0:T(8,128)} %bitcast.17, bf16[128,512]{1,0:T(8,128)(2,1)} %get-tuple-element.35.refs_0_, bf16[128,512]{1,0:T(8,128)(2,1)} %copy-done.5, ...), custom_call_target="tpu_custom_call" | custom-call | flops 1073741824 | bytes 2097152 | tf_op jit(solution)/shard_map/pallas_call | solution.py:168
  48.3 6.1 %shard_map.47 = (f32[8,128,512]{2,1,0:T(8,128)S(1)}, f32[8,8,512]{2,1,0:T(8,128)S(1)}) custom-call(s32[3]{0:T(128)} %pad_add_fusion.place_ref, s32[8]{0:T(128)} %slice_reduce_fusion.bounds_ref, s32[8,128]{1,0:T(8,128)} %bitcast.18, bf16[128,512]{1,0:T(8,128)(2,1)} %get-tuple-element.35.refs_0_, ...), custom_call_target="tpu_custom_call", output_to_operand_aliasing={{0}: (13, {}), {1}: (14, {})} | custom-call | flops 1073741824 | bytes 2097152 | tf_op jit(solution)/shard_map/pallas_call | solution.py:168
  54.4 0.0 collective-permute-done.9.refs_5_
  54.4 0.7 copy-done.2
  55.1 4.2 %shard_map.49 = (bf16[128,512]{1,0:T(8,128)(2,1)S(1)}, bf16[128,512]{1,0:T(8,128)(2,1)S(1)}, bf16[128,512]{1,0:T(8,128)(2,1)S(1)}, bf16[128,512]{1,0:T(8,128)(2,1)S(1)}) custom-call(s32[3]{0:T(128)} %pad_add_fusion.place_ref, s32[8]{0:T(128)} %slice_reduce_fusion.bounds_ref, s32[8,128]{1,0:T(8,128)} %bitcast.19, bf16[128,512]{1,0:T(8,128)(2,1)} %copy-done.7, ...), custom_call_target="tpu_custom_call" | custom-call | flops 536870912 | bytes 2097152 | tf_op jit(solution)/shard_map/pallas_call | solution.py:168
  59.4 0.1 collective-permute-start.24
  59.5 1.8 %collective-permute-start.25 = (bf16[128,512]{1,0:T(8,128)(2,1)S(1)}, bf16[128,512]{1,0:T(8,128)(2,1)S(1)}, u32[]{:S(2)}, u32[]{:S(2)}) collective-permute-start(bf16[128,512]{1,0:T(8,128)(2,1)S(1)} %get-tuple-element.26), channel_id=1, source_target_pairs={{0,5},{1,4},{2,7},{3,6},{4,1},{5,0},{6,3},{7,2},{8,13},{9,12},{10,... | collective-permute-start | bytes 393224 | tf_op jit(solution)/shard_map/ppermute | solution.py:234
  61.2 2.2 %collective-permute-start.26 = (bf16[128,512]{1,0:T(8,128)(2,1)S(1)}, bf16[128,512]{1,0:T(8,128)(2,1)}, u32[]{:S(2)}, u32[]{:S(2)}) collective-permute-start(bf16[128,512]{1,0:T(8,128)(2,1)S(1)} %get-tuple-element.27), channel_id=1, source_target_pairs={{0,6},{1,7},{2,4},{3,5},{4,2},{5,3},{6,0},{7,1},{8,14},{9,15},{10,... | collective-permute-start | bytes 393224 | tf_op jit(solution)/shard_map/ppermute | solution.py:234
  63.4 0.4 collective-permute-start.27
  63.8 1.7 %shard_map.48 = (bf16[128,512]{1,0:T(8,128)(2,1)S(1)}, bf16[128,512]{1,0:T(8,128)(2,1)S(1)}, bf16[128,512]{1,0:T(8,128)(2,1)S(1)}, bf16[128,512]{1,0:T(8,128)(2,1)S(1)}) custom-call(s32[3]{0:T(128)} %pad_add_fusion.place_ref, s32[8]{0:T(128)} %slice_reduce_fusion.bounds_ref, s32[8,128]{1,0:T(8,128)} %bitcast.20, bf16[128,512]{1,0:T(8,128)(2,1)} %get-tuple-element.35.refs_0_, ...), custom_call_target="tpu_custom_call" | custom-call | flops 536870912 | bytes 2097152 | tf_op jit(solution)/shard_map/pallas_call | solution.py:168
  65.6 0.6 copy-done
  66.2 0.4 collective-permute-start.21
  66.6 4.8 %collective-permute-done.24.refs_4_ = bf16[128,512]{1,0:T(8,128)(2,1)S(1)} collective-permute-done((bf16[128,512]{1,0:T(8,128)(2,1)S(1)}, bf16[128,512]{1,0:T(8,128)(2,1)S(1)}, u32[]{:S(2)}, u32[]{:S(2)}) %collective-permute-start.24) | collective-permute-done | bytes 131104 | tf_op jit(solution)/shard_map/ppermute | solution.py:234
  71.4 2.0 %collective-permute-start.22 = (bf16[128,512]{1,0:T(8,128)(2,1)S(1)}, bf16[128,512]{1,0:T(8,128)(2,1)S(1)}, u32[]{:S(2)}, u32[]{:S(2)}) collective-permute-start(bf16[128,512]{1,0:T(8,128)(2,1)S(1)} %get-tuple-element.23), channel_id=1, source_target_pairs={{0,2},{1,3},{2,0},{3,1},{4,6},{5,7},{6,4},{7,5},{8,10},{9,11},{10,... | collective-permute-start | bytes 393224 | tf_op jit(solution)/shard_map/ppermute | solution.py:234
  73.4 0.8 %collective-permute-start.23 = (bf16[128,512]{1,0:T(8,128)(2,1)S(1)}, bf16[128,512]{1,0:T(8,128)(2,1)S(1)}, u32[]{:S(2)}, u32[]{:S(2)}) collective-permute-start(bf16[128,512]{1,0:T(8,128)(2,1)S(1)} %get-tuple-element.24), channel_id=1, source_target_pairs={{0,3},{1,2},{2,1},{3,0},{4,7},{5,6},{6,5},{7,4},{8,11},{9,10},{10,... | collective-permute-start | bytes 393224 | tf_op jit(solution)/shard_map/ppermute | solution.py:234
  74.3 2.5 %collective-permute-done.22.refs_2_ = bf16[128,512]{1,0:T(8,128)(2,1)S(1)} collective-permute-done((bf16[128,512]{1,0:T(8,128)(2,1)S(1)}, bf16[128,512]{1,0:T(8,128)(2,1)S(1)}, u32[]{:S(2)}, u32[]{:S(2)}) %collective-permute-start.22) | collective-permute-done | bytes 131104 | tf_op jit(solution)/shard_map/ppermute | solution.py:234
  76.8 2.1 %collective-permute-done.23.refs_3_ = bf16[128,512]{1,0:T(8,128)(2,1)S(1)} collective-permute-done((bf16[128,512]{1,0:T(8,128)(2,1)S(1)}, bf16[128,512]{1,0:T(8,128)(2,1)S(1)}, u32[]{:S(2)}, u32[]{:S(2)}) %collective-permute-start.23) | collective-permute-done | bytes 131104 | tf_op jit(solution)/shard_map/ppermute | solution.py:234
  79.0 0.6 copy-done.16
  79.6 2.3 %shard_map.50 = bf16[128,4096]{1,0:T(8,128)(2,1)} custom-call(s32[3]{0:T(128)} %pad_add_fusion.place_ref, bf16[128,512]{1,0:T(8,128)(2,1)} %copy-done, bf16[128,512]{1,0:T(8,128)(2,1)} %copy-done.14, bf16[128,512]{1,0:T(8,128)(2,1)} %copy-done.15, bf16[128,512]{1,0:T(8,128)(2,1)} %copy-done.16, bf16[128,512]{1,0:T(8,128)(2,1)} %copy-done.12, ...), custom_call_target="tpu_custom_call" | custom-call | tf_op jit(solution)/shard_map/pallas_call | solution.py:214
  (65 shorter events, 0.3 us)
Async XLA Ops:
  0.0 16.8 %copy-start.3 = (bf16[128,4096]{1,0:T(8,128)(2,1)S(1)}, bf16[128,4096]{1,0:T(8,128)(2,1)}, u32[]{:S(2)}) copy-start(bf16[128,4096]{1,0:T(8,128)(2,1)} %param.4) | copy-start | bytes 3145732
  1.2 5.7 %collective-permute-start.16 = (bf16[128,256]{1,0:T(8,128)(2,1)S(1)}, bf16[128,256]{1,0:T(8,128)(2,1)S(1)}, u32[]{:S(2)}, u32[]{:S(2)}) collective-permute-start(bf16[128,256]{1,0:T(8,128)(2,1)S(1)} %pad_maximum_fusion.9), channel_id=1, source_target_pairs={{0,2},{1,3},{2,0},{3,1},{4,6},{5,7},{6,4},{7,5},{8,10},{9,11},{10,... | collective-permute-start | bytes 196616 | tf_op jit(solution)/shard_map/ppermute | solution.py:234
  4.2 5.9 %collective-permute-start.17 = (bf16[128,256]{1,0:T(8,128)(2,1)S(1)}, bf16[128,256]{1,0:T(8,128)(2,1)S(1)}, u32[]{:S(2)}, u32[]{:S(2)}) collective-permute-start(bf16[128,256]{1,0:T(8,128)(2,1)S(1)} %pad_maximum_fusion.10), channel_id=1, source_target_pairs={{0,3},{1,2},{2,1},{3,0},{4,7},{5,6},{6,5},{7,4},{8,11},{9,10},{10,... | collective-permute-start | bytes 196616 | tf_op jit(solution)/shard_map/ppermute | solution.py:234
  4.3 6.0 %collective-permute-start.14 = (bf16[128,256]{1,0:T(8,128)(2,1)S(1)}, bf16[128,256]{1,0:T(8,128)(2,1)S(1)}, u32[]{:S(2)}, u32[]{:S(2)}) collective-permute-start(bf16[128,256]{1,0:T(8,128)(2,1)S(1)} %pad_maximum_fusion.8), channel_id=1, source_target_pairs={{0,1},{1,0},{2,3},{3,2},{4,5},{5,4},{6,7},{7,6},{8,9},{9,8},{10,11... | collective-permute-start | bytes 196616 | tf_op jit(solution)/shard_map/ppermute | solution.py:234
  4.5 7.4 %collective-permute-start.3 = (bf16[128,256]{1,0:T(8,128)(2,1)S(1)}, bf16[128,256]{1,0:T(8,128)(2,1)S(1)}, u32[]{:S(2)}, u32[]{:S(2)}) collective-permute-start(bf16[128,256]{1,0:T(8,128)(2,1)S(1)} %pad_maximum_fusion.4), channel_id=1, source_target_pairs={{0,4},{1,5},{2,6},{3,7},{4,0},{5,1},{6,2},{7,3},{8,12},{9,13},{10,... | collective-permute-start | bytes 196616 | tf_op jit(solution)/shard_map/ppermute | solution.py:234
  6.6 7.0 %collective-permute-start.4 = (bf16[128,256]{1,0:T(8,128)(2,1)S(1)}, bf16[128,256]{1,0:T(8,128)(2,1)S(1)}, u32[]{:S(2)}, u32[]{:S(2)}) collective-permute-start(bf16[128,256]{1,0:T(8,128)(2,1)S(1)} %pad_maximum_fusion.5), channel_id=1, source_target_pairs={{0,5},{1,4},{2,7},{3,6},{4,1},{5,0},{6,3},{7,2},{8,13},{9,12},{10,... | collective-permute-start | bytes 196616 | tf_op jit(solution)/shard_map/ppermute | solution.py:234
  6.7 19.5 %copy-start.22 = (s32[16]{0:T(128)S(1)}, s32[16]{0:T(128)}, u32[]{:S(2)}) copy-start(s32[16]{0:T(128)} %param.7) | copy-start | bytes 196
  6.8 6.7 %collective-permute-start.5 = (bf16[128,256]{1,0:T(8,128)(2,1)S(1)}, bf16[128,256]{1,0:T(8,128)(2,1)S(1)}, u32[]{:S(2)}, u32[]{:S(2)}) collective-permute-start(bf16[128,256]{1,0:T(8,128)(2,1)S(1)} %pad_maximum_fusion.6), channel_id=1, source_target_pairs={{0,6},{1,7},{2,4},{3,5},{4,2},{5,3},{6,0},{7,1},{8,14},{9,15},{10,... | collective-permute-start | bytes 196616 | tf_op jit(solution)/shard_map/ppermute | solution.py:234
  10.1 5.0 %collective-permute-start.6 = (bf16[128,256]{1,0:T(8,128)(2,1)S(1)}, bf16[128,256]{1,0:T(8,128)(2,1)S(1)}, u32[]{:S(2)}, u32[]{:S(2)}) collective-permute-start(bf16[128,256]{1,0:T(8,128)(2,1)S(1)} %pad_maximum_fusion.7), channel_id=1, source_target_pairs={{0,7},{1,6},{2,5},{3,4},{4,3},{5,2},{6,1},{7,0},{8,15},{9,14},{10,... | collective-permute-start | bytes 196616 | tf_op jit(solution)/shard_map/ppermute | solution.py:234
  10.3 11.1 %copy-start.17 = (bf16[2,128,256]{2,1,0:T(8,128)(2,1)}, bf16[2,128,256]{2,1,0:T(8,128)(2,1)S(1)}, u32[]{:S(2)}) copy-start(bf16[2,128,256]{2,1,0:T(8,128)(2,1)S(1)} %pad_maximum_fusion.3.refs_9_) | copy-start | bytes 393220
  10.3 8.2 %collective-permute-start.18 = (bf16[2,128,256]{2,1,0:T(8,128)(2,1)S(1)}, bf16[2,128,256]{2,1,0:T(8,128)(2,1)S(1)}, u32[]{:S(2)}, u32[]{:S(2)}) collective-permute-start(bf16[2,128,256]{2,1,0:T(8,128)(2,1)S(1)} %pad_maximum_fusion.3.refs_9_), channel_id=1, source_target_pairs={{0,8},{8,16},{16,24},{24,0},{1,9},{9,17},{17,25},{25,1},{2,10},{10... | collective-permute-start | bytes 393224 | tf_op jit(solution)/shard_map/ppermute | solution.py:264
  11.9 9.4 %copy-start.18 = (bf16[2,128,256]{2,1,0:T(8,128)(2,1)}, bf16[2,128,256]{2,1,0:T(8,128)(2,1)S(1)}, u32[]{:S(2)}) copy-start(bf16[2,128,256]{2,1,0:T(8,128)(2,1)S(1)} %pad_maximum_fusion.2.refs_8_) | copy-start | bytes 393220
  11.9 9.4 %collective-permute-start.15 = (bf16[2,128,256]{2,1,0:T(8,128)(2,1)S(1)}, bf16[2,128,256]{2,1,0:T(8,128)(2,1)S(1)}, u32[]{:S(2)}, u32[]{:S(2)}) collective-permute-start(bf16[2,128,256]{2,1,0:T(8,128)(2,1)S(1)} %pad_maximum_fusion.2.refs_8_), channel_id=1, source_target_pairs={{0,8},{8,16},{16,24},{24,0},{1,9},{9,17},{17,25},{25,1},{2,10},{10... | collective-permute-start | bytes 393224 | tf_op jit(solution)/shard_map/ppermute | solution.py:264
  15.1 24.9 %copy-start.4 = (bf16[4,128,256]{2,1,0:T(8,128)(2,1)}, bf16[4,128,256]{2,1,0:T(8,128)(2,1)S(1)}, u32[]{:S(2)}) copy-start(bf16[4,128,256]{2,1,0:T(8,128)(2,1)S(1)} %pad_maximum_fusion.refs_10_) | copy-start | bytes 786436
  15.2 11.0 %collective-permute-start.7 = (bf16[4,128,256]{2,1,0:T(8,128)(2,1)S(1)}, bf16[4,128,256]{2,1,0:T(8,128)(2,1)}, u32[]{:S(2)}, u32[]{:S(2)}) collective-permute-start(bf16[4,128,256]{2,1,0:T(8,128)(2,1)S(1)} %pad_maximum_fusion.refs_10_), channel_id=1, source_target_pairs={{0,8},{8,16},{16,24},{24,0},{1,9},{9,17},{17,25},{25,1},{2,10},{10... | collective-permute-start | bytes 786440 | tf_op jit(solution)/shard_map/ppermute | solution.py:264
  17.5 3.9 %collective-permute-start = (bf16[128,512]{1,0:T(8,128)(2,1)S(1)}, bf16[128,512]{1,0:T(8,128)(2,1)S(1)}, u32[]{:S(2)}, u32[]{:S(2)}) collective-permute-start(bf16[128,512]{1,0:T(8,128)(2,1)S(1)} %get-tuple-element.34), channel_id=1, source_target_pairs={{0,1},{1,0},{2,3},{3,2},{4,5},{5,4},{6,7},{7,6},{8,9},{9,8},{10,11... | collective-permute-start | bytes 393224 | tf_op jit(solution)/shard_map/ppermute | solution.py:234
  17.5 9.0 %collective-permute-start.1 = (bf16[128,512]{1,0:T(8,128)(2,1)S(1)}, bf16[128,512]{1,0:T(8,128)(2,1)S(1)}, u32[]{:S(2)}, u32[]{:S(2)}) collective-permute-start(bf16[128,512]{1,0:T(8,128)(2,1)S(1)} %get-tuple-element.33), channel_id=1, source_target_pairs={{0,2},{1,3},{2,0},{3,1},{4,6},{5,7},{6,4},{7,5},{8,10},{9,11},{10,... | collective-permute-start | bytes 393224 | tf_op jit(solution)/shard_map/ppermute | solution.py:234
  18.5 20.2 %copy-start.19 = (bf16[2,128,256]{2,1,0:T(8,128)(2,1)}, bf16[2,128,256]{2,1,0:T(8,128)(2,1)S(1)}, u32[]{:S(2)}) copy-start(bf16[2,128,256]{2,1,0:T(8,128)(2,1)S(1)} %collective-permute-done.18.refs_12_) | copy-start | bytes 393220
  18.5 10.9 %collective-permute-start.10 = (bf16[128,512]{1,0:T(8,128)(2,1)S(1)}, bf16[128,512]{1,0:T(8,128)(2,1)S(1)}, u32[]{:S(2)}, u32[]{:S(2)}) collective-permute-start(bf16[128,512]{1,0:T(8,128)(2,1)S(1)} %get-tuple-element.31), channel_id=1, source_target_pairs={{0,4},{1,5},{2,6},{3,7},{4,0},{5,1},{6,2},{7,3},{8,12},{9,13},{10,... | collective-permute-start | bytes 393224 | tf_op jit(solution)/shard_map/ppermute | solution.py:234
  21.3 17.4 %copy-start.20 = (bf16[2,128,256]{2,1,0:T(8,128)(2,1)}, bf16[2,128,256]{2,1,0:T(8,128)(2,1)S(1)}, u32[]{:S(2)}) copy-start(bf16[2,128,256]{2,1,0:T(8,128)(2,1)S(1)} %collective-permute-done.15.refs_11_) | copy-start | bytes 393220
  21.3 8.1 %collective-permute-start.11 = (bf16[128,512]{1,0:T(8,128)(2,1)S(1)}, bf16[128,512]{1,0:T(8,128)(2,1)S(1)}, u32[]{:S(2)}, u32[]{:S(2)}) collective-permute-start(bf16[128,512]{1,0:T(8,128)(2,1)S(1)} %get-tuple-element.30), channel_id=1, source_target_pairs={{0,5},{1,4},{2,7},{3,6},{4,1},{5,0},{6,3},{7,2},{8,13},{9,12},{10,... | collective-permute-start | bytes 393224 | tf_op jit(solution)/shard_map/ppermute | solution.py:234
  21.4 18.6 %copy-start.5 = (bf16[128,512]{1,0:T(8,128)(2,1)}, bf16[128,512]{1,0:T(8,128)(2,1)S(1)}, u32[]{:S(2)}) copy-start(bf16[128,512]{1,0:T(8,128)(2,1)S(1)} %collective-permute-done.refs_1_) | copy-start | bytes 393220
  21.4 11.0 %collective-permute-start.19 = (bf16[4,128,256]{2,1,0:T(8,128)(2,1)S(1)}, bf16[4,128,256]{2,1,0:T(8,128)(2,1)}, u32[]{:S(2)}, u32[]{:S(2)}) collective-permute-start(bf16[4,128,256]{2,1,0:T(8,128)(2,1)S(1)} %pad_maximum_fusion.1), channel_id=1, source_target_pairs={{0,8},{8,16},{16,24},{24,0},{1,9},{9,17},{17,25},{25,1},{2,10},{10... | collective-permute-start | bytes 786440 | tf_op jit(solution)/shard_map/ppermute | solution.py:264
  26.2 11.8 %collective-permute-start.8 = (bf16[4,128,256]{2,1,0:T(8,128)(2,1)}, bf16[4,128,256]{2,1,0:T(8,128)(2,1)S(1)}, u32[]{:S(2)}, u32[]{:S(2)}) collective-permute-start(bf16[4,128,256]{2,1,0:T(8,128)(2,1)} %collective-permute-done.7.refs_13_), channel_id=1, source_target_pairs={{0,8},{8,16},{16,24},{24,0},{1,9},{9,17},{17,25},{25,1},{2,10},{10... | collective-permute-start | bytes 786440 | tf_op jit(solution)/shard_map/ppermute | solution.py:264
  26.6 13.4 %copy-start.21 = (s32[1024]{0:T(1024)}, s32[1024]{0:T(1024)S(1)}, u32[]{:S(2)}) copy-start(s32[1024]{0:T(1024)S(1)} %select_reduce_fusion) | copy-start | bytes 12292
  26.6 13.4 %copy-start.6 = (bf16[128,512]{1,0:T(8,128)(2,1)}, bf16[128,512]{1,0:T(8,128)(2,1)S(1)}, u32[]{:S(2)}) copy-start(bf16[128,512]{1,0:T(8,128)(2,1)S(1)} %collective-permute-done.1.refs_2_) | copy-start | bytes 393220
  26.6 12.0 %collective-permute-start.12 = (bf16[128,512]{1,0:T(8,128)(2,1)S(1)}, bf16[128,512]{1,0:T(8,128)(2,1)S(1)}, u32[]{:S(2)}, u32[]{:S(2)}) collective-permute-start(bf16[128,512]{1,0:T(8,128)(2,1)S(1)} %get-tuple-element.36), channel_id=1, source_target_pairs={{0,6},{1,7},{2,4},{3,5},{4,2},{5,3},{6,0},{7,1},{8,14},{9,15},{10,... | collective-permute-start | bytes 393224 | tf_op jit(solution)/shard_map/ppermute | solution.py:234
  29.4 9.3 %copy-start.7 = (bf16[128,512]{1,0:T(8,128)(2,1)}, bf16[128,512]{1,0:T(8,128)(2,1)S(1)}, u32[]{:S(2)}) copy-start(bf16[128,512]{1,0:T(8,128)(2,1)S(1)} %collective-permute-done.10.refs_4_.refs_0_) | copy-start | bytes 393220
  29.4 9.2 %collective-permute-start.13 = (bf16[128,512]{1,0:T(8,128)(2,1)S(1)}, bf16[128,512]{1,0:T(8,128)(2,1)S(1)}, u32[]{:S(2)}, u32[]{:S(2)}) collective-permute-start(bf16[128,512]{1,0:T(8,128)(2,1)S(1)} %get-tuple-element.29), channel_id=1, source_target_pairs={{0,7},{1,6},{2,5},{3,4},{4,3},{5,2},{6,1},{7,0},{8,15},{9,14},{10,... | collective-permute-start | bytes 393224 | tf_op jit(solution)/shard_map/ppermute | solution.py:234
  29.4 9.3 %copy-start.8 = (bf16[128,512]{1,0:T(8,128)(2,1)}, bf16[128,512]{1,0:T(8,128)(2,1)S(1)}, u32[]{:S(2)}) copy-start(bf16[128,512]{1,0:T(8,128)(2,1)S(1)} %collective-permute-done.11.refs_5_.refs_1_) | copy-start | bytes 393220
  29.4 9.2 %collective-permute-start.2 = (bf16[128,512]{1,0:T(8,128)(2,1)S(1)}, bf16[128,512]{1,0:T(8,128)(2,1)S(1)}, u32[]{:S(2)}, u32[]{:S(2)}) collective-permute-start(bf16[128,512]{1,0:T(8,128)(2,1)S(1)} %get-tuple-element.32), channel_id=1, source_target_pairs={{0,3},{1,2},{2,1},{3,0},{4,7},{5,6},{6,5},{7,4},{8,11},{9,10},{10,... | collective-permute-start | bytes 393224 | tf_op jit(solution)/shard_map/ppermute | solution.py:234
  32.5 15.9 %collective-permute-start.20 = (bf16[4,128,256]{2,1,0:T(8,128)(2,1)}, bf16[4,128,256]{2,1,0:T(8,128)(2,1)}, u32[]{:S(2)}, u32[]{:S(2)}) collective-permute-start(bf16[4,128,256]{2,1,0:T(8,128)(2,1)} %collective-permute-done.19.refs_8_), channel_id=1, source_target_pairs={{0,8},{8,16},{16,24},{24,0},{1,9},{9,17},{17,25},{25,1},{2,10},{10... | collective-permute-start | bytes 786440 | tf_op jit(solution)/shard_map/ppermute | solution.py:264
  38.0 16.4 %copy-start.1 = (bf16[4,128,256]{2,1,0:T(8,128)(2,1)}, bf16[4,128,256]{2,1,0:T(8,128)(2,1)S(1)}, u32[]{:S(2)}) copy-start(bf16[4,128,256]{2,1,0:T(8,128)(2,1)S(1)} %collective-permute-done.8.refs_4_) | copy-start | bytes 786436
  38.0 16.4 %collective-permute-start.9 = (bf16[4,128,256]{2,1,0:T(8,128)(2,1)S(1)}, bf16[4,128,256]{2,1,0:T(8,128)(2,1)S(1)}, u32[]{:S(2)}, u32[]{:S(2)}) collective-permute-start(bf16[4,128,256]{2,1,0:T(8,128)(2,1)S(1)} %collective-permute-done.8.refs_4_), channel_id=1, source_target_pairs={{0,8},{8,16},{16,24},{24,0},{1,9},{9,17},{17,25},{25,1},{2,10},{10... | collective-permute-start | bytes 786440 | tf_op jit(solution)/shard_map/ppermute | solution.py:264
  38.6 0.6 copy-start.10
  38.6 0.7 copy-start.11
  39.4 0.6 copy-start.9
  54.4 0.7 copy-start.2
  59.4 12.1 %collective-permute-start.24 = (bf16[128,512]{1,0:T(8,128)(2,1)S(1)}, bf16[128,512]{1,0:T(8,128)(2,1)S(1)}, u32[]{:S(2)}, u32[]{:S(2)}) collective-permute-start(bf16[128,512]{1,0:T(8,128)(2,1)S(1)} %get-tuple-element.25), channel_id=1, source_target_pairs={{0,4},{1,5},{2,6},{3,7},{4,0},{5,1},{6,2},{7,3},{8,12},{9,13},{10,... | collective-permute-start | bytes 393224 | tf_op jit(solution)/shard_map/ppermute | solution.py:234
  59.5 14.0 %collective-permute-start.25 = (bf16[128,512]{1,0:T(8,128)(2,1)S(1)}, bf16[128,512]{1,0:T(8,128)(2,1)S(1)}, u32[]{:S(2)}, u32[]{:S(2)}) collective-permute-start(bf16[128,512]{1,0:T(8,128)(2,1)S(1)} %get-tuple-element.26), channel_id=1, source_target_pairs={{0,5},{1,4},{2,7},{3,6},{4,1},{5,0},{6,3},{7,2},{8,13},{9,12},{10,... | collective-permute-start | bytes 393224 | tf_op jit(solution)/shard_map/ppermute | solution.py:234
  61.2 13.0 %collective-permute-start.26 = (bf16[128,512]{1,0:T(8,128)(2,1)S(1)}, bf16[128,512]{1,0:T(8,128)(2,1)}, u32[]{:S(2)}, u32[]{:S(2)}) collective-permute-start(bf16[128,512]{1,0:T(8,128)(2,1)S(1)} %get-tuple-element.27), channel_id=1, source_target_pairs={{0,6},{1,7},{2,4},{3,5},{4,2},{5,3},{6,0},{7,1},{8,14},{9,15},{10,... | collective-permute-start | bytes 393224 | tf_op jit(solution)/shard_map/ppermute | solution.py:234
  63.4 10.9 %collective-permute-start.27 = (bf16[128,512]{1,0:T(8,128)(2,1)S(1)}, bf16[128,512]{1,0:T(8,128)(2,1)}, u32[]{:S(2)}, u32[]{:S(2)}) collective-permute-start(bf16[128,512]{1,0:T(8,128)(2,1)S(1)} %get-tuple-element.28), channel_id=1, source_target_pairs={{0,7},{1,6},{2,5},{3,4},{4,3},{5,2},{6,1},{7,0},{8,15},{9,14},{10,... | collective-permute-start | bytes 393224 | tf_op jit(solution)/shard_map/ppermute | solution.py:234
  65.6 0.6 copy-start
  66.2 8.1 %collective-permute-start.21 = (bf16[128,512]{1,0:T(8,128)(2,1)S(1)}, bf16[128,512]{1,0:T(8,128)(2,1)S(1)}, u32[]{:S(2)}, u32[]{:S(2)}) collective-permute-start(bf16[128,512]{1,0:T(8,128)(2,1)S(1)} %get-tuple-element.22), channel_id=1, source_target_pairs={{0,1},{1,0},{2,3},{3,2},{4,5},{5,4},{6,7},{7,6},{8,9},{9,8},{10,11... | collective-permute-start | bytes 393224 | tf_op jit(solution)/shard_map/ppermute | solution.py:234
  71.4 7.5 %copy-start.12 = (bf16[128,512]{1,0:T(8,128)(2,1)}, bf16[128,512]{1,0:T(8,128)(2,1)S(1)}, u32[]{:S(2)}) copy-start(bf16[128,512]{1,0:T(8,128)(2,1)S(1)} %collective-permute-done.24.refs_4_) | copy-start | bytes 393220
  71.4 5.4 %collective-permute-start.22 = (bf16[128,512]{1,0:T(8,128)(2,1)S(1)}, bf16[128,512]{1,0:T(8,128)(2,1)S(1)}, u32[]{:S(2)}, u32[]{:S(2)}) collective-permute-start(bf16[128,512]{1,0:T(8,128)(2,1)S(1)} %get-tuple-element.23), channel_id=1, source_target_pairs={{0,2},{1,3},{2,0},{3,1},{4,6},{5,7},{6,4},{7,5},{8,10},{9,11},{10,... | collective-permute-start | bytes 393224 | tf_op jit(solution)/shard_map/ppermute | solution.py:234
  73.4 5.5 %copy-start.13 = (bf16[128,512]{1,0:T(8,128)(2,1)}, bf16[128,512]{1,0:T(8,128)(2,1)S(1)}, u32[]{:S(2)}) copy-start(bf16[128,512]{1,0:T(8,128)(2,1)S(1)} %collective-permute-done.25.refs_5_) | copy-start | bytes 393220
  73.4 5.5 %collective-permute-start.23 = (bf16[128,512]{1,0:T(8,128)(2,1)S(1)}, bf16[128,512]{1,0:T(8,128)(2,1)S(1)}, u32[]{:S(2)}, u32[]{:S(2)}) collective-permute-start(bf16[128,512]{1,0:T(8,128)(2,1)S(1)} %get-tuple-element.24), channel_id=1, source_target_pairs={{0,3},{1,2},{2,1},{3,0},{4,7},{5,6},{6,5},{7,4},{8,11},{9,10},{10,... | collective-permute-start | bytes 393224 | tf_op jit(solution)/shard_map/ppermute | solution.py:234
  74.3 4.7 %copy-start.14 = (bf16[128,512]{1,0:T(8,128)(2,1)}, bf16[128,512]{1,0:T(8,128)(2,1)S(1)}, u32[]{:S(2)}) copy-start(bf16[128,512]{1,0:T(8,128)(2,1)S(1)} %collective-permute-done.21.refs_1_) | copy-start | bytes 393220
  76.8 2.1 %copy-start.15 = (bf16[128,512]{1,0:T(8,128)(2,1)}, bf16[128,512]{1,0:T(8,128)(2,1)S(1)}, u32[]{:S(2)}) copy-start(bf16[128,512]{1,0:T(8,128)(2,1)S(1)} %collective-permute-done.22.refs_2_) | copy-start | bytes 393220
  79.0 0.6 copy-start.16

commit v4 on v3

--- a/solution.py
+++ b/solution.py
@@ -15,13 +15,17 @@
 HALVES = 2
 
 
+def inside(value):
+    return pltpu.with_memory_space_constraint(value, pltpu.VMEM)
+
+
 def attend_kernel(
     pieces, half, back, slots, opening, closing, parts, place_ref, bounds_ref, firsts_ref, *refs
 ):
     width = KEY_VALUE_HEADS
     count = len(slots)
     steps = sorted({step for step, _ in pieces})
-    q_refs, refs = refs[:count], refs[count:]
+    q_refs, refs = refs[: count // 2], refs[count // 2 :]
     units, refs = refs[: len(pieces)], refs[len(pieces) :]
     if not opening:
         acc_in, stat_in = refs[:2]
@@ -29,7 +33,7 @@
     if closing:
         out_refs, refs = refs[:count], refs[count:]
     acc_ref, stat_ref, score_ref, peak_ref, q_ref, kv_ref, list_ref = refs
-    rows, columns = q_refs[0].shape
+    rows, columns = q_refs[0].shape[1:]
     heads = columns // HEAD_SIZE
     lanes = heads * rows
     shard = parts * rows
@@ -63,7 +67,7 @@
         kv_ref[first : first + unit.shape[0], at : at + rows, :] = unit[...]
     for i in range(count):
         for h in range(heads):
-            q_ref[i, h * rows : (h + 1) * rows, :] = q_refs[i][:, h * HEAD_SIZE : (h + 1) * HEAD_SIZE]
+            q_ref[i, h * rows : (h + 1) * rows, :] = q_refs[i // 2][i % 2, :, h * HEAD_SIZE : (h + 1) * HEAD_SIZE]
     if opening:
         acc_ref[...] = jnp.zeros_like(acc_ref)
         stat_ref[:, 0:1, :] = jnp.full((count, 1, lanes), NEGATIVE, jnp.float32)
@@ -137,12 +141,12 @@
 def attend(place, tables, queries, pieces, half, slots, state, closing, parts, back=0):
     width = KEY_VALUE_HEADS
     bounds, firsts = tables
-    rows, columns = queries[0].shape
+    rows, columns = queries[0].shape[1:]
     lanes = columns // HEAD_SIZE * rows
     vmem = pl.BlockSpec(memory_space=pltpu.VMEM)
     smem = pl.BlockSpec(memory_space=pltpu.SMEM)
     opening = state is None
-    held = () if opening else [pltpu.with_memory_space_constraint(x, pltpu.VMEM) for x in state]
+    held = () if opening else state
     count = len(slots)
     tokens = len({step for step, _, _ in pieces}) * rows
     kept = [
@@ -162,7 +166,7 @@
         scratch = kept + scratch
     else:
         out_shape = kept
-        first = 3 + count + len(pieces)
+        first = 3 + count // 2 + len(pieces)
         aliases = {} if opening else {first: 0, first + 1: 1}
     work = count * 2 * tokens * lanes * HEAD_SIZE * 4
     return pl.pallas_call(
@@ -177,48 +181,53 @@
             parts,
         ),
         out_shape=out_shape,
-        in_specs=[smem, smem] + [vmem] * (1 + count + len(pieces) + len(held)),
+        in_specs=[smem, smem] + [vmem] * (1 + count // 2 + len(pieces) + len(held)),
         out_specs=[vmem] * len(out_shape),
         input_output_aliases=aliases,
         cost_estimate=pl.CostEstimate(
             flops=work, bytes_accessed=4 * width * HEAD_SIZE * lanes, transcendentals=0
         ),
         scratch_shapes=scratch,
+        compiler_params=pltpu.CompilerParams(vmem_limit_bytes=24 << 20),
     )(
         place,
         bounds,
         firsts,
-        *[queries[slot] for slot in slots],
-        *[unit for _, _, unit in pieces],
-        *held,
+        *[inside(queries[slot // 2]) for slot in slots[::2]],
+        *[inside(unit) for _, _, unit in pieces],
+        *[inside(part) for part in held],
     )
 
 
-def collect_kernel(place_ref, *refs):
-    sem = refs[-1]
-    out_ref = refs[-2]
+def collect_kernel(slots, place_ref, *refs):
+    out_ref, sem = refs[-2:]
     copies = []
-    for k, ref in enumerate(refs[:-2]):
-        columns = ref.shape[1]
-        at = pl.multiple_of(jnp.bitwise_xor(place_ref[1], k) * columns, columns)
-        copies.append(pltpu.make_async_copy(ref, out_ref.at[:, pl.ds(at, columns)], sem.at[k]))
+    for i, slot in enumerate(slots):
+        columns = refs[i].shape[1]
+        at = pl.multiple_of(jnp.bitwise_xor(place_ref[1], slot) * columns, columns)
+        copies.append(pltpu.make_async_copy(refs[i], out_ref.at[:, pl.ds(at, columns)], sem.at[i]))
     for copy in copies:
         copy.start()
     for copy in copies:
         copy.wait()
 
 
-def collect(place, blocks):
+def collect(place, blocks, slots, target):
     rows, columns = blocks[0].shape
-    count = len(blocks)
+    count = len(slots)
+    smem = pl.BlockSpec(memory_space=pltpu.SMEM)
+    vmem = pl.BlockSpec(memory_space=pltpu.VMEM)
+    hbm = pl.BlockSpec(memory_space=pltpu.HBM)
+    held = () if target is None else (target,)
     return pl.pallas_call(
-        collect_kernel,
-        out_shape=jax.ShapeDtypeStruct((rows, count * columns), blocks[0].dtype),
-        in_specs=[pl.BlockSpec(memory_space=pltpu.SMEM)]
-        + [pl.BlockSpec(memory_space=pltpu.VMEM)] * count,
-        out_specs=pl.BlockSpec(memory_space=pltpu.HBM),
+        functools.partial(collect_kernel, tuple(slots)),
+        out_shape=jax.ShapeDtypeStruct((rows, len(blocks) * columns), blocks[0].dtype),
+        in_specs=[smem] + [vmem] * count + [hbm] * len(held),
+        out_specs=hbm,
+        input_output_aliases={1 + count: 0} if held else {},
         scratch_shapes=[pltpu.SemaphoreType.DMA((count,))],
-    )(place, *blocks)
+        compiler_params=pltpu.CompilerParams(vmem_limit_bytes=4 << 20),
+    )(place, *[inside(blocks[slot]) for slot in slots], *held)
 
 
 def doc_starts(doc_lengths, positions):
@@ -253,17 +262,25 @@
         return lax.dynamic_slice_in_dim(value, jnp.bitwise_xor(member, k) * size, size, 1)
 
     ring = [(i, (i + 1) % parts) for i in range(parts)]
-    pairs = [
-        swap(jnp.concatenate([cut(packed_key_rows, k), cut(packed_value_rows, k)], axis=1), k)
-        for k in range(width)
-    ]
+
+    def pair(k):
+        return jnp.concatenate([cut(packed_key_rows, k), cut(packed_value_rows, k)], axis=1)
+
+    def spread(block):
+        given = swap(jnp.stack([block(k) for k in range(1, width, 2)]), 1)
+        both = []
+        for k in range(0, width, 2):
+            both.append(jnp.stack([block(k), given[k // 2]]))
+        return [swap(value, 2 * t) for t, value in enumerate(both)]
+
+    pairs = spread(pair)
+    queries = spread(lambda k: cut(packed_query_rows, k))
     opens = [(0, chunk // 2), (chunk // 2, chunk), (chunk, width)]
-    queries = [swap(cut(packed_query_rows, k), k) for k in range(width)]
 
     def move(piece):
         return lax.ppermute(piece, "head", ring)
 
-    held = [(low, jnp.stack(pairs[low:high])) for low, high in opens]
+    held = [(low, jnp.concatenate(pairs[low // 2 : high // 2])) for low, high in opens]
     pieces = [(0, low, piece) for low, piece in held]
     held = [(low, move(piece)) for low, piece in held]
     pieces += [(1, low, piece) for low, piece in held]
@@ -291,7 +308,11 @@
         outs = attends(rest, 1, slots, state, True, parts)
         for slot, out in zip(slots, outs):
             results[slot] = swap(out, slot)
-    return collect(place, [results[k] for k in range(width)])
+    blocks = [results[k] for k in range(width)]
+    target = None
+    for slots in [[0, *range(chunk, width)], list(range(1, chunk))]:
+        target = collect(place, blocks, slots, target)
+    return target
 
 
 def solution(mesh):

time: 82.2 us -> 79.1 us (0.962)
  waiting for transfers between devices: 24.5 us -> 32.6 us
  local copies, waits for them, and re-layouts: 5.91 us -> 1.52 us
  starting transfers between devices: 27.2 us -> 24.1 us
  Pallas kernels: 22.6 us -> 19.8 us
    ppermute x7, waiting for transfers between devices: 13.5 us -> 18.3 us  [move(): return lax.ppermute(piece, 'head', ring)]
    ppermute x21 -> x15, starting transfers between devices: 22.2 us -> 17.4 us  [swap(): return lax.ppermute(block, 'doc', [(i, i ^ k) for i in range(length)])]
    unnamed x46 -> x5, local copies, waits for them, and re-layouts: 3.32 us -> 0.02 us
    pallas_call x4, Pallas kernels: 20.3 us -> 17 us  [attend(): pl.pallas_call(functools.partial(attend_kernel, tuple(((step, first) for...]
    ppermute x21 -> x15, waiting for transfers between devices: 11.1 us -> 14.3 us  [swap(): return lax.ppermute(block, 'doc', [(i, i ^ k) for i in range(length)])]
    ppermute x7, starting transfers between devices: 5.01 us -> 6.63 us  [move(): return lax.ppermute(piece, 'head', ring)]
    dynamic_slice x2 -> x1, local copies, waits for them, and re-layouts: 1.88 us -> 1.13 us  [cut(): lax.dynamic_slice_in_dim(value, jnp.bitwise_xor(member, k) * size, size, 1)]
    pallas_call x1 -> x2, Pallas kernels: 2.32 us -> 2.73 us  [collect(): pl.pallas_call(functools.partial(collect_kernel, tuple(slots)), out_shape...]
  transfers between devices with their start and end apart: 28 -> 22, of which waited for: 9 -> 8; matrix products, arithmetic and copies ran while one was open for 3% -> 1% of each run, Pallas kernels for 20% -> 19%
where the time goes in v4:
time: 79.1 us; the launch traced here: 79 us
  waiting for transfers between devices  32.6 us (41%)
  starting transfers between devices  24.1 us (30%)
  Pallas kernels  19.8 us (25%)
  local copies, waits for them, and re-layouts  1.52 us (2%)
    ppermute x7, waiting for transfers between devices, move(): return lax.ppermute(piece, 'head', ring)  18.3 us
    ppermute x15, starting transfers between devices, swap(): return lax.ppermute(block, 'doc', [(i, i ^ k) for i in range(length)])  17.4 us
    pallas_call x4, Pallas kernels, attend(): pl.pallas_call(functools.partial(attend_kernel, tuple(((step, first) for...  17 us
    ppermute x15, waiting for transfers between devices, swap(): return lax.ppermute(block, 'doc', [(i, i ^ k) for i in range(length)])  14.3 us
    ppermute x7, starting transfers between devices, move(): return lax.ppermute(piece, 'head', ring)  6.63 us
    pallas_call x2, Pallas kernels, collect(): pl.pallas_call(functools.partial(collect_kernel, tuple(slots)), out_shape...  2.73 us
  transfers between devices with their start and end apart: 22, of which 8 were waited for; matrix products, arithmetic and copies ran while one was open for 1% of the time, Pallas kernels for 19%

profile of v4, /device:TPU:0, one launch (start us, length us, event | category | flops | bytes accessed | tf_op | source)
XLA Modules:
  0.0 79.0 jit_solution(15832532780331563377)
XLA Ops:
  0.0 0.0 copy-start
  0.0 1.1 %constant_dynamic-slice_fusion.2 = (bf16[128,128]{1,0:T(8,128)(2,1)S(1)}, bf16[128,128]{1,0:T(8,128)(2,1)S(1)}, bf16[128,128]{1,0:T(8,128)(2,1)S(1)}, bf16[128,1...) fusion(bf16[128,1024]{1,0:T(8,128)(2,1)} %param.6, ...), kind=kLoop, calls=%fused_computation.32 | loop fusion | bytes 1048608 | tf_op jit(solution)/shard_map/dynamic_slice | solution.py:262
  1.2 0.0 copy-start.1
  1.3 0.6 collective-permute-start.2
  1.8 0.0 copy-done
  1.8 0.1 dynamic-slice_bitcast_fusion
  1.9 0.1 pad_maximum_fusion
  2.0 0.2 collective-permute-start
  2.2 0.1 add_bitcast_fusion
  2.4 0.0 copy-done.1
  2.4 0.1 copy.10
  2.5 0.1 reduce
  2.6 0.1 select_reduce_fusion
  2.7 0.3 collective-permute-done.2
  3.0 2.9 %collective-permute-start.11 = (bf16[2,128,256]{2,1,0:T(8,128)(2,1)S(1)}, bf16[2,128,256]{2,1,0:T(8,128)(2,1)S(1)}, u32[]{:S(2)}, u32[]{:S(2)}) collective-permute-start(bf16[2,128,256]{2,1,0:T(8,128)(2,1)S(1)} %pad_maximum_fusion.10), channel_id=1, source_target_pairs={{0,2},{1,3},{2,0},{3,1},{4,6},{5,7},{6,4},{7,5},{8,10},{9,11},{10,... | collective-permute-start | bytes 393224 | tf_op jit(solution)/shard_map/ppermute | solution.py:243
  6.0 1.6 %collective-permute-start.3 = (bf16[2,128,256]{2,1,0:T(8,128)(2,1)S(1)}, bf16[2,128,256]{2,1,0:T(8,128)(2,1)S(1)}, u32[]{:S(2)}, u32[]{:S(2)}) collective-permute-start(bf16[2,128,256]{2,1,0:T(8,128)(2,1)S(1)} %pad_maximum_fusion.7), channel_id=1, source_target_pairs={{0,4},{1,5},{2,6},{3,7},{4,0},{5,1},{6,2},{7,3},{8,12},{9,13},{10,... | collective-permute-start | bytes 393224 | tf_op jit(solution)/shard_map/ppermute | solution.py:243
  7.6 0.1 collective-permute-start.4
  7.7 2.1 %collective-permute-start.10 = (bf16[2,128,256]{2,1,0:T(8,128)(2,1)S(1)}, bf16[2,128,256]{2,1,0:T(8,128)(2,1)S(1)}, u32[]{:S(2)}, u32[]{:S(2)}) collective-permute-start(bf16[2,128,256]{2,1,0:T(8,128)(2,1)S(1)} %pad_maximum_fusion.9.refs_4_), channel_id=1, source_target_pairs={{0,8},{8,16},{16,24},{24,0},{1,9},{9,17},{17,25},{25,1},{2,10},{10... | collective-permute-start | bytes 393224 | tf_op jit(solution)/shard_map/ppermute | solution.py:281
  9.8 4.3 %collective-permute-done.3 = bf16[2,128,256]{2,1,0:T(8,128)(2,1)S(1)} collective-permute-done((bf16[2,128,256]{2,1,0:T(8,128)(2,1)S(1)}, bf16[2,128,256]{2,1,0:T(8,128)(2,1)S(1)}, u32[]{:S(2)}, u32[]{:S(2)}) %collective-permute-start.3) | collective-permute-done | bytes 131104 | tf_op jit(solution)/shard_map/ppermute | solution.py:243
  14.1 0.0 collective-permute-done.4
  14.1 1.6 %collective-permute-start.5 = (bf16[4,128,256]{2,1,0:T(8,128)(2,1)S(1)}, bf16[4,128,256]{2,1,0:T(8,128)(2,1)S(1)}, u32[]{:S(2)}, u32[]{:S(2)}) collective-permute-start(bf16[4,128,256]{2,1,0:T(8,128)(2,1)S(1)} %constant_dynamic-update-slice_fusion.refs_6_), channel_id=1, source_target_pairs={{0,8},{8,16},{16,24},{24,0},{1,9},{9,17},{17,25},{25,1},{2,10},{10... | collective-permute-start | bytes 786440 | tf_op jit(solution)/shard_map/ppermute | solution.py:281
  15.8 0.0 collective-permute-done.11.refs_5_
  15.8 1.6 %collective-permute-start.12 = (bf16[2,128,256]{2,1,0:T(8,128)(2,1)S(1)}, bf16[2,128,256]{2,1,0:T(8,128)(2,1)S(1)}, u32[]{:S(2)}, u32[]{:S(2)}) collective-permute-start(bf16[2,128,256]{2,1,0:T(8,128)(2,1)S(1)} %collective-permute-done.11.refs_5_), channel_id=1, source_target_pairs={{0,8},{8,16},{16,24},{24,0},{1,9},{9,17},{17,25},{25,1},{2,10},{10... | collective-permute-start | bytes 393224 | tf_op jit(solution)/shard_map/ppermute | solution.py:281
  17.4 0.0 collective-permute-done
  17.4 1.6 %collective-permute-start.8 = (bf16[2,128,512]{2,1,0:T(8,128)(2,1)S(1)}, bf16[2,128,512]{2,1,0:T(8,128)(2,1)S(1)}, u32[]{:S(2)}, u32[]{:S(2)}) collective-permute-start(bf16[2,128,512]{2,1,0:T(8,128)(2,1)S(1)} %pad_maximum_fusion.4), channel_id=1, source_target_pairs={{0,4},{1,5},{2,6},{3,7},{4,0},{5,1},{6,2},{7,3},{8,12},{9,13},{10,... | collective-permute-start | bytes 786440 | tf_op jit(solution)/shard_map/ppermute | solution.py:243
  19.0 0.0 collective-permute-done.10.refs_7_
  19.0 6.7 %collective-permute-done.12.refs_8_ = bf16[2,128,256]{2,1,0:T(8,128)(2,1)S(1)} collective-permute-done((bf16[2,128,256]{2,1,0:T(8,128)(2,1)S(1)}, bf16[2,128,256]{2,1,0:T(8,128)(2,1)S(1)}, u32[]{:S(2)}, u32[]{:S(2)}) %collective-permute-start.12) | collective-permute-done | bytes 131104 | tf_op jit(solution)/shard_map/ppermute | solution.py:281
  25.8 0.1 collective-permute-start.13
  25.9 1.8 %collective-permute-start.9 = (bf16[2,128,512]{2,1,0:T(8,128)(2,1)S(1)}, bf16[2,128,512]{2,1,0:T(8,128)(2,1)S(1)}, u32[]{:S(2)}, u32[]{:S(2)}) collective-permute-start(bf16[2,128,512]{2,1,0:T(8,128)(2,1)S(1)} %pad_maximum_fusion.5), channel_id=1, source_target_pairs={{0,6},{1,7},{2,4},{3,5},{4,2},{5,3},{6,0},{7,1},{8,14},{9,15},{10,... | collective-permute-start | bytes 786440 | tf_op jit(solution)/shard_map/ppermute | solution.py:243
  27.7 0.0 collective-permute-done.5.refs_9_
  27.7 1.3 %collective-permute-start.6 = (bf16[4,128,256]{2,1,0:T(8,128)(2,1)S(1)}, bf16[4,128,256]{2,1,0:T(8,128)(2,1)S(1)}, u32[]{:S(2)}, u32[]{:S(2)}) collective-permute-start(bf16[4,128,256]{2,1,0:T(8,128)(2,1)S(1)} %collective-permute-done.5.refs_9_), channel_id=1, source_target_pairs={{0,8},{8,16},{16,24},{24,0},{1,9},{9,17},{17,25},{25,1},{2,10},{10... | collective-permute-start | bytes 786440 | tf_op jit(solution)/shard_map/ppermute | solution.py:281
  29.0 1.6 %collective-permute-start.1 = (bf16[2,128,512]{2,1,0:T(8,128)(2,1)S(1)}, bf16[2,128,512]{2,1,0:T(8,128)(2,1)S(1)}, u32[]{:S(2)}, u32[]{:S(2)}) collective-permute-start(bf16[2,128,512]{2,1,0:T(8,128)(2,1)S(1)} %pad_maximum_fusion.2), channel_id=1, source_target_pairs={{0,2},{1,3},{2,0},{3,1},{4,6},{5,7},{6,4},{7,5},{8,10},{9,11},{10,... | collective-permute-start | bytes 786440 | tf_op jit(solution)/shard_map/ppermute | solution.py:243
  30.6 0.1 slice_reduce_fusion.bounds_ref
  30.7 6.0 %collective-permute-done.13.refs_4_ = bf16[4,128,256]{2,1,0:T(8,128)(2,1)S(1)} collective-permute-done((bf16[4,128,256]{2,1,0:T(8,128)(2,1)S(1)}, bf16[4,128,256]{2,1,0:T(8,128)(2,1)S(1)}, u32[]{:S(2)}, u32[]{:S(2)}) %collective-permute-start.13) | collective-permute-done | bytes 262176 | tf_op jit(solution)/shard_map/ppermute | solution.py:281
  36.8 0.0 collective-permute-start.14
  36.8 0.1 pad_add_fusion.place_ref
  36.9 5.5 %collective-permute-done.6.refs_2_ = bf16[4,128,256]{2,1,0:T(8,128)(2,1)S(1)} collective-permute-done((bf16[4,128,256]{2,1,0:T(8,128)(2,1)S(1)}, bf16[4,128,256]{2,1,0:T(8,128)(2,1)S(1)}, u32[]{:S(2)}, u32[]{:S(2)}) %collective-permute-start.6) | collective-permute-done | bytes 262176 | tf_op jit(solution)/shard_map/ppermute | solution.py:281
  42.4 0.0 collective-permute-start.7
  42.4 0.0 collective-permute-done.8.refs_2_.refs_0_
  42.4 0.0 collective-permute-done.9.refs_3_.refs_1_
  42.5 0.0 collective-permute-done.1.refs_1_
  42.5 7.4 %shard_map.46 = (f32[8,128,512]{2,1,0:T(8,128)S(1)}, f32[8,8,512]{2,1,0:T(8,128)S(1)}) custom-call(s32[3]{0:T(128)S(1)} %pad_add_fusion.place_ref, s32[8]{0:T(128)S(1)} %slice_reduce_fusion.bounds_ref, s32[8,128]{1,0:T(8,128)S(1)} %bitcast.40, bf16[2,128,512]{2,1,0:T(8,128)(2,1)S(1)} %pad_maximum_fusion.1.refs_0_, ...), custom_call_target="tpu_custom_call" | custom-call | flops 1073741824 | bytes 2097152 | tf_op jit(solution)/shard_map/pallas_call | solution.py:172
  49.8 0.0 collective-permute-done.14.refs_5_
  49.8 5.1 %shard_map.47 = (f32[8,128,512]{2,1,0:T(8,128)S(1)}, f32[8,8,512]{2,1,0:T(8,128)S(1)}) custom-call(s32[3]{0:T(128)S(1)} %pad_add_fusion.place_ref, s32[8]{0:T(128)S(1)} %slice_reduce_fusion.bounds_ref, s32[8,128]{1,0:T(8,128)S(1)} %bitcast.41, bf16[2,128,512]{2,1,0:T(8,128)(2,1)S(1)} %pad_maximum_fusion.1.refs_0_, ...), custom_call_target="tpu_custom_call", output_to_operand_aliasing={{0}: (9, {}), {1}: (10, {})} | custom-call | flops 1073741824 | bytes 2097152 | tf_op jit(solution)/shard_map/pallas_call | solution.py:172
  55.0 0.0 collective-permute-done.7.refs_3_
  55.0 3.5 %shard_map.49 = (bf16[128,512]{1,0:T(8,128)(2,1)S(1)}, bf16[128,512]{1,0:T(8,128)(2,1)S(1)}, bf16[128,512]{1,0:T(8,128)(2,1)S(1)}, bf16[128,512]{1,0:T(8,128)(2,1)S(1)}) custom-call(s32[3]{0:T(128)S(1)} %pad_add_fusion.place_ref, s32[8]{0:T(128)S(1)} %slice_reduce_fusion.bounds_ref, s32[8,128]{1,0:T(8,128)S(1)} %bitcast.42, ...), custom_call_target="tpu_custom_call" | custom-call | flops 536870912 | bytes 2097152 | tf_op jit(solution)/shard_map/pallas_call | solution.py:172
  58.5 0.2 collective-permute-start.18
  58.7 0.0 collective-permute-start.19
  58.7 3.1 %collective-permute-start.20 = (bf16[128,512]{1,0:T(8,128)(2,1)S(1)}, bf16[128,512]{1,0:T(8,128)(2,1)S(1)}, u32[]{:S(2)}, u32[]{:S(2)}) collective-permute-start(bf16[128,512]{1,0:T(8,128)(2,1)S(1)} %get-tuple-element.27), channel_id=1, source_target_pairs={{0,6},{1,7},{2,4},{3,5},{4,2},{5,3},{6,0},{7,1},{8,14},{9,15},{10,... | collective-permute-start | bytes 393224 | tf_op jit(solution)/shard_map/ppermute | solution.py:243
  61.8 1.2 %collective-permute-start.21 = (bf16[128,512]{1,0:T(8,128)(2,1)S(1)}, bf16[128,512]{1,0:T(8,128)(2,1)S(1)}, u32[]{:S(2)}, u32[]{:S(2)}) collective-permute-start(bf16[128,512]{1,0:T(8,128)(2,1)S(1)} %get-tuple-element.28), channel_id=1, source_target_pairs={{0,7},{1,6},{2,5},{3,4},{4,3},{5,2},{6,1},{7,0},{8,15},{9,14},{10,... | collective-permute-start | bytes 393224 | tf_op jit(solution)/shard_map/ppermute | solution.py:243
  63.0 1.0 %shard_map.48 = (bf16[128,512]{1,0:T(8,128)(2,1)S(1)}, bf16[128,512]{1,0:T(8,128)(2,1)S(1)}, bf16[128,512]{1,0:T(8,128)(2,1)S(1)}, bf16[128,512]{1,0:T(8,128)(2,1)S(1)}) custom-call(s32[3]{0:T(128)S(1)} %pad_add_fusion.place_ref, s32[8]{0:T(128)S(1)} %slice_reduce_fusion.bounds_ref, s32[8,128]{1,0:T(8,128)S(1)} %bitcast.43, ...), custom_call_target="tpu_custom_call" | custom-call | flops 536870912 | bytes 2097152 | tf_op jit(solution)/shard_map/pallas_call | solution.py:172
  64.0 0.1 collective-permute-start.15
  64.1 6.1 %collective-permute-done.18.refs_1_ = bf16[128,512]{1,0:T(8,128)(2,1)S(1)} collective-permute-done((bf16[128,512]{1,0:T(8,128)(2,1)S(1)}, bf16[128,512]{1,0:T(8,128)(2,1)S(1)}, u32[]{:S(2)}, u32[]{:S(2)}) %collective-permute-start.18) | collective-permute-done | bytes 131104 | tf_op jit(solution)/shard_map/ppermute | solution.py:243
  70.2 1.7 %collective-permute-start.16 = (bf16[128,512]{1,0:T(8,128)(2,1)S(1)}, bf16[128,512]{1,0:T(8,128)(2,1)S(1)}, u32[]{:S(2)}, u32[]{:S(2)}) collective-permute-start(bf16[128,512]{1,0:T(8,128)(2,1)S(1)} %get-tuple-element.22), channel_id=1, source_target_pairs={{0,2},{1,3},{2,0},{3,1},{4,6},{5,7},{6,4},{7,5},{8,10},{9,11},{10,... | collective-permute-start | bytes 393224 | tf_op jit(solution)/shard_map/ppermute | solution.py:243
  71.9 0.0 collective-permute-done.19.refs_2_
  71.9 0.8 %collective-permute-start.17 = (bf16[128,512]{1,0:T(8,128)(2,1)S(1)}, bf16[128,512]{1,0:T(8,128)(2,1)S(1)}, u32[]{:S(2)}, u32[]{:S(2)}) collective-permute-start(bf16[128,512]{1,0:T(8,128)(2,1)S(1)} %get-tuple-element.23), channel_id=1, source_target_pairs={{0,3},{1,2},{2,1},{3,0},{4,7},{5,6},{6,5},{7,4},{8,11},{9,10},{10,... | collective-permute-start | bytes 393224 | tf_op jit(solution)/shard_map/ppermute | solution.py:243
  72.7 0.0 collective-permute-done.20.refs_3_
  72.7 0.0 collective-permute-done.21.refs_4_
  72.7 1.4 %shard_map.50.refs_3_ = bf16[128,4096]{1,0:T(8,128)(2,1)} custom-call(s32[3]{0:T(128)S(1)} %pad_add_fusion.place_ref, bf16[128,512]{1,0:T(8,128)(2,1)S(1)} %get-tuple-element.24.refs_0_, bf16[128,512]{1,0:T(8,128)(2,1)S(1)} %collective-permute-done.18.refs_1_, bf16[128,512]{1,0:T(8,128)(2,1)S(1)} %collective-permute-done.19.refs_2_, ...), custom_call_target="tpu_custom_call" | custom-call | tf_op jit(solution)/shard_map/pallas_call | solution.py:222
  74.1 0.0 collective-permute-done.15.refs_0_
  74.1 1.4 %collective-permute-done.16.refs_1_ = bf16[128,512]{1,0:T(8,128)(2,1)S(1)} collective-permute-done((bf16[128,512]{1,0:T(8,128)(2,1)S(1)}, bf16[128,512]{1,0:T(8,128)(2,1)S(1)}, u32[]{:S(2)}, u32[]{:S(2)}) %collective-permute-start.16) | collective-permute-done | bytes 131104 | tf_op jit(solution)/shard_map/ppermute | solution.py:243
  75.5 2.2 %collective-permute-done.17.refs_2_ = bf16[128,512]{1,0:T(8,128)(2,1)S(1)} collective-permute-done((bf16[128,512]{1,0:T(8,128)(2,1)S(1)}, bf16[128,512]{1,0:T(8,128)(2,1)S(1)}, u32[]{:S(2)}, u32[]{:S(2)}) %collective-permute-start.17) | collective-permute-done | bytes 131104 | tf_op jit(solution)/shard_map/ppermute | solution.py:243
  77.7 1.3 %shard_map.51 = bf16[128,4096]{1,0:T(8,128)(2,1)} custom-call(s32[3]{0:T(128)S(1)} %pad_add_fusion.place_ref, bf16[128,512]{1,0:T(8,128)(2,1)S(1)} %collective-permute-done.15.refs_0_, bf16[128,512]{1,0:T(8,128)(2,1)S(1)} %collective-permute-done.16.refs_1_, bf16[128,512]{1,0:T(8,128)(2,1)S(1)} %collective-permute-done.17.refs_2_, ...), custom_call_target="tpu_custom_call", output_to_operand_aliasing={{}: (4, {})} | custom-call | tf_op jit(solution)/shard_map/pallas_call | solution.py:222
  (24 shorter events, 0.4 us)
Async XLA Ops:
  0.0 1.8 %copy-start = (bf16[128,4096]{1,0:T(8,128)(2,1)S(1)}, bf16[128,4096]{1,0:T(8,128)(2,1)}, u32[]{:S(2)}) copy-start(bf16[128,4096]{1,0:T(8,128)(2,1)} %param.4) | copy-start | bytes 3145732
  1.2 1.1 %copy-start.1 = (s32[16]{0:T(128)S(1)}, s32[16]{0:T(128)}, u32[]{:S(2)}) copy-start(s32[16]{0:T(128)} %param.7) | copy-start | bytes 196
  1.3 1.7 %collective-permute-start.2 = (bf16[4,128,256]{2,1,0:T(8,128)(2,1)S(1)}, bf16[4,128,256]{2,1,0:T(8,128)(2,1)S(1)}, u32[]{:S(2)}, u32[]{:S(2)}) collective-permute-start(bf16[4,128,256]{2,1,0:T(8,128)(2,1)S(1)} %pad_maximum_fusion.3), channel_id=1, source_target_pairs={{0,1},{1,0},{2,3},{3,2},{4,5},{5,4},{6,7},{7,6},{8,9},{9,8},{10,11... | collective-permute-start | bytes 786440 | tf_op jit(solution)/shard_map/ppermute | solution.py:243
  2.0 15.3 %collective-permute-start = (bf16[4,128,512]{2,1,0:T(8,128)(2,1)S(1)}, bf16[4,128,512]{2,1,0:T(8,128)(2,1)S(1)}, u32[]{:S(2)}, u32[]{:S(2)}) collective-permute-start(bf16[4,128,512]{2,1,0:T(8,128)(2,1)S(1)} %pad_maximum_fusion), channel_id=1, source_target_pairs={{0,1},{1,0},{2,3},{3,2},{4,5},{5,4},{6,7},{7,6},{8,9},{9,8},{10,11... | collective-permute-start | bytes 1572872 | tf_op jit(solution)/shard_map/ppermute | solution.py:243
  3.0 12.7 %collective-permute-start.11 = (bf16[2,128,256]{2,1,0:T(8,128)(2,1)S(1)}, bf16[2,128,256]{2,1,0:T(8,128)(2,1)S(1)}, u32[]{:S(2)}, u32[]{:S(2)}) collective-permute-start(bf16[2,128,256]{2,1,0:T(8,128)(2,1)S(1)} %pad_maximum_fusion.10), channel_id=1, source_target_pairs={{0,2},{1,3},{2,0},{3,1},{4,6},{5,7},{6,4},{7,5},{8,10},{9,11},{10,... | collective-permute-start | bytes 393224 | tf_op jit(solution)/shard_map/ppermute | solution.py:243
  6.0 8.1 %collective-permute-start.3 = (bf16[2,128,256]{2,1,0:T(8,128)(2,1)S(1)}, bf16[2,128,256]{2,1,0:T(8,128)(2,1)S(1)}, u32[]{:S(2)}, u32[]{:S(2)}) collective-permute-start(bf16[2,128,256]{2,1,0:T(8,128)(2,1)S(1)} %pad_maximum_fusion.7), channel_id=1, source_target_pairs={{0,4},{1,5},{2,6},{3,7},{4,0},{5,1},{6,2},{7,3},{8,12},{9,13},{10,... | collective-permute-start | bytes 393224 | tf_op jit(solution)/shard_map/ppermute | solution.py:243
  7.6 6.5 %collective-permute-start.4 = (bf16[2,128,256]{2,1,0:T(8,128)(2,1)S(1)}, bf16[2,128,256]{2,1,0:T(8,128)(2,1)S(1)}, u32[]{:S(2)}, u32[]{:S(2)}) collective-permute-start(bf16[2,128,256]{2,1,0:T(8,128)(2,1)S(1)} %pad_maximum_fusion.8), channel_id=1, source_target_pairs={{0,6},{1,7},{2,4},{3,5},{4,2},{5,3},{6,0},{7,1},{8,14},{9,15},{10,... | collective-permute-start | bytes 393224 | tf_op jit(solution)/shard_map/ppermute | solution.py:243
  7.7 11.3 %collective-permute-start.10 = (bf16[2,128,256]{2,1,0:T(8,128)(2,1)S(1)}, bf16[2,128,256]{2,1,0:T(8,128)(2,1)S(1)}, u32[]{:S(2)}, u32[]{:S(2)}) collective-permute-start(bf16[2,128,256]{2,1,0:T(8,128)(2,1)S(1)} %pad_maximum_fusion.9.refs_4_), channel_id=1, source_target_pairs={{0,8},{8,16},{16,24},{24,0},{1,9},{9,17},{17,25},{25,1},{2,10},{10... | collective-permute-start | bytes 393224 | tf_op jit(solution)/shard_map/ppermute | solution.py:281
  14.1 13.5 %collective-permute-start.5 = (bf16[4,128,256]{2,1,0:T(8,128)(2,1)S(1)}, bf16[4,128,256]{2,1,0:T(8,128)(2,1)S(1)}, u32[]{:S(2)}, u32[]{:S(2)}) collective-permute-start(bf16[4,128,256]{2,1,0:T(8,128)(2,1)S(1)} %constant_dynamic-update-slice_fusion.refs_6_), channel_id=1, source_target_pairs={{0,8},{8,16},{16,24},{24,0},{1,9},{9,17},{17,25},{25,1},{2,10},{10... | collective-permute-start | bytes 786440 | tf_op jit(solution)/shard_map/ppermute | solution.py:281
  15.8 9.9 %collective-permute-start.12 = (bf16[2,128,256]{2,1,0:T(8,128)(2,1)S(1)}, bf16[2,128,256]{2,1,0:T(8,128)(2,1)S(1)}, u32[]{:S(2)}, u32[]{:S(2)}) collective-permute-start(bf16[2,128,256]{2,1,0:T(8,128)(2,1)S(1)} %collective-permute-done.11.refs_5_), channel_id=1, source_target_pairs={{0,8},{8,16},{16,24},{24,0},{1,9},{9,17},{17,25},{25,1},{2,10},{10... | collective-permute-start | bytes 393224 | tf_op jit(solution)/shard_map/ppermute | solution.py:281
  17.4 25.0 %collective-permute-start.8 = (bf16[2,128,512]{2,1,0:T(8,128)(2,1)S(1)}, bf16[2,128,512]{2,1,0:T(8,128)(2,1)S(1)}, u32[]{:S(2)}, u32[]{:S(2)}) collective-permute-start(bf16[2,128,512]{2,1,0:T(8,128)(2,1)S(1)} %pad_maximum_fusion.4), channel_id=1, source_target_pairs={{0,4},{1,5},{2,6},{3,7},{4,0},{5,1},{6,2},{7,3},{8,12},{9,13},{10,... | collective-permute-start | bytes 786440 | tf_op jit(solution)/shard_map/ppermute | solution.py:243
  25.8 11.0 %collective-permute-start.13 = (bf16[4,128,256]{2,1,0:T(8,128)(2,1)S(1)}, bf16[4,128,256]{2,1,0:T(8,128)(2,1)S(1)}, u32[]{:S(2)}, u32[]{:S(2)}) collective-permute-start(bf16[4,128,256]{2,1,0:T(8,128)(2,1)S(1)} %pad_maximum_fusion.6), channel_id=1, source_target_pairs={{0,8},{8,16},{16,24},{24,0},{1,9},{9,17},{17,25},{25,1},{2,10},{10... | collective-permute-start | bytes 786440 | tf_op jit(solution)/shard_map/ppermute | solution.py:281
  25.9 16.6 %collective-permute-start.9 = (bf16[2,128,512]{2,1,0:T(8,128)(2,1)S(1)}, bf16[2,128,512]{2,1,0:T(8,128)(2,1)S(1)}, u32[]{:S(2)}, u32[]{:S(2)}) collective-permute-start(bf16[2,128,512]{2,1,0:T(8,128)(2,1)S(1)} %pad_maximum_fusion.5), channel_id=1, source_target_pairs={{0,6},{1,7},{2,4},{3,5},{4,2},{5,3},{6,0},{7,1},{8,14},{9,15},{10,... | collective-permute-start | bytes 786440 | tf_op jit(solution)/shard_map/ppermute | solution.py:243
  27.7 14.7 %collective-permute-start.6 = (bf16[4,128,256]{2,1,0:T(8,128)(2,1)S(1)}, bf16[4,128,256]{2,1,0:T(8,128)(2,1)S(1)}, u32[]{:S(2)}, u32[]{:S(2)}) collective-permute-start(bf16[4,128,256]{2,1,0:T(8,128)(2,1)S(1)} %collective-permute-done.5.refs_9_), channel_id=1, source_target_pairs={{0,8},{8,16},{16,24},{24,0},{1,9},{9,17},{17,25},{25,1},{2,10},{10... | collective-permute-start | bytes 786440 | tf_op jit(solution)/shard_map/ppermute | solution.py:281
  29.0 13.5 %collective-permute-start.1 = (bf16[2,128,512]{2,1,0:T(8,128)(2,1)S(1)}, bf16[2,128,512]{2,1,0:T(8,128)(2,1)S(1)}, u32[]{:S(2)}, u32[]{:S(2)}) collective-permute-start(bf16[2,128,512]{2,1,0:T(8,128)(2,1)S(1)} %pad_maximum_fusion.2), channel_id=1, source_target_pairs={{0,2},{1,3},{2,0},{3,1},{4,6},{5,7},{6,4},{7,5},{8,10},{9,11},{10,... | collective-permute-start | bytes 786440 | tf_op jit(solution)/shard_map/ppermute | solution.py:243
  36.8 13.0 %collective-permute-start.14 = (bf16[4,128,256]{2,1,0:T(8,128)(2,1)S(1)}, bf16[4,128,256]{2,1,0:T(8,128)(2,1)S(1)}, u32[]{:S(2)}, u32[]{:S(2)}) collective-permute-start(bf16[4,128,256]{2,1,0:T(8,128)(2,1)S(1)} %collective-permute-done.13.refs_4_), channel_id=1, source_target_pairs={{0,8},{8,16},{16,24},{24,0},{1,9},{9,17},{17,25},{25,1},{2,10},{10... | collective-permute-start | bytes 786440 | tf_op jit(solution)/shard_map/ppermute | solution.py:281
  42.4 12.6 %collective-permute-start.7 = (bf16[4,128,256]{2,1,0:T(8,128)(2,1)S(1)}, bf16[4,128,256]{2,1,0:T(8,128)(2,1)S(1)}, u32[]{:S(2)}, u32[]{:S(2)}) collective-permute-start(bf16[4,128,256]{2,1,0:T(8,128)(2,1)S(1)} %collective-permute-done.6.refs_2_), channel_id=1, source_target_pairs={{0,8},{8,16},{16,24},{24,0},{1,9},{9,17},{17,25},{25,1},{2,10},{10... | collective-permute-start | bytes 786440 | tf_op jit(solution)/shard_map/ppermute | solution.py:281
  58.5 11.6 %collective-permute-start.18 = (bf16[128,512]{1,0:T(8,128)(2,1)S(1)}, bf16[128,512]{1,0:T(8,128)(2,1)S(1)}, u32[]{:S(2)}, u32[]{:S(2)}) collective-permute-start(bf16[128,512]{1,0:T(8,128)(2,1)S(1)} %get-tuple-element.25), channel_id=1, source_target_pairs={{0,4},{1,5},{2,6},{3,7},{4,0},{5,1},{6,2},{7,3},{8,12},{9,13},{10,... | collective-permute-start | bytes 393224 | tf_op jit(solution)/shard_map/ppermute | solution.py:243
  58.7 13.1 %collective-permute-start.19 = (bf16[128,512]{1,0:T(8,128)(2,1)S(1)}, bf16[128,512]{1,0:T(8,128)(2,1)S(1)}, u32[]{:S(2)}, u32[]{:S(2)}) collective-permute-start(bf16[128,512]{1,0:T(8,128)(2,1)S(1)} %get-tuple-element.26), channel_id=1, source_target_pairs={{0,5},{1,4},{2,7},{3,6},{4,1},{5,0},{6,3},{7,2},{8,13},{9,12},{10,... | collective-permute-start | bytes 393224 | tf_op jit(solution)/shard_map/ppermute | solution.py:243
  58.7 13.9 %collective-permute-start.20 = (bf16[128,512]{1,0:T(8,128)(2,1)S(1)}, bf16[128,512]{1,0:T(8,128)(2,1)S(1)}, u32[]{:S(2)}, u32[]{:S(2)}) collective-permute-start(bf16[128,512]{1,0:T(8,128)(2,1)S(1)} %get-tuple-element.27), channel_id=1, source_target_pairs={{0,6},{1,7},{2,4},{3,5},{4,2},{5,3},{6,0},{7,1},{8,14},{9,15},{10,... | collective-permute-start | bytes 393224 | tf_op jit(solution)/shard_map/ppermute | solution.py:243
  61.8 10.9 %collective-permute-start.21 = (bf16[128,512]{1,0:T(8,128)(2,1)S(1)}, bf16[128,512]{1,0:T(8,128)(2,1)S(1)}, u32[]{:S(2)}, u32[]{:S(2)}) collective-permute-start(bf16[128,512]{1,0:T(8,128)(2,1)S(1)} %get-tuple-element.28), channel_id=1, source_target_pairs={{0,7},{1,6},{2,5},{3,4},{4,3},{5,2},{6,1},{7,0},{8,15},{9,14},{10,... | collective-permute-start | bytes 393224 | tf_op jit(solution)/shard_map/ppermute | solution.py:243
  64.0 10.1 %collective-permute-start.15 = (bf16[128,512]{1,0:T(8,128)(2,1)S(1)}, bf16[128,512]{1,0:T(8,128)(2,1)S(1)}, u32[]{:S(2)}, u32[]{:S(2)}) collective-permute-start(bf16[128,512]{1,0:T(8,128)(2,1)S(1)} %get-tuple-element.21), channel_id=1, source_target_pairs={{0,1},{1,0},{2,3},{3,2},{4,5},{5,4},{6,7},{7,6},{8,9},{9,8},{10,11... | collective-permute-start | bytes 393224 | tf_op jit(solution)/shard_map/ppermute | solution.py:243
  70.2 5.3 %collective-permute-start.16 = (bf16[128,512]{1,0:T(8,128)(2,1)S(1)}, bf16[128,512]{1,0:T(8,128)(2,1)S(1)}, u32[]{:S(2)}, u32[]{:S(2)}) collective-permute-start(bf16[128,512]{1,0:T(8,128)(2,1)S(1)} %get-tuple-element.22), channel_id=1, source_target_pairs={{0,2},{1,3},{2,0},{3,1},{4,6},{5,7},{6,4},{7,5},{8,10},{9,11},{10,... | collective-permute-start | bytes 393224 | tf_op jit(solution)/shard_map/ppermute | solution.py:243
  71.9 5.8 %collective-permute-start.17 = (bf16[128,512]{1,0:T(8,128)(2,1)S(1)}, bf16[128,512]{1,0:T(8,128)(2,1)S(1)}, u32[]{:S(2)}, u32[]{:S(2)}) collective-permute-start(bf16[128,512]{1,0:T(8,128)(2,1)S(1)} %get-tuple-element.23), channel_id=1, source_target_pairs={{0,3},{1,2},{2,1},{3,0},{4,7},{5,6},{6,5},{7,4},{8,11},{9,10},{10,... | collective-permute-start | bytes 393224 | tf_op jit(solution)/shard_map/ppermute | solution.py:243

commit v5 on v4

--- a/solution.py
+++ b/solution.py
@@ -199,35 +199,32 @@
     )
 
 
-def collect_kernel(slots, place_ref, *refs):
-    out_ref, sem = refs[-2:]
+def collect_kernel(place_ref, *refs):
+    sem = refs[-1]
+    out_ref = refs[-2]
     copies = []
-    for i, slot in enumerate(slots):
-        columns = refs[i].shape[1]
-        at = pl.multiple_of(jnp.bitwise_xor(place_ref[1], slot) * columns, columns)
-        copies.append(pltpu.make_async_copy(refs[i], out_ref.at[:, pl.ds(at, columns)], sem.at[i]))
+    for k, ref in enumerate(refs[:-2]):
+        columns = ref.shape[1]
+        at = pl.multiple_of(jnp.bitwise_xor(place_ref[1], k) * columns, columns)
+        copies.append(pltpu.make_async_copy(ref, out_ref.at[:, pl.ds(at, columns)], sem.at[k]))
     for copy in copies:
         copy.start()
     for copy in copies:
         copy.wait()
 
 
-def collect(place, blocks, slots, target):
+def collect(place, blocks):
     rows, columns = blocks[0].shape
-    count = len(slots)
-    smem = pl.BlockSpec(memory_space=pltpu.SMEM)
-    vmem = pl.BlockSpec(memory_space=pltpu.VMEM)
-    hbm = pl.BlockSpec(memory_space=pltpu.HBM)
-    held = () if target is None else (target,)
+    count = len(blocks)
     return pl.pallas_call(
-        functools.partial(collect_kernel, tuple(slots)),
-        out_shape=jax.ShapeDtypeStruct((rows, len(blocks) * columns), blocks[0].dtype),
-        in_specs=[smem] + [vmem] * count + [hbm] * len(held),
-        out_specs=hbm,
-        input_output_aliases={1 + count: 0} if held else {},
+        collect_kernel,
+        out_shape=jax.ShapeDtypeStruct((rows, count * columns), blocks[0].dtype),
+        in_specs=[pl.BlockSpec(memory_space=pltpu.SMEM)]
+        + [pl.BlockSpec(memory_space=pltpu.VMEM)] * count,
+        out_specs=pl.BlockSpec(memory_space=pltpu.HBM),
         scratch_shapes=[pltpu.SemaphoreType.DMA((count,))],
         compiler_params=pltpu.CompilerParams(vmem_limit_bytes=4 << 20),
-    )(place, *[inside(blocks[slot]) for slot in slots], *held)
+    )(place, *[inside(block) for block in blocks])
 
 
 def doc_starts(doc_lengths, positions):
@@ -308,11 +305,7 @@
         outs = attends(rest, 1, slots, state, True, parts)
         for slot, out in zip(slots, outs):
             results[slot] = swap(out, slot)
-    blocks = [results[k] for k in range(width)]
-    target = None
-    for slots in [[0, *range(chunk, width)], list(range(1, chunk))]:
-        target = collect(place, blocks, slots, target)
-    return target
+    return collect(place, [results[k] for k in range(width)])
 
 
 def solution(mesh):

time: 79.1 us -> 79.4 us (level)
  waiting for transfers between devices: 32.6 us -> 34 us
  Pallas kernels: 19.8 us -> 18.6 us
    ppermute x15, waiting for transfers between devices: 14.3 us -> 15.7 us  [swap(): return lax.ppermute(block, 'doc', [(i, i ^ k) for i in range(length)])]
    pallas_call x2 -> x1, Pallas kernels: 2.73 us -> 1.57 us  [collect(): pl.pallas_call(collect_kernel, out_shape=jax.ShapeDtypeStruct((rows, coun...]
  transfers between devices with their start and end apart: 22 -> 22, of which waited for: 8 -> 8; matrix products, arithmetic and copies ran while one was open for 1% -> 1% of each run, Pallas kernels for 19% -> 17%
where the time goes in v5:
time: 79.4 us; the launch traced here: 79.2 us
  waiting for transfers between devices  34 us (43%)
  starting transfers between devices  24.1 us (30%)
  Pallas kernels  18.6 us (23%)
  local copies, waits for them, and re-layouts  1.52 us (2%)
    ppermute x7, waiting for transfers between devices, move(): return lax.ppermute(piece, 'head', ring)  18.3 us
    ppermute x15, starting transfers between devices, swap(): return lax.ppermute(block, 'doc', [(i, i ^ k) for i in range(length)])  17.4 us
    pallas_call x4, Pallas kernels, attend(): pl.pallas_call(functools.partial(attend_kernel, tuple(((step, first) for...  17 us
    ppermute x15, waiting for transfers between devices, swap(): return lax.ppermute(block, 'doc', [(i, i ^ k) for i in range(length)])  15.7 us
    ppermute x7, starting transfers between devices, move(): return lax.ppermute(piece, 'head', ring)  6.63 us
  transfers between devices with their start and end apart: 22, of which 8 were waited for; matrix products, arithmetic and copies ran while one was open for 1% of the time, Pallas kernels for 17%

profile of v5, /device:TPU:0, one launch (start us, length us, event | category | flops | bytes accessed | tf_op | source)
XLA Modules:
  0.0 79.2 jit_solution(17123047602792283385)
XLA Ops:
  0.0 0.0 copy-start
  0.0 1.1 %constant_dynamic-slice_fusion.2 = (bf16[128,128]{1,0:T(8,128)(2,1)S(1)}, bf16[128,128]{1,0:T(8,128)(2,1)S(1)}, bf16[128,128]{1,0:T(8,128)(2,1)S(1)}, bf16[128,1...) fusion(bf16[128,1024]{1,0:T(8,128)(2,1)} %param.6, ...), kind=kLoop, calls=%fused_computation.32 | loop fusion | bytes 1048608 | tf_op jit(solution)/shard_map/dynamic_slice | solution.py:259
  1.2 0.0 copy-start.1
  1.3 0.6 collective-permute-start.2
  1.8 0.0 copy-done
  1.8 0.1 dynamic-slice_bitcast_fusion
  1.9 0.1 pad_maximum_fusion
  2.0 0.2 collective-permute-start
  2.2 0.1 add_bitcast_fusion
  2.4 0.0 copy-done.1
  2.4 0.1 copy.9
  2.5 0.1 reduce
  2.6 0.1 select_reduce_fusion
  2.7 0.3 collective-permute-done.2
  3.0 2.9 %collective-permute-start.11 = (bf16[2,128,256]{2,1,0:T(8,128)(2,1)S(1)}, bf16[2,128,256]{2,1,0:T(8,128)(2,1)S(1)}, u32[]{:S(2)}, u32[]{:S(2)}) collective-permute-start(bf16[2,128,256]{2,1,0:T(8,128)(2,1)S(1)} %pad_maximum_fusion.10), channel_id=1, source_target_pairs={{0,2},{1,3},{2,0},{3,1},{4,6},{5,7},{6,4},{7,5},{8,10},{9,11},{10,... | collective-permute-start | bytes 393224 | tf_op jit(solution)/shard_map/ppermute | solution.py:240
  6.0 1.6 %collective-permute-start.3 = (bf16[2,128,256]{2,1,0:T(8,128)(2,1)S(1)}, bf16[2,128,256]{2,1,0:T(8,128)(2,1)S(1)}, u32[]{:S(2)}, u32[]{:S(2)}) collective-permute-start(bf16[2,128,256]{2,1,0:T(8,128)(2,1)S(1)} %pad_maximum_fusion.7), channel_id=1, source_target_pairs={{0,4},{1,5},{2,6},{3,7},{4,0},{5,1},{6,2},{7,3},{8,12},{9,13},{10,... | collective-permute-start | bytes 393224 | tf_op jit(solution)/shard_map/ppermute | solution.py:240
  7.6 0.1 collective-permute-start.4
  7.7 2.1 %collective-permute-start.10 = (bf16[2,128,256]{2,1,0:T(8,128)(2,1)S(1)}, bf16[2,128,256]{2,1,0:T(8,128)(2,1)S(1)}, u32[]{:S(2)}, u32[]{:S(2)}) collective-permute-start(bf16[2,128,256]{2,1,0:T(8,128)(2,1)S(1)} %pad_maximum_fusion.9.refs_4_), channel_id=1, source_target_pairs={{0,8},{8,16},{16,24},{24,0},{1,9},{9,17},{17,25},{25,1},{2,10},{10... | collective-permute-start | bytes 393224 | tf_op jit(solution)/shard_map/ppermute | solution.py:278
  9.8 4.3 %collective-permute-done.3 = bf16[2,128,256]{2,1,0:T(8,128)(2,1)S(1)} collective-permute-done((bf16[2,128,256]{2,1,0:T(8,128)(2,1)S(1)}, bf16[2,128,256]{2,1,0:T(8,128)(2,1)S(1)}, u32[]{:S(2)}, u32[]{:S(2)}) %collective-permute-start.3) | collective-permute-done | bytes 131104 | tf_op jit(solution)/shard_map/ppermute | solution.py:240
  14.1 0.0 collective-permute-done.4
  14.1 1.6 %collective-permute-start.5 = (bf16[4,128,256]{2,1,0:T(8,128)(2,1)S(1)}, bf16[4,128,256]{2,1,0:T(8,128)(2,1)S(1)}, u32[]{:S(2)}, u32[]{:S(2)}) collective-permute-start(bf16[4,128,256]{2,1,0:T(8,128)(2,1)S(1)} %constant_dynamic-update-slice_fusion.refs_6_), channel_id=1, source_target_pairs={{0,8},{8,16},{16,24},{24,0},{1,9},{9,17},{17,25},{25,1},{2,10},{10... | collective-permute-start | bytes 786440 | tf_op jit(solution)/shard_map/ppermute | solution.py:278
  15.8 0.0 collective-permute-done.11.refs_5_
  15.8 1.6 %collective-permute-start.12 = (bf16[2,128,256]{2,1,0:T(8,128)(2,1)S(1)}, bf16[2,128,256]{2,1,0:T(8,128)(2,1)S(1)}, u32[]{:S(2)}, u32[]{:S(2)}) collective-permute-start(bf16[2,128,256]{2,1,0:T(8,128)(2,1)S(1)} %collective-permute-done.11.refs_5_), channel_id=1, source_target_pairs={{0,8},{8,16},{16,24},{24,0},{1,9},{9,17},{17,25},{25,1},{2,10},{10... | collective-permute-start | bytes 393224 | tf_op jit(solution)/shard_map/ppermute | solution.py:278
  17.4 0.0 collective-permute-done
  17.4 1.6 %collective-permute-start.8 = (bf16[2,128,512]{2,1,0:T(8,128)(2,1)S(1)}, bf16[2,128,512]{2,1,0:T(8,128)(2,1)S(1)}, u32[]{:S(2)}, u32[]{:S(2)}) collective-permute-start(bf16[2,128,512]{2,1,0:T(8,128)(2,1)S(1)} %pad_maximum_fusion.4), channel_id=1, source_target_pairs={{0,4},{1,5},{2,6},{3,7},{4,0},{5,1},{6,2},{7,3},{8,12},{9,13},{10,... | collective-permute-start | bytes 786440 | tf_op jit(solution)/shard_map/ppermute | solution.py:240
  19.0 0.0 collective-permute-done.10.refs_7_
  19.0 6.7 %collective-permute-done.12.refs_8_ = bf16[2,128,256]{2,1,0:T(8,128)(2,1)S(1)} collective-permute-done((bf16[2,128,256]{2,1,0:T(8,128)(2,1)S(1)}, bf16[2,128,256]{2,1,0:T(8,128)(2,1)S(1)}, u32[]{:S(2)}, u32[]{:S(2)}) %collective-permute-start.12) | collective-permute-done | bytes 131104 | tf_op jit(solution)/shard_map/ppermute | solution.py:278
  25.8 0.1 collective-permute-start.13
  25.9 1.8 %collective-permute-start.9 = (bf16[2,128,512]{2,1,0:T(8,128)(2,1)S(1)}, bf16[2,128,512]{2,1,0:T(8,128)(2,1)S(1)}, u32[]{:S(2)}, u32[]{:S(2)}) collective-permute-start(bf16[2,128,512]{2,1,0:T(8,128)(2,1)S(1)} %pad_maximum_fusion.5), channel_id=1, source_target_pairs={{0,6},{1,7},{2,4},{3,5},{4,2},{5,3},{6,0},{7,1},{8,14},{9,15},{10,... | collective-permute-start | bytes 786440 | tf_op jit(solution)/shard_map/ppermute | solution.py:240
  27.7 0.0 collective-permute-done.5.refs_9_
  27.7 1.3 %collective-permute-start.6 = (bf16[4,128,256]{2,1,0:T(8,128)(2,1)S(1)}, bf16[4,128,256]{2,1,0:T(8,128)(2,1)S(1)}, u32[]{:S(2)}, u32[]{:S(2)}) collective-permute-start(bf16[4,128,256]{2,1,0:T(8,128)(2,1)S(1)} %collective-permute-done.5.refs_9_), channel_id=1, source_target_pairs={{0,8},{8,16},{16,24},{24,0},{1,9},{9,17},{17,25},{25,1},{2,10},{10... | collective-permute-start | bytes 786440 | tf_op jit(solution)/shard_map/ppermute | solution.py:278
  29.0 1.6 %collective-permute-start.1 = (bf16[2,128,512]{2,1,0:T(8,128)(2,1)S(1)}, bf16[2,128,512]{2,1,0:T(8,128)(2,1)S(1)}, u32[]{:S(2)}, u32[]{:S(2)}) collective-permute-start(bf16[2,128,512]{2,1,0:T(8,128)(2,1)S(1)} %pad_maximum_fusion.2), channel_id=1, source_target_pairs={{0,2},{1,3},{2,0},{3,1},{4,6},{5,7},{6,4},{7,5},{8,10},{9,11},{10,... | collective-permute-start | bytes 786440 | tf_op jit(solution)/shard_map/ppermute | solution.py:240
  30.6 0.1 slice_reduce_fusion.bounds_ref
  30.7 6.0 %collective-permute-done.13.refs_4_ = bf16[4,128,256]{2,1,0:T(8,128)(2,1)S(1)} collective-permute-done((bf16[4,128,256]{2,1,0:T(8,128)(2,1)S(1)}, bf16[4,128,256]{2,1,0:T(8,128)(2,1)S(1)}, u32[]{:S(2)}, u32[]{:S(2)}) %collective-permute-start.13) | collective-permute-done | bytes 262176 | tf_op jit(solution)/shard_map/ppermute | solution.py:278
  36.8 0.0 collective-permute-start.14
  36.8 0.1 pad_add_fusion.place_ref
  36.9 5.5 %collective-permute-done.6.refs_2_ = bf16[4,128,256]{2,1,0:T(8,128)(2,1)S(1)} collective-permute-done((bf16[4,128,256]{2,1,0:T(8,128)(2,1)S(1)}, bf16[4,128,256]{2,1,0:T(8,128)(2,1)S(1)}, u32[]{:S(2)}, u32[]{:S(2)}) %collective-permute-start.6) | collective-permute-done | bytes 262176 | tf_op jit(solution)/shard_map/ppermute | solution.py:278
  42.4 0.0 collective-permute-start.7
  42.4 0.0 collective-permute-done.8.refs_2_.refs_0_
  42.4 0.0 collective-permute-done.9.refs_3_.refs_1_
  42.5 0.0 collective-permute-done.1.refs_1_
  42.5 7.4 %shard_map.46 = (f32[8,128,512]{2,1,0:T(8,128)S(1)}, f32[8,8,512]{2,1,0:T(8,128)S(1)}) custom-call(s32[3]{0:T(128)S(1)} %pad_add_fusion.place_ref, s32[8]{0:T(128)S(1)} %slice_reduce_fusion.bounds_ref, s32[8,128]{1,0:T(8,128)S(1)} %bitcast.40, bf16[2,128,512]{2,1,0:T(8,128)(2,1)S(1)} %pad_maximum_fusion.1.refs_0_, ...), custom_call_target="tpu_custom_call" | custom-call | flops 1073741824 | bytes 2097152 | tf_op jit(solution)/shard_map/pallas_call | solution.py:172
  49.8 0.0 collective-permute-done.14.refs_5_
  49.8 5.1 %shard_map.47 = (f32[8,128,512]{2,1,0:T(8,128)S(1)}, f32[8,8,512]{2,1,0:T(8,128)S(1)}) custom-call(s32[3]{0:T(128)S(1)} %pad_add_fusion.place_ref, s32[8]{0:T(128)S(1)} %slice_reduce_fusion.bounds_ref, s32[8,128]{1,0:T(8,128)S(1)} %bitcast.41, bf16[2,128,512]{2,1,0:T(8,128)(2,1)S(1)} %pad_maximum_fusion.1.refs_0_, ...), custom_call_target="tpu_custom_call", output_to_operand_aliasing={{0}: (9, {}), {1}: (10, {})} | custom-call | flops 1073741824 | bytes 2097152 | tf_op jit(solution)/shard_map/pallas_call | solution.py:172
  55.0 0.0 collective-permute-done.7.refs_3_
  55.0 3.5 %shard_map.49 = (bf16[128,512]{1,0:T(8,128)(2,1)S(1)}, bf16[128,512]{1,0:T(8,128)(2,1)S(1)}, bf16[128,512]{1,0:T(8,128)(2,1)S(1)}, bf16[128,512]{1,0:T(8,128)(2,1)S(1)}) custom-call(s32[3]{0:T(128)S(1)} %pad_add_fusion.place_ref, s32[8]{0:T(128)S(1)} %slice_reduce_fusion.bounds_ref, s32[8,128]{1,0:T(8,128)S(1)} %bitcast.42, ...), custom_call_target="tpu_custom_call" | custom-call | flops 536870912 | bytes 2097152 | tf_op jit(solution)/shard_map/pallas_call | solution.py:172
  58.5 0.2 collective-permute-start.18
  58.7 0.0 collective-permute-start.19
  58.7 3.1 %collective-permute-start.20 = (bf16[128,512]{1,0:T(8,128)(2,1)S(1)}, bf16[128,512]{1,0:T(8,128)(2,1)S(1)}, u32[]{:S(2)}, u32[]{:S(2)}) collective-permute-start(bf16[128,512]{1,0:T(8,128)(2,1)S(1)} %get-tuple-element.27), channel_id=1, source_target_pairs={{0,6},{1,7},{2,4},{3,5},{4,2},{5,3},{6,0},{7,1},{8,14},{9,15},{10,... | collective-permute-start | bytes 393224 | tf_op jit(solution)/shard_map/ppermute | solution.py:240
  61.8 1.2 %collective-permute-start.21 = (bf16[128,512]{1,0:T(8,128)(2,1)S(1)}, bf16[128,512]{1,0:T(8,128)(2,1)S(1)}, u32[]{:S(2)}, u32[]{:S(2)}) collective-permute-start(bf16[128,512]{1,0:T(8,128)(2,1)S(1)} %get-tuple-element.28), channel_id=1, source_target_pairs={{0,7},{1,6},{2,5},{3,4},{4,3},{5,2},{6,1},{7,0},{8,15},{9,14},{10,... | collective-permute-start | bytes 393224 | tf_op jit(solution)/shard_map/ppermute | solution.py:240
  63.0 1.0 %shard_map.48 = (bf16[128,512]{1,0:T(8,128)(2,1)S(1)}, bf16[128,512]{1,0:T(8,128)(2,1)S(1)}, bf16[128,512]{1,0:T(8,128)(2,1)S(1)}, bf16[128,512]{1,0:T(8,128)(2,1)S(1)}) custom-call(s32[3]{0:T(128)S(1)} %pad_add_fusion.place_ref, s32[8]{0:T(128)S(1)} %slice_reduce_fusion.bounds_ref, s32[8,128]{1,0:T(8,128)S(1)} %bitcast.43, ...), custom_call_target="tpu_custom_call" | custom-call | flops 536870912 | bytes 2097152 | tf_op jit(solution)/shard_map/pallas_call | solution.py:172
  64.0 0.1 collective-permute-start.15
  64.1 6.1 %collective-permute-done.18.refs_4_ = bf16[128,512]{1,0:T(8,128)(2,1)S(1)} collective-permute-done((bf16[128,512]{1,0:T(8,128)(2,1)S(1)}, bf16[128,512]{1,0:T(8,128)(2,1)S(1)}, u32[]{:S(2)}, u32[]{:S(2)}) %collective-permute-start.18) | collective-permute-done | bytes 131104 | tf_op jit(solution)/shard_map/ppermute | solution.py:240
  70.2 1.7 %collective-permute-start.16 = (bf16[128,512]{1,0:T(8,128)(2,1)S(1)}, bf16[128,512]{1,0:T(8,128)(2,1)S(1)}, u32[]{:S(2)}, u32[]{:S(2)}) collective-permute-start(bf16[128,512]{1,0:T(8,128)(2,1)S(1)} %get-tuple-element.23), channel_id=1, source_target_pairs={{0,2},{1,3},{2,0},{3,1},{4,6},{5,7},{6,4},{7,5},{8,10},{9,11},{10,... | collective-permute-start | bytes 393224 | tf_op jit(solution)/shard_map/ppermute | solution.py:240
  71.9 0.0 collective-permute-done.19.refs_5_
  71.9 0.8 %collective-permute-start.17 = (bf16[128,512]{1,0:T(8,128)(2,1)S(1)}, bf16[128,512]{1,0:T(8,128)(2,1)S(1)}, u32[]{:S(2)}, u32[]{:S(2)}) collective-permute-start(bf16[128,512]{1,0:T(8,128)(2,1)S(1)} %get-tuple-element.24), channel_id=1, source_target_pairs={{0,3},{1,2},{2,1},{3,0},{4,7},{5,6},{6,5},{7,4},{8,11},{9,10},{10,... | collective-permute-start | bytes 393224 | tf_op jit(solution)/shard_map/ppermute | solution.py:240
  72.7 0.0 collective-permute-done.20.refs_6_
  72.7 0.0 collective-permute-done.21.refs_7_
  72.7 0.0 collective-permute-done.15.refs_1_
  72.7 2.8 %collective-permute-done.16.refs_2_ = bf16[128,512]{1,0:T(8,128)(2,1)S(1)} collective-permute-done((bf16[128,512]{1,0:T(8,128)(2,1)S(1)}, bf16[128,512]{1,0:T(8,128)(2,1)S(1)}, u32[]{:S(2)}, u32[]{:S(2)}) %collective-permute-start.16) | collective-permute-done | bytes 131104 | tf_op jit(solution)/shard_map/ppermute | solution.py:240
  75.5 2.2 %collective-permute-done.17.refs_3_ = bf16[128,512]{1,0:T(8,128)(2,1)S(1)} collective-permute-done((bf16[128,512]{1,0:T(8,128)(2,1)S(1)}, bf16[128,512]{1,0:T(8,128)(2,1)S(1)}, u32[]{:S(2)}, u32[]{:S(2)}) %collective-permute-start.17) | collective-permute-done | bytes 131104 | tf_op jit(solution)/shard_map/ppermute | solution.py:240
  77.7 1.6 %shard_map.50 = bf16[128,4096]{1,0:T(8,128)(2,1)} custom-call(s32[3]{0:T(128)S(1)} %pad_add_fusion.place_ref, bf16[128,512]{1,0:T(8,128)(2,1)S(1)} %get-tuple-element.21.refs_0_, bf16[128,512]{1,0:T(8,128)(2,1)S(1)} %collective-permute-done.15.refs_1_, bf16[128,512]{1,0:T(8,128)(2,1)S(1)} %collective-permute-done.16.refs_2_, ...), custom_call_target="tpu_custom_call" | custom-call | tf_op jit(solution)/shard_map/pallas_call | solution.py:219
  (24 shorter events, 0.4 us)
Async XLA Ops:
  0.0 1.8 %copy-start = (bf16[128,4096]{1,0:T(8,128)(2,1)S(1)}, bf16[128,4096]{1,0:T(8,128)(2,1)}, u32[]{:S(2)}) copy-start(bf16[128,4096]{1,0:T(8,128)(2,1)} %param.4) | copy-start | bytes 3145732
  1.2 1.1 %copy-start.1 = (s32[16]{0:T(128)S(1)}, s32[16]{0:T(128)}, u32[]{:S(2)}) copy-start(s32[16]{0:T(128)} %param.7) | copy-start | bytes 196
  1.3 1.7 %collective-permute-start.2 = (bf16[4,128,256]{2,1,0:T(8,128)(2,1)S(1)}, bf16[4,128,256]{2,1,0:T(8,128)(2,1)S(1)}, u32[]{:S(2)}, u32[]{:S(2)}) collective-permute-start(bf16[4,128,256]{2,1,0:T(8,128)(2,1)S(1)} %pad_maximum_fusion.3), channel_id=1, source_target_pairs={{0,1},{1,0},{2,3},{3,2},{4,5},{5,4},{6,7},{7,6},{8,9},{9,8},{10,11... | collective-permute-start | bytes 786440 | tf_op jit(solution)/shard_map/ppermute | solution.py:240
  2.0 15.3 %collective-permute-start = (bf16[4,128,512]{2,1,0:T(8,128)(2,1)S(1)}, bf16[4,128,512]{2,1,0:T(8,128)(2,1)S(1)}, u32[]{:S(2)}, u32[]{:S(2)}) collective-permute-start(bf16[4,128,512]{2,1,0:T(8,128)(2,1)S(1)} %pad_maximum_fusion), channel_id=1, source_target_pairs={{0,1},{1,0},{2,3},{3,2},{4,5},{5,4},{6,7},{7,6},{8,9},{9,8},{10,11... | collective-permute-start | bytes 1572872 | tf_op jit(solution)/shard_map/ppermute | solution.py:240
  3.0 12.7 %collective-permute-start.11 = (bf16[2,128,256]{2,1,0:T(8,128)(2,1)S(1)}, bf16[2,128,256]{2,1,0:T(8,128)(2,1)S(1)}, u32[]{:S(2)}, u32[]{:S(2)}) collective-permute-start(bf16[2,128,256]{2,1,0:T(8,128)(2,1)S(1)} %pad_maximum_fusion.10), channel_id=1, source_target_pairs={{0,2},{1,3},{2,0},{3,1},{4,6},{5,7},{6,4},{7,5},{8,10},{9,11},{10,... | collective-permute-start | bytes 393224 | tf_op jit(solution)/shard_map/ppermute | solution.py:240
  6.0 8.1 %collective-permute-start.3 = (bf16[2,128,256]{2,1,0:T(8,128)(2,1)S(1)}, bf16[2,128,256]{2,1,0:T(8,128)(2,1)S(1)}, u32[]{:S(2)}, u32[]{:S(2)}) collective-permute-start(bf16[2,128,256]{2,1,0:T(8,128)(2,1)S(1)} %pad_maximum_fusion.7), channel_id=1, source_target_pairs={{0,4},{1,5},{2,6},{3,7},{4,0},{5,1},{6,2},{7,3},{8,12},{9,13},{10,... | collective-permute-start | bytes 393224 | tf_op jit(solution)/shard_map/ppermute | solution.py:240
  7.6 6.5 %collective-permute-start.4 = (bf16[2,128,256]{2,1,0:T(8,128)(2,1)S(1)}, bf16[2,128,256]{2,1,0:T(8,128)(2,1)S(1)}, u32[]{:S(2)}, u32[]{:S(2)}) collective-permute-start(bf16[2,128,256]{2,1,0:T(8,128)(2,1)S(1)} %pad_maximum_fusion.8), channel_id=1, source_target_pairs={{0,6},{1,7},{2,4},{3,5},{4,2},{5,3},{6,0},{7,1},{8,14},{9,15},{10,... | collective-permute-start | bytes 393224 | tf_op jit(solution)/shard_map/ppermute | solution.py:240
  7.7 11.3 %collective-permute-start.10 = (bf16[2,128,256]{2,1,0:T(8,128)(2,1)S(1)}, bf16[2,128,256]{2,1,0:T(8,128)(2,1)S(1)}, u32[]{:S(2)}, u32[]{:S(2)}) collective-permute-start(bf16[2,128,256]{2,1,0:T(8,128)(2,1)S(1)} %pad_maximum_fusion.9.refs_4_), channel_id=1, source_target_pairs={{0,8},{8,16},{16,24},{24,0},{1,9},{9,17},{17,25},{25,1},{2,10},{10... | collective-permute-start | bytes 393224 | tf_op jit(solution)/shard_map/ppermute | solution.py:278
  14.1 13.5 %collective-permute-start.5 = (bf16[4,128,256]{2,1,0:T(8,128)(2,1)S(1)}, bf16[4,128,256]{2,1,0:T(8,128)(2,1)S(1)}, u32[]{:S(2)}, u32[]{:S(2)}) collective-permute-start(bf16[4,128,256]{2,1,0:T(8,128)(2,1)S(1)} %constant_dynamic-update-slice_fusion.refs_6_), channel_id=1, source_target_pairs={{0,8},{8,16},{16,24},{24,0},{1,9},{9,17},{17,25},{25,1},{2,10},{10... | collective-permute-start | bytes 786440 | tf_op jit(solution)/shard_map/ppermute | solution.py:278
  15.8 9.9 %collective-permute-start.12 = (bf16[2,128,256]{2,1,0:T(8,128)(2,1)S(1)}, bf16[2,128,256]{2,1,0:T(8,128)(2,1)S(1)}, u32[]{:S(2)}, u32[]{:S(2)}) collective-permute-start(bf16[2,128,256]{2,1,0:T(8,128)(2,1)S(1)} %collective-permute-done.11.refs_5_), channel_id=1, source_target_pairs={{0,8},{8,16},{16,24},{24,0},{1,9},{9,17},{17,25},{25,1},{2,10},{10... | collective-permute-start | bytes 393224 | tf_op jit(solution)/shard_map/ppermute | solution.py:278
  17.4 25.0 %collective-permute-start.8 = (bf16[2,128,512]{2,1,0:T(8,128)(2,1)S(1)}, bf16[2,128,512]{2,1,0:T(8,128)(2,1)S(1)}, u32[]{:S(2)}, u32[]{:S(2)}) collective-permute-start(bf16[2,128,512]{2,1,0:T(8,128)(2,1)S(1)} %pad_maximum_fusion.4), channel_id=1, source_target_pairs={{0,4},{1,5},{2,6},{3,7},{4,0},{5,1},{6,2},{7,3},{8,12},{9,13},{10,... | collective-permute-start | bytes 786440 | tf_op jit(solution)/shard_map/ppermute | solution.py:240
  25.8 11.0 %collective-permute-start.13 = (bf16[4,128,256]{2,1,0:T(8,128)(2,1)S(1)}, bf16[4,128,256]{2,1,0:T(8,128)(2,1)S(1)}, u32[]{:S(2)}, u32[]{:S(2)}) collective-permute-start(bf16[4,128,256]{2,1,0:T(8,128)(2,1)S(1)} %pad_maximum_fusion.6), channel_id=1, source_target_pairs={{0,8},{8,16},{16,24},{24,0},{1,9},{9,17},{17,25},{25,1},{2,10},{10... | collective-permute-start | bytes 786440 | tf_op jit(solution)/shard_map/ppermute | solution.py:278
  25.9 16.6 %collective-permute-start.9 = (bf16[2,128,512]{2,1,0:T(8,128)(2,1)S(1)}, bf16[2,128,512]{2,1,0:T(8,128)(2,1)S(1)}, u32[]{:S(2)}, u32[]{:S(2)}) collective-permute-start(bf16[2,128,512]{2,1,0:T(8,128)(2,1)S(1)} %pad_maximum_fusion.5), channel_id=1, source_target_pairs={{0,6},{1,7},{2,4},{3,5},{4,2},{5,3},{6,0},{7,1},{8,14},{9,15},{10,... | collective-permute-start | bytes 786440 | tf_op jit(solution)/shard_map/ppermute | solution.py:240
  27.7 14.7 %collective-permute-start.6 = (bf16[4,128,256]{2,1,0:T(8,128)(2,1)S(1)}, bf16[4,128,256]{2,1,0:T(8,128)(2,1)S(1)}, u32[]{:S(2)}, u32[]{:S(2)}) collective-permute-start(bf16[4,128,256]{2,1,0:T(8,128)(2,1)S(1)} %collective-permute-done.5.refs_9_), channel_id=1, source_target_pairs={{0,8},{8,16},{16,24},{24,0},{1,9},{9,17},{17,25},{25,1},{2,10},{10... | collective-permute-start | bytes 786440 | tf_op jit(solution)/shard_map/ppermute | solution.py:278
  29.0 13.5 %collective-permute-start.1 = (bf16[2,128,512]{2,1,0:T(8,128)(2,1)S(1)}, bf16[2,128,512]{2,1,0:T(8,128)(2,1)S(1)}, u32[]{:S(2)}, u32[]{:S(2)}) collective-permute-start(bf16[2,128,512]{2,1,0:T(8,128)(2,1)S(1)} %pad_maximum_fusion.2), channel_id=1, source_target_pairs={{0,2},{1,3},{2,0},{3,1},{4,6},{5,7},{6,4},{7,5},{8,10},{9,11},{10,... | collective-permute-start | bytes 786440 | tf_op jit(solution)/shard_map/ppermute | solution.py:240
  36.8 13.0 %collective-permute-start.14 = (bf16[4,128,256]{2,1,0:T(8,128)(2,1)S(1)}, bf16[4,128,256]{2,1,0:T(8,128)(2,1)S(1)}, u32[]{:S(2)}, u32[]{:S(2)}) collective-permute-start(bf16[4,128,256]{2,1,0:T(8,128)(2,1)S(1)} %collective-permute-done.13.refs_4_), channel_id=1, source_target_pairs={{0,8},{8,16},{16,24},{24,0},{1,9},{9,17},{17,25},{25,1},{2,10},{10... | collective-permute-start | bytes 786440 | tf_op jit(solution)/shard_map/ppermute | solution.py:278
  42.4 12.6 %collective-permute-start.7 = (bf16[4,128,256]{2,1,0:T(8,128)(2,1)S(1)}, bf16[4,128,256]{2,1,0:T(8,128)(2,1)S(1)}, u32[]{:S(2)}, u32[]{:S(2)}) collective-permute-start(bf16[4,128,256]{2,1,0:T(8,128)(2,1)S(1)} %collective-permute-done.6.refs_2_), channel_id=1, source_target_pairs={{0,8},{8,16},{16,24},{24,0},{1,9},{9,17},{17,25},{25,1},{2,10},{10... | collective-permute-start | bytes 786440 | tf_op jit(solution)/shard_map/ppermute | solution.py:278
  58.5 11.6 %collective-permute-start.18 = (bf16[128,512]{1,0:T(8,128)(2,1)S(1)}, bf16[128,512]{1,0:T(8,128)(2,1)S(1)}, u32[]{:S(2)}, u32[]{:S(2)}) collective-permute-start(bf16[128,512]{1,0:T(8,128)(2,1)S(1)} %get-tuple-element.25), channel_id=1, source_target_pairs={{0,4},{1,5},{2,6},{3,7},{4,0},{5,1},{6,2},{7,3},{8,12},{9,13},{10,... | collective-permute-start | bytes 393224 | tf_op jit(solution)/shard_map/ppermute | solution.py:240
  58.7 13.1 %collective-permute-start.19 = (bf16[128,512]{1,0:T(8,128)(2,1)S(1)}, bf16[128,512]{1,0:T(8,128)(2,1)S(1)}, u32[]{:S(2)}, u32[]{:S(2)}) collective-permute-start(bf16[128,512]{1,0:T(8,128)(2,1)S(1)} %get-tuple-element.26), channel_id=1, source_target_pairs={{0,5},{1,4},{2,7},{3,6},{4,1},{5,0},{6,3},{7,2},{8,13},{9,12},{10,... | collective-permute-start | bytes 393224 | tf_op jit(solution)/shard_map/ppermute | solution.py:240
  58.7 13.9 %collective-permute-start.20 = (bf16[128,512]{1,0:T(8,128)(2,1)S(1)}, bf16[128,512]{1,0:T(8,128)(2,1)S(1)}, u32[]{:S(2)}, u32[]{:S(2)}) collective-permute-start(bf16[128,512]{1,0:T(8,128)(2,1)S(1)} %get-tuple-element.27), channel_id=1, source_target_pairs={{0,6},{1,7},{2,4},{3,5},{4,2},{5,3},{6,0},{7,1},{8,14},{9,15},{10,... | collective-permute-start | bytes 393224 | tf_op jit(solution)/shard_map/ppermute | solution.py:240
  61.8 10.9 %collective-permute-start.21 = (bf16[128,512]{1,0:T(8,128)(2,1)S(1)}, bf16[128,512]{1,0:T(8,128)(2,1)S(1)}, u32[]{:S(2)}, u32[]{:S(2)}) collective-permute-start(bf16[128,512]{1,0:T(8,128)(2,1)S(1)} %get-tuple-element.28), channel_id=1, source_target_pairs={{0,7},{1,6},{2,5},{3,4},{4,3},{5,2},{6,1},{7,0},{8,15},{9,14},{10,... | collective-permute-start | bytes 393224 | tf_op jit(solution)/shard_map/ppermute | solution.py:240
  64.0 8.7 %collective-permute-start.15 = (bf16[128,512]{1,0:T(8,128)(2,1)S(1)}, bf16[128,512]{1,0:T(8,128)(2,1)S(1)}, u32[]{:S(2)}, u32[]{:S(2)}) collective-permute-start(bf16[128,512]{1,0:T(8,128)(2,1)S(1)} %get-tuple-element.22), channel_id=1, source_target_pairs={{0,1},{1,0},{2,3},{3,2},{4,5},{5,4},{6,7},{7,6},{8,9},{9,8},{10,11... | collective-permute-start | bytes 393224 | tf_op jit(solution)/shard_map/ppermute | solution.py:240
  70.2 5.3 %collective-permute-start.16 = (bf16[128,512]{1,0:T(8,128)(2,1)S(1)}, bf16[128,512]{1,0:T(8,128)(2,1)S(1)}, u32[]{:S(2)}, u32[]{:S(2)}) collective-permute-start(bf16[128,512]{1,0:T(8,128)(2,1)S(1)} %get-tuple-element.23), channel_id=1, source_target_pairs={{0,2},{1,3},{2,0},{3,1},{4,6},{5,7},{6,4},{7,5},{8,10},{9,11},{10,... | collective-permute-start | bytes 393224 | tf_op jit(solution)/shard_map/ppermute | solution.py:240
  71.9 5.8 %collective-permute-start.17 = (bf16[128,512]{1,0:T(8,128)(2,1)S(1)}, bf16[128,512]{1,0:T(8,128)(2,1)S(1)}, u32[]{:S(2)}, u32[]{:S(2)}) collective-permute-start(bf16[128,512]{1,0:T(8,128)(2,1)S(1)} %get-tuple-element.24), channel_id=1, source_target_pairs={{0,3},{1,2},{2,1},{3,0},{4,7},{5,6},{6,5},{7,4},{8,11},{9,10},{10,... | collective-permute-start | bytes 393224 | tf_op jit(solution)/shard_map/ppermute | solution.py:240

commit v6 on v5

--- a/solution.py
+++ b/solution.py
@@ -93,8 +93,7 @@
         firsts = firsts_ref[pl.ds(slot, 1), :]
         seen = []
         for step in steps:
-            behind = depth - step
-            behind = jnp.where(behind < 0, behind + parts, behind)
+            behind = place_ref[3 + step]
             spot = lax.broadcasted_iota(jnp.int32, (rows, rows), 0)
             corner = base + behind * rows
             here = (spot >= firsts - corner) & (spot <= at - corner)
@@ -247,7 +246,11 @@
     index = lax.axis_index("doc")
     member, group = index % width, index // width
     depth = lax.axis_index("head")
-    place = jnp.stack([depth, member, group]).astype(jnp.int32)
+    fold = [0, *range(1, parts, 2), *reversed(range(2, parts, 2))]
+    ahead = [fold.index(z) for z in range(parts)]
+    origins = [[fold[(ahead[z] - step) % parts] for step in range(parts)] for z in range(parts)]
+    sources = jnp.asarray(origins, jnp.int32)[depth]
+    place = jnp.concatenate([jnp.stack([depth, member, group]).astype(jnp.int32), sources])
     rows = packed_query_rows.shape[0]
     blocks = (group * width + jnp.bitwise_xor(member, jnp.arange(width))) * parts + depth
     spots = blocks[:, None] * rows + jnp.arange(rows)[None, :]
@@ -258,7 +261,7 @@
         size = value.shape[1] // width
         return lax.dynamic_slice_in_dim(value, jnp.bitwise_xor(member, k) * size, size, 1)
 
-    ring = [(i, (i + 1) % parts) for i in range(parts)]
+    ring = [(fold[i], fold[(i + 1) % parts]) for i in range(parts)]
 
     def pair(k):
         return jnp.concatenate([cut(packed_key_rows, k), cut(packed_value_rows, k)], axis=1)
@@ -299,8 +302,7 @@
     near = [piece for piece in late if piece[1] < chunk]
     state = attends(near, 0, everyone, state, False, parts)
     results = {}
-    for turn in reversed(range(HALVES)):
-        slots = list(range(turn * chunk, (turn + 1) * chunk))
+    for slots in (everyone[-2:], everyone[:-2]):
         rest = [piece for piece in late if piece[1] >= chunk]
         outs = attends(rest, 1, slots, state, True, parts)
         for slot, out in zip(slots, outs):

time: 79.4 us -> 74.1 us (0.933)
  waiting for transfers between devices: 34 us -> 23.1 us
  starting transfers between devices: 24.1 us -> 28.3 us
    ppermute x7, waiting for transfers between devices: 18.3 us -> 12.2 us  [move(): return lax.ppermute(piece, 'head', ring)]
    ppermute x7, starting transfers between devices: 6.63 us -> 12.1 us  [move(): return lax.ppermute(piece, 'head', ring)]
    ppermute x15, waiting for transfers between devices: 15.7 us -> 10.9 us  [swap(): return lax.ppermute(block, 'doc', [(i, i ^ k) for i in range(length)])]
    ppermute x15, starting transfers between devices: 17.4 us -> 16.2 us  [swap(): return lax.ppermute(block, 'doc', [(i, i ^ k) for i in range(length)])]
  transfers between devices with their start and end apart: 22 -> 22, of which waited for: 8 -> 9; matrix products, arithmetic and copies ran while one was open for 1% -> 2% of each run, Pallas kernels for 17% -> 20%
where the time goes in v6:
time: 74.1 us; the launch traced here: 73.5 us
  starting transfers between devices  28.3 us (38%)
  waiting for transfers between devices  23.1 us (31%)
  Pallas kernels  18.8 us (25%)
  local copies, waits for them, and re-layouts  2.2 us (3%)
  other arithmetic  0.77 us (1%)
    pallas_call x4, Pallas kernels, attend(): pl.pallas_call(functools.partial(attend_kernel, tuple(((step, first) for...  17.3 us
    ppermute x15, starting transfers between devices, swap(): return lax.ppermute(block, 'doc', [(i, i ^ k) for i in range(length)])  16.2 us
    ppermute x7, waiting for transfers between devices, move(): return lax.ppermute(piece, 'head', ring)  12.2 us
    ppermute x7, starting transfers between devices, move(): return lax.ppermute(piece, 'head', ring)  12.1 us
    ppermute x15, waiting for transfers between devices, swap(): return lax.ppermute(block, 'doc', [(i, i ^ k) for i in range(length)])  10.9 us
    pallas_call x1, Pallas kernels, collect(): pl.pallas_call(collect_kernel, out_shape=jax.ShapeDtypeStruct((rows, coun...  1.57 us
  transfers between devices with their start and end apart: 22, of which 9 were waited for; matrix products, arithmetic and copies ran while one was open for 2% of the time, Pallas kernels for 20%

profile of v6, /device:TPU:0, one launch (start us, length us, event | category | flops | bytes accessed | tf_op | source)
XLA Modules:
  0.0 73.5 jit_solution(5023356217116149168)
XLA Ops:
  0.0 0.0 copy-start
  0.0 1.1 %constant_dynamic-slice_fusion.2 = (bf16[128,128]{1,0:T(8,128)(2,1)S(1)}, bf16[128,128]{1,0:T(8,128)(2,1)S(1)}, bf16[128,128]{1,0:T(8,128)(2,1)S(1)}, bf16[128,1...) fusion(bf16[128,1024]{1,0:T(8,128)(2,1)} %param.7, ...), kind=kLoop, calls=%fused_computation.30 | loop fusion | bytes 1048608 | tf_op jit(solution)/shard_map/dynamic_slice | solution.py:262
  1.2 0.0 copy-start.1
  1.3 0.6 collective-permute-start.3
  1.8 0.0 copy-done
  1.8 0.1 dynamic-slice_bitcast_fusion
  1.9 0.1 pad_maximum_fusion
  2.0 0.2 collective-permute-start
  2.2 0.1 add_bitcast_fusion
  2.3 0.0 copy-done.1
  2.3 0.1 copy.10
  2.4 0.1 reduce
  2.6 0.1 select_reduce_fusion
  2.7 0.1 slice_reduce_fusion.bounds_ref
  2.8 0.2 collective-permute-done.3
  3.0 2.9 %collective-permute-start.11 = (bf16[2,128,256]{2,1,0:T(8,128)(2,1)S(1)}, bf16[2,128,256]{2,1,0:T(8,128)(2,1)S(1)}, u32[]{:S(2)}, u32[]{:S(2)}) collective-permute-start(bf16[2,128,256]{2,1,0:T(8,128)(2,1)S(1)} %pad_maximum_fusion.10), channel_id=1, source_target_pairs={{0,2},{1,3},{2,0},{3,1},{4,6},{5,7},{6,4},{7,5},{8,10},{9,11},{10,... | collective-permute-start | bytes 393224 | tf_op jit(solution)/shard_map/ppermute | solution.py:239
  6.0 1.6 %collective-permute-start.4 = (bf16[2,128,256]{2,1,0:T(8,128)(2,1)S(1)}, bf16[2,128,256]{2,1,0:T(8,128)(2,1)S(1)}, u32[]{:S(2)}, u32[]{:S(2)}) collective-permute-start(bf16[2,128,256]{2,1,0:T(8,128)(2,1)S(1)} %pad_maximum_fusion.7), channel_id=1, source_target_pairs={{0,4},{1,5},{2,6},{3,7},{4,0},{5,1},{6,2},{7,3},{8,12},{9,13},{10,... | collective-permute-start | bytes 393224 | tf_op jit(solution)/shard_map/ppermute | solution.py:239
  7.6 0.1 collective-permute-start.5
  7.7 2.1 %collective-permute-start.10 = (bf16[2,128,256]{2,1,0:T(8,128)(2,1)S(1)}, bf16[2,128,256]{2,1,0:T(8,128)(2,1)S(1)}, u32[]{:S(2)}, u32[]{:S(2)}) collective-permute-start(bf16[2,128,256]{2,1,0:T(8,128)(2,1)S(1)} %pad_maximum_fusion.9.refs_4_), channel_id=1, source_target_pairs={{0,8},{8,24},{24,16},{16,0},{1,9},{9,25},{25,17},{17,1},{2,10},{10... | collective-permute-start | bytes 393224 | tf_op jit(solution)/shard_map/ppermute | solution.py:281
  9.8 4.3 %collective-permute-done.4 = bf16[2,128,256]{2,1,0:T(8,128)(2,1)S(1)} collective-permute-done((bf16[2,128,256]{2,1,0:T(8,128)(2,1)S(1)}, bf16[2,128,256]{2,1,0:T(8,128)(2,1)S(1)}, u32[]{:S(2)}, u32[]{:S(2)}) %collective-permute-start.4) | collective-permute-done | bytes 131104 | tf_op jit(solution)/shard_map/ppermute | solution.py:239
  14.1 0.0 collective-permute-done.5
  14.1 1.6 %collective-permute-start.6 = (bf16[4,128,256]{2,1,0:T(8,128)(2,1)S(1)}, bf16[4,128,256]{2,1,0:T(8,128)(2,1)S(1)}, u32[]{:S(2)}, u32[]{:S(2)}) collective-permute-start(bf16[4,128,256]{2,1,0:T(8,128)(2,1)S(1)} %constant_dynamic-update-slice_fusion.refs_6_), channel_id=1, source_target_pairs={{0,8},{8,24},{24,16},{16,0},{1,9},{9,25},{25,17},{17,1},{2,10},{10... | collective-permute-start | bytes 786440 | tf_op jit(solution)/shard_map/ppermute | solution.py:281
  15.8 0.0 collective-permute-done.11.refs_5_
  15.8 2.6 %collective-permute-start.12 = (bf16[2,128,256]{2,1,0:T(8,128)(2,1)S(1)}, bf16[2,128,256]{2,1,0:T(8,128)(2,1)S(1)}, u32[]{:S(2)}, u32[]{:S(2)}) collective-permute-start(bf16[2,128,256]{2,1,0:T(8,128)(2,1)S(1)} %collective-permute-done.11.refs_5_), channel_id=1, source_target_pairs={{0,8},{8,24},{24,16},{16,0},{1,9},{9,25},{25,17},{17,1},{2,10},{10... | collective-permute-start | bytes 393224 | tf_op jit(solution)/shard_map/ppermute | solution.py:281
  18.4 0.0 collective-permute-done
  18.4 1.6 %collective-permute-start.9 = (bf16[2,128,512]{2,1,0:T(8,128)(2,1)S(1)}, bf16[2,128,512]{2,1,0:T(8,128)(2,1)S(1)}, u32[]{:S(2)}, u32[]{:S(2)}) collective-permute-start(bf16[2,128,512]{2,1,0:T(8,128)(2,1)S(1)} %pad_maximum_fusion.5), channel_id=1, source_target_pairs={{0,6},{1,7},{2,4},{3,5},{4,2},{5,3},{6,0},{7,1},{8,14},{9,15},{10,... | collective-permute-start | bytes 786440 | tf_op jit(solution)/shard_map/ppermute | solution.py:239
  20.0 0.0 collective-permute-done.10.refs_7_
  20.0 4.8 %collective-permute-done.12.refs_8_ = bf16[2,128,256]{2,1,0:T(8,128)(2,1)S(1)} collective-permute-done((bf16[2,128,256]{2,1,0:T(8,128)(2,1)S(1)}, bf16[2,128,256]{2,1,0:T(8,128)(2,1)S(1)}, u32[]{:S(2)}, u32[]{:S(2)}) %collective-permute-start.12) | collective-permute-done | bytes 131104 | tf_op jit(solution)/shard_map/ppermute | solution.py:281
  24.8 0.8 %collective-permute-start.13 = (bf16[4,128,256]{2,1,0:T(8,128)(2,1)S(1)}, bf16[4,128,256]{2,1,0:T(8,128)(2,1)S(1)}, u32[]{:S(2)}, u32[]{:S(2)}) collective-permute-start(bf16[4,128,256]{2,1,0:T(8,128)(2,1)S(1)} %pad_maximum_fusion.6), channel_id=1, source_target_pairs={{0,8},{8,24},{24,16},{16,0},{1,9},{9,25},{25,17},{17,1},{2,10},{10... | collective-permute-start | bytes 786440 | tf_op jit(solution)/shard_map/ppermute | solution.py:281
  25.7 1.9 %collective-permute-start.2 = (bf16[2,128,512]{2,1,0:T(8,128)(2,1)S(1)}, bf16[2,128,512]{2,1,0:T(8,128)(2,1)S(1)}, u32[]{:S(2)}, u32[]{:S(2)}) collective-permute-start(bf16[2,128,512]{2,1,0:T(8,128)(2,1)S(1)} %pad_maximum_fusion.3), channel_id=1, source_target_pairs={{0,4},{1,5},{2,6},{3,7},{4,0},{5,1},{6,2},{7,3},{8,12},{9,13},{10,... | collective-permute-start | bytes 786440 | tf_op jit(solution)/shard_map/ppermute | solution.py:239
  27.6 0.0 collective-permute-done.6.refs_9_
  27.6 3.4 %collective-permute-start.7 = (bf16[4,128,256]{2,1,0:T(8,128)(2,1)S(1)}, bf16[4,128,256]{2,1,0:T(8,128)(2,1)S(1)}, u32[]{:S(2)}, u32[]{:S(2)}) collective-permute-start(bf16[4,128,256]{2,1,0:T(8,128)(2,1)S(1)} %collective-permute-done.6.refs_9_), channel_id=1, source_target_pairs={{0,8},{8,24},{24,16},{16,0},{1,9},{9,25},{25,17},{17,1},{2,10},{10... | collective-permute-start | bytes 786440 | tf_op jit(solution)/shard_map/ppermute | solution.py:281
  31.0 0.5 collective-permute-start.1
  31.5 0.7 fusion
  32.2 2.7 %collective-permute-done.13.refs_4_ = bf16[4,128,256]{2,1,0:T(8,128)(2,1)S(1)} collective-permute-done((bf16[4,128,256]{2,1,0:T(8,128)(2,1)S(1)}, bf16[4,128,256]{2,1,0:T(8,128)(2,1)S(1)}, u32[]{:S(2)}, u32[]{:S(2)}) %collective-permute-start.13) | collective-permute-done | bytes 262176 | tf_op jit(solution)/shard_map/ppermute | solution.py:281
  34.9 0.8 %collective-permute-start.14 = (bf16[4,128,256]{2,1,0:T(8,128)(2,1)S(1)}, bf16[4,128,256]{2,1,0:T(8,128)(2,1)S(1)}, u32[]{:S(2)}, u32[]{:S(2)}) collective-permute-start(bf16[4,128,256]{2,1,0:T(8,128)(2,1)S(1)} %collective-permute-done.13.refs_4_), channel_id=1, source_target_pairs={{0,8},{8,24},{24,16},{16,0},{1,9},{9,25},{25,17},{17,1},{2,10},{10... | collective-permute-start | bytes 786440 | tf_op jit(solution)/shard_map/ppermute | solution.py:281
  35.7 0.1 pad_add_fusion.place_ref
  35.8 4.8 %collective-permute-done.7.refs_3_.refs_1_ = bf16[4,128,256]{2,1,0:T(8,128)(2,1)S(1)} collective-permute-done((bf16[4,128,256]{2,1,0:T(8,128)(2,1)S(1)}, bf16[4,128,256]{2,1,0:T(8,128)(2,1)S(1)}, u32[]{:S(2)}, u32[]{:S(2)}) %collective-permute-start.7) | collective-permute-done | bytes 262176 | tf_op jit(solution)/shard_map/ppermute | solution.py:281
  40.5 0.8 %collective-permute-start.8 = (bf16[4,128,256]{2,1,0:T(8,128)(2,1)S(1)}, bf16[4,128,256]{2,1,0:T(8,128)(2,1)S(1)}, u32[]{:S(2)}, u32[]{:S(2)}) collective-permute-start(bf16[4,128,256]{2,1,0:T(8,128)(2,1)S(1)} %collective-permute-done.7.refs_3_.refs_1_), channel_id=1, source_target_pairs={{0,8},{8,24},{24,16},{16,0},{1,9},{9,25},{25,17},{17,1},{2,10},{10... | collective-permute-start | bytes 786440 | tf_op jit(solution)/shard_map/ppermute | solution.py:281
  41.3 0.0 collective-permute-done.9.refs_3_.refs_0_
  41.4 0.0 collective-permute-done.2.refs_2_
  41.4 0.0 collective-permute-done.1.refs_1_
  41.4 7.3 %shard_map.55 = (f32[8,128,512]{2,1,0:T(8,128)S(1)}, f32[8,8,512]{2,1,0:T(8,128)S(1)}) custom-call(s32[7]{0:T(128)S(1)} %pad_add_fusion.place_ref, s32[8]{0:T(128)S(1)} %slice_reduce_fusion.bounds_ref, s32[8,128]{1,0:T(8,128)S(1)} %bitcast.42, bf16[2,128,512]{2,1,0:T(8,128)(2,1)S(1)} %pad_maximum_fusion.1.refs_0_, ...), custom_call_target="tpu_custom_call" | custom-call | flops 1073741824 | bytes 2097152 | tf_op jit(solution)/shard_map/pallas_call | solution.py:171
  48.7 0.0 collective-permute-done.14.refs_5_
  48.7 5.1 %shard_map.56 = (f32[8,128,512]{2,1,0:T(8,128)S(1)}, f32[8,8,512]{2,1,0:T(8,128)S(1)}) custom-call(s32[7]{0:T(128)S(1)} %pad_add_fusion.place_ref, s32[8]{0:T(128)S(1)} %slice_reduce_fusion.bounds_ref, s32[8,128]{1,0:T(8,128)S(1)} %bitcast.43, bf16[2,128,512]{2,1,0:T(8,128)(2,1)S(1)} %pad_maximum_fusion.1.refs_0_, ...), custom_call_target="tpu_custom_call", output_to_operand_aliasing={{0}: (9, {}), {1}: (10, {})} | custom-call | flops 1073741824 | bytes 2097152 | tf_op jit(solution)/shard_map/pallas_call | solution.py:171
  53.9 0.0 collective-permute-done.8.refs_4_.refs_2_
  53.9 2.5 %shard_map.58 = (bf16[128,512]{1,0:T(8,128)(2,1)S(1)}, bf16[128,512]{1,0:T(8,128)(2,1)S(1)}) custom-call(s32[7]{0:T(128)S(1)} %pad_add_fusion.place_ref, s32[8]{0:T(128)S(1)} %slice_reduce_fusion.bounds_ref, s32[8,128]{1,0:T(8,128)S(1)} %bitcast.44, bf16[2,128,512]{2,1,0:T(8,128)(2,1)S(1)} %collective-permute-done.9.refs_3_.refs_0_, ...), custom_call_target="tpu_custom_call" | custom-call | flops 268435456 | bytes 2097152 | tf_op jit(solution)/shard_map/pallas_call | solution.py:171
  56.4 0.1 collective-permute-start.20
  56.5 0.1 collective-permute-start.21
  56.6 2.3 %shard_map.57 = (bf16[128,512]{1,0:T(8,128)(2,1)S(1)}, bf16[128,512]{1,0:T(8,128)(2,1)S(1)}, bf16[128,512]{1,0:T(8,128)(2,1)S(1)}, bf16[128,512]{1,0:T(8,128)(2,...) custom-call(s32[7]{0:T(128)S(1)} %pad_add_fusion.place_ref, s32[8]{0:T(128)S(1)} %slice_reduce_fusion.bounds_ref, ...), custom_call_target="tpu_custom_call" | custom-call | flops 805306368 | bytes 2097152 | tf_op jit(solution)/shard_map/pallas_call | solution.py:171
  58.8 3.0 %collective-permute-start.15 = (bf16[128,512]{1,0:T(8,128)(2,1)S(1)}, bf16[128,512]{1,0:T(8,128)(2,1)S(1)}, u32[]{:S(2)}, u32[]{:S(2)}) collective-permute-start(bf16[128,512]{1,0:T(8,128)(2,1)S(1)} %get-tuple-element.22), channel_id=1, source_target_pairs={{0,1},{1,0},{2,3},{3,2},{4,5},{5,4},{6,7},{7,6},{8,9},{9,8},{10,11... | collective-permute-start | bytes 393224 | tf_op jit(solution)/shard_map/ppermute | solution.py:239
  61.9 1.8 %collective-permute-start.16 = (bf16[128,512]{1,0:T(8,128)(2,1)S(1)}, bf16[128,512]{1,0:T(8,128)(2,1)S(1)}, u32[]{:S(2)}, u32[]{:S(2)}) collective-permute-start(bf16[128,512]{1,0:T(8,128)(2,1)S(1)} %get-tuple-element.23), channel_id=1, source_target_pairs={{0,2},{1,3},{2,0},{3,1},{4,6},{5,7},{6,4},{7,5},{8,10},{9,11},{10,... | collective-permute-start | bytes 393224 | tf_op jit(solution)/shard_map/ppermute | solution.py:239
  63.6 0.0 collective-permute-start.17
  63.6 0.0 collective-permute-done.20.refs_6_
  63.6 1.5 %collective-permute-start.18 = (bf16[128,512]{1,0:T(8,128)(2,1)S(1)}, bf16[128,512]{1,0:T(8,128)(2,1)S(1)}, u32[]{:S(2)}, u32[]{:S(2)}) collective-permute-start(bf16[128,512]{1,0:T(8,128)(2,1)S(1)} %get-tuple-element.25), channel_id=1, source_target_pairs={{0,4},{1,5},{2,6},{3,7},{4,0},{5,1},{6,2},{7,3},{8,12},{9,13},{10,... | collective-permute-start | bytes 393224 | tf_op jit(solution)/shard_map/ppermute | solution.py:239
  65.2 0.0 collective-permute-done.21.refs_7_
  65.2 0.4 collective-permute-start.19
  65.6 0.0 collective-permute-done.15.refs_1_
  65.6 2.5 %collective-permute-done.16.refs_2_ = bf16[128,512]{1,0:T(8,128)(2,1)S(1)} collective-permute-done((bf16[128,512]{1,0:T(8,128)(2,1)S(1)}, bf16[128,512]{1,0:T(8,128)(2,1)S(1)}, u32[]{:S(2)}, u32[]{:S(2)}) %collective-permute-start.16) | collective-permute-done | bytes 131104 | tf_op jit(solution)/shard_map/ppermute | solution.py:239
  68.1 1.3 %collective-permute-done.17.refs_3_ = bf16[128,512]{1,0:T(8,128)(2,1)S(1)} collective-permute-done((bf16[128,512]{1,0:T(8,128)(2,1)S(1)}, bf16[128,512]{1,0:T(8,128)(2,1)S(1)}, u32[]{:S(2)}, u32[]{:S(2)}) %collective-permute-start.17) | collective-permute-done | bytes 131104 | tf_op jit(solution)/shard_map/ppermute | solution.py:239
  69.4 0.6 collective-permute-done.18.refs_4_
  70.0 1.9 %collective-permute-done.19.refs_5_ = bf16[128,512]{1,0:T(8,128)(2,1)S(1)} collective-permute-done((bf16[128,512]{1,0:T(8,128)(2,1)S(1)}, bf16[128,512]{1,0:T(8,128)(2,1)S(1)}, u32[]{:S(2)}, u32[]{:S(2)}) %collective-permute-start.19) | collective-permute-done | bytes 131104 | tf_op jit(solution)/shard_map/ppermute | solution.py:239
  71.9 1.6 %shard_map.59 = bf16[128,4096]{1,0:T(8,128)(2,1)} custom-call(s32[7]{0:T(128)S(1)} %pad_add_fusion.place_ref, bf16[128,512]{1,0:T(8,128)(2,1)S(1)} %get-tuple-element.21.refs_0_, bf16[128,512]{1,0:T(8,128)(2,1)S(1)} %collective-permute-done.15.refs_1_, bf16[128,512]{1,0:T(8,128)(2,1)S(1)} %collective-permute-done.16.refs_2_, ...), custom_call_target="tpu_custom_call" | custom-call | tf_op jit(solution)/shard_map/pallas_call | solution.py:218
  (24 shorter events, 0.4 us)
Async XLA Ops:
  0.0 1.8 %copy-start = (bf16[128,4096]{1,0:T(8,128)(2,1)S(1)}, bf16[128,4096]{1,0:T(8,128)(2,1)}, u32[]{:S(2)}) copy-start(bf16[128,4096]{1,0:T(8,128)(2,1)} %param.5) | copy-start | bytes 3145732
  1.2 1.2 %copy-start.1 = (s32[16]{0:T(128)S(1)}, s32[16]{0:T(128)}, u32[]{:S(2)}) copy-start(s32[16]{0:T(128)} %param.8) | copy-start | bytes 196
  1.3 1.7 %collective-permute-start.3 = (bf16[4,128,256]{2,1,0:T(8,128)(2,1)S(1)}, bf16[4,128,256]{2,1,0:T(8,128)(2,1)S(1)}, u32[]{:S(2)}, u32[]{:S(2)}) collective-permute-start(bf16[4,128,256]{2,1,0:T(8,128)(2,1)S(1)} %pad_maximum_fusion.4), channel_id=1, source_target_pairs={{0,1},{1,0},{2,3},{3,2},{4,5},{5,4},{6,7},{7,6},{8,9},{9,8},{10,11... | collective-permute-start | bytes 786440 | tf_op jit(solution)/shard_map/ppermute | solution.py:239
  2.0 16.4 %collective-permute-start = (bf16[4,128,512]{2,1,0:T(8,128)(2,1)S(1)}, bf16[4,128,512]{2,1,0:T(8,128)(2,1)S(1)}, u32[]{:S(2)}, u32[]{:S(2)}) collective-permute-start(bf16[4,128,512]{2,1,0:T(8,128)(2,1)S(1)} %pad_maximum_fusion), channel_id=1, source_target_pairs={{0,1},{1,0},{2,3},{3,2},{4,5},{5,4},{6,7},{7,6},{8,9},{9,8},{10,11... | collective-permute-start | bytes 1572872 | tf_op jit(solution)/shard_map/ppermute | solution.py:239
  3.0 12.7 %collective-permute-start.11 = (bf16[2,128,256]{2,1,0:T(8,128)(2,1)S(1)}, bf16[2,128,256]{2,1,0:T(8,128)(2,1)S(1)}, u32[]{:S(2)}, u32[]{:S(2)}) collective-permute-start(bf16[2,128,256]{2,1,0:T(8,128)(2,1)S(1)} %pad_maximum_fusion.10), channel_id=1, source_target_pairs={{0,2},{1,3},{2,0},{3,1},{4,6},{5,7},{6,4},{7,5},{8,10},{9,11},{10,... | collective-permute-start | bytes 393224 | tf_op jit(solution)/shard_map/ppermute | solution.py:239
  6.0 8.1 %collective-permute-start.4 = (bf16[2,128,256]{2,1,0:T(8,128)(2,1)S(1)}, bf16[2,128,256]{2,1,0:T(8,128)(2,1)S(1)}, u32[]{:S(2)}, u32[]{:S(2)}) collective-permute-start(bf16[2,128,256]{2,1,0:T(8,128)(2,1)S(1)} %pad_maximum_fusion.7), channel_id=1, source_target_pairs={{0,4},{1,5},{2,6},{3,7},{4,0},{5,1},{6,2},{7,3},{8,12},{9,13},{10,... | collective-permute-start | bytes 393224 | tf_op jit(solution)/shard_map/ppermute | solution.py:239
  7.6 6.5 %collective-permute-start.5 = (bf16[2,128,256]{2,1,0:T(8,128)(2,1)S(1)}, bf16[2,128,256]{2,1,0:T(8,128)(2,1)S(1)}, u32[]{:S(2)}, u32[]{:S(2)}) collective-permute-start(bf16[2,128,256]{2,1,0:T(8,128)(2,1)S(1)} %pad_maximum_fusion.8), channel_id=1, source_target_pairs={{0,6},{1,7},{2,4},{3,5},{4,2},{5,3},{6,0},{7,1},{8,14},{9,15},{10,... | collective-permute-start | bytes 393224 | tf_op jit(solution)/shard_map/ppermute | solution.py:239
  7.7 12.3 %collective-permute-start.10 = (bf16[2,128,256]{2,1,0:T(8,128)(2,1)S(1)}, bf16[2,128,256]{2,1,0:T(8,128)(2,1)S(1)}, u32[]{:S(2)}, u32[]{:S(2)}) collective-permute-start(bf16[2,128,256]{2,1,0:T(8,128)(2,1)S(1)} %pad_maximum_fusion.9.refs_4_), channel_id=1, source_target_pairs={{0,8},{8,24},{24,16},{16,0},{1,9},{9,25},{25,17},{17,1},{2,10},{10... | collective-permute-start | bytes 393224 | tf_op jit(solution)/shard_map/ppermute | solution.py:281
  14.1 13.5 %collective-permute-start.6 = (bf16[4,128,256]{2,1,0:T(8,128)(2,1)S(1)}, bf16[4,128,256]{2,1,0:T(8,128)(2,1)S(1)}, u32[]{:S(2)}, u32[]{:S(2)}) collective-permute-start(bf16[4,128,256]{2,1,0:T(8,128)(2,1)S(1)} %constant_dynamic-update-slice_fusion.refs_6_), channel_id=1, source_target_pairs={{0,8},{8,24},{24,16},{16,0},{1,9},{9,25},{25,17},{17,1},{2,10},{10... | collective-permute-start | bytes 786440 | tf_op jit(solution)/shard_map/ppermute | solution.py:281
  15.8 9.0 %collective-permute-start.12 = (bf16[2,128,256]{2,1,0:T(8,128)(2,1)S(1)}, bf16[2,128,256]{2,1,0:T(8,128)(2,1)S(1)}, u32[]{:S(2)}, u32[]{:S(2)}) collective-permute-start(bf16[2,128,256]{2,1,0:T(8,128)(2,1)S(1)} %collective-permute-done.11.refs_5_), channel_id=1, source_target_pairs={{0,8},{8,24},{24,16},{16,0},{1,9},{9,25},{25,17},{17,1},{2,10},{10... | collective-permute-start | bytes 393224 | tf_op jit(solution)/shard_map/ppermute | solution.py:281
  18.4 22.9 %collective-permute-start.9 = (bf16[2,128,512]{2,1,0:T(8,128)(2,1)S(1)}, bf16[2,128,512]{2,1,0:T(8,128)(2,1)S(1)}, u32[]{:S(2)}, u32[]{:S(2)}) collective-permute-start(bf16[2,128,512]{2,1,0:T(8,128)(2,1)S(1)} %pad_maximum_fusion.5), channel_id=1, source_target_pairs={{0,6},{1,7},{2,4},{3,5},{4,2},{5,3},{6,0},{7,1},{8,14},{9,15},{10,... | collective-permute-start | bytes 786440 | tf_op jit(solution)/shard_map/ppermute | solution.py:239
  24.8 10.1 %collective-permute-start.13 = (bf16[4,128,256]{2,1,0:T(8,128)(2,1)S(1)}, bf16[4,128,256]{2,1,0:T(8,128)(2,1)S(1)}, u32[]{:S(2)}, u32[]{:S(2)}) collective-permute-start(bf16[4,128,256]{2,1,0:T(8,128)(2,1)S(1)} %pad_maximum_fusion.6), channel_id=1, source_target_pairs={{0,8},{8,24},{24,16},{16,0},{1,9},{9,25},{25,17},{17,1},{2,10},{10... | collective-permute-start | bytes 786440 | tf_op jit(solution)/shard_map/ppermute | solution.py:281
  25.7 15.7 %collective-permute-start.2 = (bf16[2,128,512]{2,1,0:T(8,128)(2,1)S(1)}, bf16[2,128,512]{2,1,0:T(8,128)(2,1)S(1)}, u32[]{:S(2)}, u32[]{:S(2)}) collective-permute-start(bf16[2,128,512]{2,1,0:T(8,128)(2,1)S(1)} %pad_maximum_fusion.3), channel_id=1, source_target_pairs={{0,4},{1,5},{2,6},{3,7},{4,0},{5,1},{6,2},{7,3},{8,12},{9,13},{10,... | collective-permute-start | bytes 786440 | tf_op jit(solution)/shard_map/ppermute | solution.py:239
  27.6 12.9 %collective-permute-start.7 = (bf16[4,128,256]{2,1,0:T(8,128)(2,1)S(1)}, bf16[4,128,256]{2,1,0:T(8,128)(2,1)S(1)}, u32[]{:S(2)}, u32[]{:S(2)}) collective-permute-start(bf16[4,128,256]{2,1,0:T(8,128)(2,1)S(1)} %collective-permute-done.6.refs_9_), channel_id=1, source_target_pairs={{0,8},{8,24},{24,16},{16,0},{1,9},{9,25},{25,17},{17,1},{2,10},{10... | collective-permute-start | bytes 786440 | tf_op jit(solution)/shard_map/ppermute | solution.py:281
  31.0 10.4 %collective-permute-start.1 = (bf16[2,128,512]{2,1,0:T(8,128)(2,1)S(1)}, bf16[2,128,512]{2,1,0:T(8,128)(2,1)S(1)}, u32[]{:S(2)}, u32[]{:S(2)}) collective-permute-start(bf16[2,128,512]{2,1,0:T(8,128)(2,1)S(1)} %pad_maximum_fusion.2), channel_id=1, source_target_pairs={{0,2},{1,3},{2,0},{3,1},{4,6},{5,7},{6,4},{7,5},{8,10},{9,11},{10,... | collective-permute-start | bytes 786440 | tf_op jit(solution)/shard_map/ppermute | solution.py:239
  34.9 13.8 %collective-permute-start.14 = (bf16[4,128,256]{2,1,0:T(8,128)(2,1)S(1)}, bf16[4,128,256]{2,1,0:T(8,128)(2,1)S(1)}, u32[]{:S(2)}, u32[]{:S(2)}) collective-permute-start(bf16[4,128,256]{2,1,0:T(8,128)(2,1)S(1)} %collective-permute-done.13.refs_4_), channel_id=1, source_target_pairs={{0,8},{8,24},{24,16},{16,0},{1,9},{9,25},{25,17},{17,1},{2,10},{10... | collective-permute-start | bytes 786440 | tf_op jit(solution)/shard_map/ppermute | solution.py:281
  40.5 13.3 %collective-permute-start.8 = (bf16[4,128,256]{2,1,0:T(8,128)(2,1)S(1)}, bf16[4,128,256]{2,1,0:T(8,128)(2,1)S(1)}, u32[]{:S(2)}, u32[]{:S(2)}) collective-permute-start(bf16[4,128,256]{2,1,0:T(8,128)(2,1)S(1)} %collective-permute-done.7.refs_3_.refs_1_), channel_id=1, source_target_pairs={{0,8},{8,24},{24,16},{16,0},{1,9},{9,25},{25,17},{17,1},{2,10},{10... | collective-permute-start | bytes 786440 | tf_op jit(solution)/shard_map/ppermute | solution.py:281
  56.4 7.2 %collective-permute-start.20 = (bf16[128,512]{1,0:T(8,128)(2,1)S(1)}, bf16[128,512]{1,0:T(8,128)(2,1)S(1)}, u32[]{:S(2)}, u32[]{:S(2)}) collective-permute-start(bf16[128,512]{1,0:T(8,128)(2,1)S(1)} %get-tuple-element.27), channel_id=1, source_target_pairs={{0,6},{1,7},{2,4},{3,5},{4,2},{5,3},{6,0},{7,1},{8,14},{9,15},{10,... | collective-permute-start | bytes 393224 | tf_op jit(solution)/shard_map/ppermute | solution.py:239
  56.5 8.7 %collective-permute-start.21 = (bf16[128,512]{1,0:T(8,128)(2,1)S(1)}, bf16[128,512]{1,0:T(8,128)(2,1)S(1)}, u32[]{:S(2)}, u32[]{:S(2)}) collective-permute-start(bf16[128,512]{1,0:T(8,128)(2,1)S(1)} %get-tuple-element.28), channel_id=1, source_target_pairs={{0,7},{1,6},{2,5},{3,4},{4,3},{5,2},{6,1},{7,0},{8,15},{9,14},{10,... | collective-permute-start | bytes 393224 | tf_op jit(solution)/shard_map/ppermute | solution.py:239
  58.8 6.7 %collective-permute-start.15 = (bf16[128,512]{1,0:T(8,128)(2,1)S(1)}, bf16[128,512]{1,0:T(8,128)(2,1)S(1)}, u32[]{:S(2)}, u32[]{:S(2)}) collective-permute-start(bf16[128,512]{1,0:T(8,128)(2,1)S(1)} %get-tuple-element.22), channel_id=1, source_target_pairs={{0,1},{1,0},{2,3},{3,2},{4,5},{5,4},{6,7},{7,6},{8,9},{9,8},{10,11... | collective-permute-start | bytes 393224 | tf_op jit(solution)/shard_map/ppermute | solution.py:239
  61.9 6.2 %collective-permute-start.16 = (bf16[128,512]{1,0:T(8,128)(2,1)S(1)}, bf16[128,512]{1,0:T(8,128)(2,1)S(1)}, u32[]{:S(2)}, u32[]{:S(2)}) collective-permute-start(bf16[128,512]{1,0:T(8,128)(2,1)S(1)} %get-tuple-element.23), channel_id=1, source_target_pairs={{0,2},{1,3},{2,0},{3,1},{4,6},{5,7},{6,4},{7,5},{8,10},{9,11},{10,... | collective-permute-start | bytes 393224 | tf_op jit(solution)/shard_map/ppermute | solution.py:239
  63.6 5.8 %collective-permute-start.17 = (bf16[128,512]{1,0:T(8,128)(2,1)S(1)}, bf16[128,512]{1,0:T(8,128)(2,1)S(1)}, u32[]{:S(2)}, u32[]{:S(2)}) collective-permute-start(bf16[128,512]{1,0:T(8,128)(2,1)S(1)} %get-tuple-element.24), channel_id=1, source_target_pairs={{0,3},{1,2},{2,1},{3,0},{4,7},{5,6},{6,5},{7,4},{8,11},{9,10},{10,... | collective-permute-start | bytes 393224 | tf_op jit(solution)/shard_map/ppermute | solution.py:239
  63.6 6.4 %collective-permute-start.18 = (bf16[128,512]{1,0:T(8,128)(2,1)S(1)}, bf16[128,512]{1,0:T(8,128)(2,1)S(1)}, u32[]{:S(2)}, u32[]{:S(2)}) collective-permute-start(bf16[128,512]{1,0:T(8,128)(2,1)S(1)} %get-tuple-element.25), channel_id=1, source_target_pairs={{0,4},{1,5},{2,6},{3,7},{4,0},{5,1},{6,2},{7,3},{8,12},{9,13},{10,... | collective-permute-start | bytes 393224 | tf_op jit(solution)/shard_map/ppermute | solution.py:239
  65.2 6.7 %collective-permute-start.19 = (bf16[128,512]{1,0:T(8,128)(2,1)S(1)}, bf16[128,512]{1,0:T(8,128)(2,1)S(1)}, u32[]{:S(2)}, u32[]{:S(2)}) collective-permute-start(bf16[128,512]{1,0:T(8,128)(2,1)S(1)} %get-tuple-element.26), channel_id=1, source_target_pairs={{0,5},{1,4},{2,7},{3,6},{4,1},{5,0},{6,3},{7,2},{8,13},{9,12},{10,... | collective-permute-start | bytes 393224 | tf_op jit(solution)/shard_map/ppermute | solution.py:239

commit v7 on v6

--- a/solution.py
+++ b/solution.py
@@ -20,16 +20,14 @@
 
 
 def attend_kernel(
-    pieces, half, back, slots, opening, closing, parts, place_ref, bounds_ref, firsts_ref, *refs
+    pieces, half, back, slots, spans, closing, parts, place_ref, bounds_ref, firsts_ref, *refs
 ):
     width = KEY_VALUE_HEADS
     count = len(slots)
     steps = sorted({step for step, _ in pieces})
     q_refs, refs = refs[: count // 2], refs[count // 2 :]
     units, refs = refs[: len(pieces)], refs[len(pieces) :]
-    if not opening:
-        acc_in, stat_in = refs[:2]
-        refs = refs[2:]
+    kept, refs = refs[: 2 * len(spans)], refs[2 * len(spans) :]
     if closing:
         out_refs, refs = refs[:count], refs[count:]
     acc_ref, stat_ref, score_ref, peak_ref, q_ref, kv_ref, list_ref = refs
@@ -68,13 +66,16 @@
     for i in range(count):
         for h in range(heads):
             q_ref[i, h * rows : (h + 1) * rows, :] = q_refs[i // 2][i % 2, :, h * HEAD_SIZE : (h + 1) * HEAD_SIZE]
-    if opening:
+    if not spans:
         acc_ref[...] = jnp.zeros_like(acc_ref)
         stat_ref[:, 0:1, :] = jnp.full((count, 1, lanes), NEGATIVE, jnp.float32)
         stat_ref[:, 1:2, :] = jnp.zeros((count, 1, lanes), jnp.float32)
-    else:
-        acc_ref[...] = acc_in[slots[0] : slots[0] + count]
-        stat_ref[...] = stat_in[slots[0] : slots[0] + count]
+    for i, (first, size) in enumerate(spans):
+        low, high = max(first, slots[0]), min(first + size, slots[0] + count)
+        if low < high:
+            to, source = slice(low - slots[0], high - slots[0]), slice(low - first, high - first)
+            acc_ref[to] = kept[2 * i][source]
+            stat_ref[to] = kept[2 * i + 1][source]
 
     def multiply(i):
         turn, key_doc = list_ref[0, i], list_ref[1, i]
@@ -144,8 +145,8 @@
     lanes = columns // HEAD_SIZE * rows
     vmem = pl.BlockSpec(memory_space=pltpu.VMEM)
     smem = pl.BlockSpec(memory_space=pltpu.SMEM)
-    opening = state is None
-    held = () if opening else state
+    spans = tuple((first, acc.shape[0]) for first, acc, _ in state)
+    held = [part for _, acc, stat in state for part in (acc, stat)]
     count = len(slots)
     tokens = len({step for step, _, _ in pieces}) * rows
     kept = [
@@ -166,7 +167,7 @@
     else:
         out_shape = kept
         first = 3 + count // 2 + len(pieces)
-        aliases = {} if opening else {first: 0, first + 1: 1}
+        aliases = {first: 0, first + 1: 1} if spans == ((slots[0], count),) else {}
     work = count * 2 * tokens * lanes * HEAD_SIZE * 4
     return pl.pallas_call(
         functools.partial(
@@ -175,7 +176,7 @@
             half,
             back,
             tuple(slots),
-            opening,
+            spans,
             closing,
             parts,
         ),
@@ -263,19 +264,20 @@
 
     ring = [(fold[i], fold[(i + 1) % parts]) for i in range(parts)]
 
-    def pair(k):
-        return jnp.concatenate([cut(packed_key_rows, k), cut(packed_value_rows, k)], axis=1)
-
-    def spread(block):
-        given = swap(jnp.stack([block(k) for k in range(1, width, 2)]), 1)
+    def spread(rows):
+        def block(k):
+            return jnp.concatenate([cut(value, k) for value in rows], axis=1)
+
+        given = jnp.stack([block(k) for k in range(1, width, 2)])
+        given = swap(given, 1)
         both = []
         for k in range(0, width, 2):
             both.append(jnp.stack([block(k), given[k // 2]]))
         return [swap(value, 2 * t) for t, value in enumerate(both)]
 
-    pairs = spread(pair)
-    queries = spread(lambda k: cut(packed_query_rows, k))
-    opens = [(0, chunk // 2), (chunk // 2, chunk), (chunk, width)]
+    pairs = spread([packed_key_rows, packed_value_rows])
+    queries = spread([packed_query_rows])
+    opens = [(low, low + 2) for low in range(0, width, 2)]
 
     def move(piece):
         return lax.ppermute(piece, "head", ring)
@@ -284,7 +286,10 @@
     pieces = [(0, low, piece) for low, piece in held]
     held = [(low, move(piece)) for low, piece in held]
     pieces += [(1, low, piece) for low, piece in held]
-    held = [(0, jnp.concatenate([held[0][1], held[1][1]], axis=0)), held[2]]
+    held = [
+        (low, jnp.concatenate([piece for at, piece in held if low <= at < low + chunk]))
+        for low in range(0, width, chunk)
+    ]
     for step in range(2, parts):
         held = [(low, move(piece)) for low, piece in held]
         pieces += [(step, low, piece) for low, piece in held]
@@ -293,14 +298,16 @@
     everyone = list(range(width))
     soon = parts // 2
     first = [piece for piece in pieces if piece[0] < soon]
-    state = attends(first, None, everyone, None, False, parts)
+    state = []
+    for slots in (everyone[:chunk], everyone[chunk:]):
+        state.append((slots[0], *attends(first, None, slots, [], False, parts)))
     late = [piece for piece in pieces if piece[0] >= soon]
     if docs > width:
         over = [(i, i + width) for i in range(docs - width)]
         far = [(step, low, lax.ppermute(piece, "doc", over)) for step, low, piece in pieces]
-        state = attends(far, None, everyone, state, False, parts, back=1)
+        state = [(0, *attends(far, None, everyone, state, False, parts, back=1))]
     near = [piece for piece in late if piece[1] < chunk]
-    state = attends(near, 0, everyone, state, False, parts)
+    state = [(0, *attends(near, 0, everyone, state, False, parts))]
     results = {}
     for slots in (everyone[-2:], everyone[:-2]):
         rest = [piece for piece in late if piece[1] >= chunk]

time: 74.1 us -> 69.7 us (0.941)
  waiting for transfers between devices: 23.1 us -> 16.6 us
  starting transfers between devices: 28.3 us -> 29.8 us
  Pallas kernels: 18.8 us -> 19.6 us
    ppermute x7 -> x8, waiting for transfers between devices: 12.2 us -> 8.84 us  [move(): return lax.ppermute(piece, 'head', ring)]
    ppermute x15, waiting for transfers between devices: 10.9 us -> 7.78 us  [swap(): return lax.ppermute(block, 'doc', [(i, i ^ k) for i in range(length)])]
    ppermute x7 -> x8, starting transfers between devices: 12.1 us -> 13.3 us  [move(): return lax.ppermute(piece, 'head', ring)]
    pallas_call x4 -> x5, Pallas kernels: 17.3 us -> 18 us  [attend(): pl.pallas_call(functools.partial(attend_kernel, tuple(((step, first) for...]
  transfers between devices with their start and end apart: 22 -> 23, of which waited for: 9 -> 11; matrix products, arithmetic and copies ran while one was open for 2% -> 3% of each run, Pallas kernels for 20% -> 22%
where the time goes in v7:
time: 69.7 us; the launch traced here: 69.2 us
  starting transfers between devices  29.8 us (43%)
  Pallas kernels  19.6 us (28%)
  waiting for transfers between devices  16.6 us (24%)
  local copies, waits for them, and re-layouts  2.19 us (3%)
  other arithmetic  0.8 us (1%)
    pallas_call x5, Pallas kernels, attend(): pl.pallas_call(functools.partial(attend_kernel, tuple(((step, first) for...  18 us
    ppermute x15, starting transfers between devices, swap(): return lax.ppermute(block, 'doc', [(i, i ^ k) for i in range(length)])  16.5 us
    ppermute x8, starting transfers between devices, move(): return lax.ppermute(piece, 'head', ring)  13.3 us
    ppermute x8, waiting for transfers between devices, move(): return lax.ppermute(piece, 'head', ring)  8.84 us
    ppermute x15, waiting for transfers between devices, swap(): return lax.ppermute(block, 'doc', [(i, i ^ k) for i in range(length)])  7.78 us
    pallas_call x1, Pallas kernels, collect(): pl.pallas_call(collect_kernel, out_shape=jax.ShapeDtypeStruct((rows, coun...  1.57 us
  transfers between devices with their start and end apart: 23, of which 11 were waited for; matrix products, arithmetic and copies ran while one was open for 3% of the time, Pallas kernels for 22%

profile of v7, /device:TPU:0, one launch (start us, length us, event | category | flops | bytes accessed | tf_op | source)
XLA Modules:
  0.0 69.2 jit_solution(15821448397921810130)
XLA Ops:
  0.0 1.1 %constant_dynamic-slice_fusion.2 = (bf16[128,128]{1,0:T(8,128)(2,1)S(1)}, bf16[128,128]{1,0:T(8,128)(2,1)S(1)}, bf16[128,128]{1,0:T(8,128)(2,1)S(1)}, bf16[128,1...) fusion(bf16[128,1024]{1,0:T(8,128)(2,1)} %param.7, ...), kind=kLoop, calls=%fused_computation.31 | loop fusion | bytes 1048608 | tf_op jit(solution)/shard_map/dynamic_slice | solution.py:263
  1.2 0.0 copy-start.1
  1.3 0.6 collective-permute-start.3
  1.8 0.0 copy-done
  1.8 0.1 dynamic-slice_bitcast_fusion
  1.9 0.1 pad_maximum_fusion
  2.0 0.2 collective-permute-start
  2.2 0.1 add_bitcast_fusion
  2.3 0.1 copy.8
  2.4 0.1 reduce
  2.6 0.1 select_reduce_fusion
  2.7 0.1 slice_reduce_fusion.bounds_ref
  2.8 0.2 collective-permute-done.3
  3.0 2.9 %collective-permute-start.12 = (bf16[2,128,256]{2,1,0:T(8,128)(2,1)S(1)}, bf16[2,128,256]{2,1,0:T(8,128)(2,1)S(1)}, u32[]{:S(2)}, u32[]{:S(2)}) collective-permute-start(bf16[2,128,256]{2,1,0:T(8,128)(2,1)S(1)} %pad_maximum_fusion.11), channel_id=1, source_target_pairs={{0,2},{1,3},{2,0},{3,1},{4,6},{5,7},{6,4},{7,5},{8,10},{9,11},{10,... | collective-permute-start | bytes 393224 | tf_op jit(solution)/shard_map/ppermute | solution.py:240
  6.0 1.6 %collective-permute-start.4 = (bf16[2,128,256]{2,1,0:T(8,128)(2,1)S(1)}, bf16[2,128,256]{2,1,0:T(8,128)(2,1)S(1)}, u32[]{:S(2)}, u32[]{:S(2)}) collective-permute-start(bf16[2,128,256]{2,1,0:T(8,128)(2,1)S(1)} %pad_maximum_fusion.8), channel_id=1, source_target_pairs={{0,4},{1,5},{2,6},{3,7},{4,0},{5,1},{6,2},{7,3},{8,12},{9,13},{10,... | collective-permute-start | bytes 393224 | tf_op jit(solution)/shard_map/ppermute | solution.py:240
  7.6 0.1 collective-permute-start.6
  7.6 0.7 %fusion = s32[4]{0:T(128)S(1)} fusion(s32[4,4]{1,0:T(4,128)} %constant.61.clone, s32[]{:T(128)S(6)} %select_n.76), kind=kLoop, calls=%fused_computation.48 | loop fusion | bytes 36 | tf_op jit(solution)/shard_map/squeeze | solution.py:253
  8.4 2.1 %collective-permute-start.11 = (bf16[2,128,256]{2,1,0:T(8,128)(2,1)S(1)}, bf16[2,128,256]{2,1,0:T(8,128)(2,1)S(1)}, u32[]{:S(2)}, u32[]{:S(2)}) collective-permute-start(bf16[2,128,256]{2,1,0:T(8,128)(2,1)S(1)} %pad_maximum_fusion.10.refs_2_), channel_id=1, source_target_pairs={{0,8},{8,24},{24,16},{16,0},{1,9},{9,25},{25,17},{17,1},{2,10},{10... | collective-permute-start | bytes 393224 | tf_op jit(solution)/shard_map/ppermute | solution.py:283
  10.4 0.0 collective-permute-done.12.refs_3_
  10.4 2.6 %collective-permute-start.13 = (bf16[2,128,256]{2,1,0:T(8,128)(2,1)S(1)}, bf16[2,128,256]{2,1,0:T(8,128)(2,1)S(1)}, u32[]{:S(2)}, u32[]{:S(2)}) collective-permute-start(bf16[2,128,256]{2,1,0:T(8,128)(2,1)S(1)} %collective-permute-done.12.refs_3_), channel_id=1, source_target_pairs={{0,8},{8,24},{24,16},{16,0},{1,9},{9,25},{25,17},{17,1},{2,10},{10... | collective-permute-start | bytes 393224 | tf_op jit(solution)/shard_map/ppermute | solution.py:283
  13.0 1.1 %collective-permute-done.4.refs_4_ = bf16[2,128,256]{2,1,0:T(8,128)(2,1)S(1)} collective-permute-done((bf16[2,128,256]{2,1,0:T(8,128)(2,1)S(1)}, bf16[2,128,256]{2,1,0:T(8,128)(2,1)S(1)}, u32[]{:S(2)}, u32[]{:S(2)}) %collective-permute-start.4) | collective-permute-done | bytes 131104 | tf_op jit(solution)/shard_map/ppermute | solution.py:240
  14.1 1.6 %collective-permute-start.5 = (bf16[2,128,256]{2,1,0:T(8,128)(2,1)S(1)}, bf16[2,128,256]{2,1,0:T(8,128)(2,1)S(1)}, u32[]{:S(2)}, u32[]{:S(2)}) collective-permute-start(bf16[2,128,256]{2,1,0:T(8,128)(2,1)S(1)} %collective-permute-done.4.refs_4_), channel_id=1, source_target_pairs={{0,8},{8,24},{24,16},{16,0},{1,9},{9,25},{25,17},{17,1},{2,10},{10... | collective-permute-start | bytes 393224 | tf_op jit(solution)/shard_map/ppermute | solution.py:283
  15.7 0.0 collective-permute-done.6.refs_5_
  15.7 2.6 %collective-permute-start.7 = (bf16[2,128,256]{2,1,0:T(8,128)(2,1)S(1)}, bf16[2,128,256]{2,1,0:T(8,128)(2,1)S(1)}, u32[]{:S(2)}, u32[]{:S(2)}) collective-permute-start(bf16[2,128,256]{2,1,0:T(8,128)(2,1)S(1)} %collective-permute-done.6.refs_5_), channel_id=1, source_target_pairs={{0,8},{8,24},{24,16},{16,0},{1,9},{9,25},{25,17},{17,1},{2,10},{10... | collective-permute-start | bytes 393224 | tf_op jit(solution)/shard_map/ppermute | solution.py:283
  18.3 0.0 collective-permute-done
  18.3 1.6 %collective-permute-start.10 = (bf16[2,128,512]{2,1,0:T(8,128)(2,1)S(1)}, bf16[2,128,512]{2,1,0:T(8,128)(2,1)S(1)}, u32[]{:S(2)}, u32[]{:S(2)}) collective-permute-start(bf16[2,128,512]{2,1,0:T(8,128)(2,1)S(1)} %pad_maximum_fusion.6), channel_id=1, source_target_pairs={{0,6},{1,7},{2,4},{3,5},{4,2},{5,3},{6,0},{7,1},{8,14},{9,15},{10,... | collective-permute-start | bytes 786440 | tf_op jit(solution)/shard_map/ppermute | solution.py:240
  19.9 0.0 collective-permute-done.11.refs_6_
  19.9 0.0 collective-permute-done.13.refs_7_
  19.9 0.5 collective-permute-start.14
  20.4 1.0 %collective-permute-done.5.refs_8_ = bf16[2,128,256]{2,1,0:T(8,128)(2,1)S(1)} collective-permute-done((bf16[2,128,256]{2,1,0:T(8,128)(2,1)S(1)}, bf16[2,128,256]{2,1,0:T(8,128)(2,1)S(1)}, u32[]{:S(2)}, u32[]{:S(2)}) %collective-permute-start.5) | collective-permute-done | bytes 131104 | tf_op jit(solution)/shard_map/ppermute | solution.py:283
  21.4 2.8 %collective-permute-done.7.refs_9_ = bf16[2,128,256]{2,1,0:T(8,128)(2,1)S(1)} collective-permute-done((bf16[2,128,256]{2,1,0:T(8,128)(2,1)S(1)}, bf16[2,128,256]{2,1,0:T(8,128)(2,1)S(1)}, u32[]{:S(2)}, u32[]{:S(2)}) %collective-permute-start.7) | collective-permute-done | bytes 131104 | tf_op jit(solution)/shard_map/ppermute | solution.py:283
  24.3 1.2 %collective-permute-start.8 = (bf16[4,128,256]{2,1,0:T(8,128)(2,1)S(1)}, bf16[4,128,256]{2,1,0:T(8,128)(2,1)S(1)}, u32[]{:S(2)}, u32[]{:S(2)}) collective-permute-start(bf16[4,128,256]{2,1,0:T(8,128)(2,1)S(1)} %pad_maximum_fusion.5), channel_id=1, source_target_pairs={{0,8},{8,24},{24,16},{16,0},{1,9},{9,25},{25,17},{17,1},{2,10},{10... | collective-permute-start | bytes 786440 | tf_op jit(solution)/shard_map/ppermute | solution.py:283
  25.5 1.2 %collective-permute-start.2 = (bf16[2,128,512]{2,1,0:T(8,128)(2,1)S(1)}, bf16[2,128,512]{2,1,0:T(8,128)(2,1)S(1)}, u32[]{:S(2)}, u32[]{:S(2)}) collective-permute-start(bf16[2,128,512]{2,1,0:T(8,128)(2,1)S(1)} %pad_maximum_fusion.3), channel_id=1, source_target_pairs={{0,4},{1,5},{2,6},{3,7},{4,0},{5,1},{6,2},{7,3},{8,12},{9,13},{10,... | collective-permute-start | bytes 786440 | tf_op jit(solution)/shard_map/ppermute | solution.py:240
  26.7 1.9 %collective-permute-start.1 = (bf16[2,128,512]{2,1,0:T(8,128)(2,1)S(1)}, bf16[2,128,512]{2,1,0:T(8,128)(2,1)S(1)}, u32[]{:S(2)}, u32[]{:S(2)}) collective-permute-start(bf16[2,128,512]{2,1,0:T(8,128)(2,1)S(1)} %pad_maximum_fusion.2), channel_id=1, source_target_pairs={{0,2},{1,3},{2,0},{3,1},{4,6},{5,7},{6,4},{7,5},{8,10},{9,11},{10,... | collective-permute-start | bytes 786440 | tf_op jit(solution)/shard_map/ppermute | solution.py:240
  28.6 1.4 %collective-permute-done.14.refs_4_ = bf16[4,128,256]{2,1,0:T(8,128)(2,1)S(1)} collective-permute-done((bf16[4,128,256]{2,1,0:T(8,128)(2,1)S(1)}, bf16[4,128,256]{2,1,0:T(8,128)(2,1)S(1)}, u32[]{:S(2)}, u32[]{:S(2)}) %collective-permute-start.14) | collective-permute-done | bytes 262176 | tf_op jit(solution)/shard_map/ppermute | solution.py:283
  30.1 1.9 %collective-permute-start.15 = (bf16[4,128,256]{2,1,0:T(8,128)(2,1)S(1)}, bf16[4,128,256]{2,1,0:T(8,128)(2,1)S(1)}, u32[]{:S(2)}, u32[]{:S(2)}) collective-permute-start(bf16[4,128,256]{2,1,0:T(8,128)(2,1)S(1)} %collective-permute-done.14.refs_4_), channel_id=1, source_target_pairs={{0,8},{8,24},{24,16},{16,0},{1,9},{9,25},{25,17},{17,1},{2,10},{10... | collective-permute-start | bytes 786440 | tf_op jit(solution)/shard_map/ppermute | solution.py:283
  32.0 0.1 pad_add_fusion.place_ref
  32.1 3.6 %collective-permute-done.8.refs_3_.refs_1_ = bf16[4,128,256]{2,1,0:T(8,128)(2,1)S(1)} collective-permute-done((bf16[4,128,256]{2,1,0:T(8,128)(2,1)S(1)}, bf16[4,128,256]{2,1,0:T(8,128)(2,1)S(1)}, u32[]{:S(2)}, u32[]{:S(2)}) %collective-permute-start.8) | collective-permute-done | bytes 262176 | tf_op jit(solution)/shard_map/ppermute | solution.py:283
  35.7 0.9 %collective-permute-start.9 = (bf16[4,128,256]{2,1,0:T(8,128)(2,1)S(1)}, bf16[4,128,256]{2,1,0:T(8,128)(2,1)S(1)}, u32[]{:S(2)}, u32[]{:S(2)}) collective-permute-start(bf16[4,128,256]{2,1,0:T(8,128)(2,1)S(1)} %collective-permute-done.8.refs_3_.refs_1_), channel_id=1, source_target_pairs={{0,8},{8,24},{24,16},{16,0},{1,9},{9,25},{25,17},{17,1},{2,10},{10... | collective-permute-start | bytes 786440 | tf_op jit(solution)/shard_map/ppermute | solution.py:283
  36.6 0.0 collective-permute-done.10.refs_1_.refs_3_.refs_0_
  36.6 0.0 collective-permute-done.2.refs_0_.refs_2_
  36.6 5.1 %shard_map.56 = (f32[4,128,512]{2,1,0:T(8,128)S(1)}, f32[4,8,512]{2,1,0:T(8,128)S(1)}) custom-call(s32[7]{0:T(128)S(1)} %pad_add_fusion.place_ref, s32[8]{0:T(128)S(1)} %slice_reduce_fusion.bounds_ref, s32[8,128]{1,0:T(8,128)S(1)} %bitcast.42, bf16[2,128,512]{2,1,0:T(8,128)(2,1)S(1)} %collective-permute-done.2.refs_0_.refs_2_, ...), custom_call_target="tpu_custom_call" | custom-call | flops 536870912 | bytes 2097152 | tf_op jit(solution)/shard_map/pallas_call | solution.py:172
  41.8 0.0 collective-permute-done.1.refs_1_
  41.8 3.1 %shard_map.55 = (f32[4,128,512]{2,1,0:T(8,128)S(1)}, f32[4,8,512]{2,1,0:T(8,128)S(1)}) custom-call(s32[7]{0:T(128)S(1)} %pad_add_fusion.place_ref, s32[8]{0:T(128)S(1)} %slice_reduce_fusion.bounds_ref, s32[8,128]{1,0:T(8,128)S(1)} %bitcast.43, bf16[2,128,512]{2,1,0:T(8,128)(2,1)S(1)} %pad_maximum_fusion.1.refs_0_, ...), custom_call_target="tpu_custom_call" | custom-call | flops 536870912 | bytes 2097152 | tf_op jit(solution)/shard_map/pallas_call | solution.py:172
  44.9 0.0 collective-permute-done.15.refs_5_
  44.9 5.0 %shard_map.57 = (f32[8,128,512]{2,1,0:T(8,128)S(1)}, f32[8,8,512]{2,1,0:T(8,128)S(1)}) custom-call(s32[7]{0:T(128)S(1)} %pad_add_fusion.place_ref, s32[8]{0:T(128)S(1)} %slice_reduce_fusion.bounds_ref, s32[8,128]{1,0:T(8,128)S(1)} %bitcast.44, bf16[2,128,512]{2,1,0:T(8,128)(2,1)S(1)} %pad_maximum_fusion.1.refs_0_, ...), custom_call_target="tpu_custom_call" | custom-call | flops 1073741824 | bytes 2097152 | tf_op jit(solution)/shard_map/pallas_call | solution.py:172
  49.9 0.0 collective-permute-done.9.refs_4_.refs_2_
  49.9 2.5 %shard_map.59 = (bf16[128,512]{1,0:T(8,128)(2,1)S(1)}, bf16[128,512]{1,0:T(8,128)(2,1)S(1)}) custom-call(s32[7]{0:T(128)S(1)} %pad_add_fusion.place_ref, s32[8]{0:T(128)S(1)} %slice_reduce_fusion.bounds_ref, s32[8,128]{1,0:T(8,128)S(1)} %bitcast.45, bf16[2,128,512]{2,1,0:T(8,128)(2,1)S(1)} %collective-permute-done.10.refs_1_.refs_3_.refs_0_, ...), custom_call_target="tpu_custom_call" | custom-call | flops 268435456 | bytes 2097152 | tf_op jit(solution)/shard_map/pallas_call | solution.py:172
  52.4 0.5 collective-permute-start.21
  52.9 0.0 collective-permute-start.22
  52.9 2.3 %shard_map.58 = (bf16[128,512]{1,0:T(8,128)(2,1)S(1)}, bf16[128,512]{1,0:T(8,128)(2,1)S(1)}, bf16[128,512]{1,0:T(8,128)(2,1)S(1)}, bf16[128,512]{1,0:T(8,128)(2,...) custom-call(s32[7]{0:T(128)S(1)} %pad_add_fusion.place_ref, s32[8]{0:T(128)S(1)} %slice_reduce_fusion.bounds_ref, ...), custom_call_target="tpu_custom_call" | custom-call | flops 805306368 | bytes 2097152 | tf_op jit(solution)/shard_map/pallas_call | solution.py:172
  55.2 2.7 %collective-permute-start.16 = (bf16[128,512]{1,0:T(8,128)(2,1)S(1)}, bf16[128,512]{1,0:T(8,128)(2,1)S(1)}, u32[]{:S(2)}, u32[]{:S(2)}) collective-permute-start(bf16[128,512]{1,0:T(8,128)(2,1)S(1)} %get-tuple-element.26), channel_id=1, source_target_pairs={{0,1},{1,0},{2,3},{3,2},{4,5},{5,4},{6,7},{7,6},{8,9},{9,8},{10,11... | collective-permute-start | bytes 393224 | tf_op jit(solution)/shard_map/ppermute | solution.py:240
  57.9 1.5 %collective-permute-start.17 = (bf16[128,512]{1,0:T(8,128)(2,1)S(1)}, bf16[128,512]{1,0:T(8,128)(2,1)S(1)}, u32[]{:S(2)}, u32[]{:S(2)}) collective-permute-start(bf16[128,512]{1,0:T(8,128)(2,1)S(1)} %get-tuple-element.27), channel_id=1, source_target_pairs={{0,2},{1,3},{2,0},{3,1},{4,6},{5,7},{6,4},{7,5},{8,10},{9,11},{10,... | collective-permute-start | bytes 393224 | tf_op jit(solution)/shard_map/ppermute | solution.py:240
  59.4 0.0 collective-permute-start.18
  59.4 0.2 collective-permute-done.21.refs_6_
  59.6 1.3 %collective-permute-start.19 = (bf16[128,512]{1,0:T(8,128)(2,1)S(1)}, bf16[128,512]{1,0:T(8,128)(2,1)S(1)}, u32[]{:S(2)}, u32[]{:S(2)}) collective-permute-start(bf16[128,512]{1,0:T(8,128)(2,1)S(1)} %get-tuple-element.29), channel_id=1, source_target_pairs={{0,4},{1,5},{2,6},{3,7},{4,0},{5,1},{6,2},{7,3},{8,12},{9,13},{10,... | collective-permute-start | bytes 393224 | tf_op jit(solution)/shard_map/ppermute | solution.py:240
  60.9 0.0 collective-permute-done.22.refs_7_
  60.9 0.5 collective-permute-start.20
  61.4 0.0 collective-permute-done.16.refs_1_
  61.4 2.9 %collective-permute-done.17.refs_2_ = bf16[128,512]{1,0:T(8,128)(2,1)S(1)} collective-permute-done((bf16[128,512]{1,0:T(8,128)(2,1)S(1)}, bf16[128,512]{1,0:T(8,128)(2,1)S(1)}, u32[]{:S(2)}, u32[]{:S(2)}) %collective-permute-start.17) | collective-permute-done | bytes 131104 | tf_op jit(solution)/shard_map/ppermute | solution.py:240
  64.2 1.0 %collective-permute-done.18.refs_3_ = bf16[128,512]{1,0:T(8,128)(2,1)S(1)} collective-permute-done((bf16[128,512]{1,0:T(8,128)(2,1)S(1)}, bf16[128,512]{1,0:T(8,128)(2,1)S(1)}, u32[]{:S(2)}, u32[]{:S(2)}) %collective-permute-start.18) | collective-permute-done | bytes 131104 | tf_op jit(solution)/shard_map/ppermute | solution.py:240
  65.3 0.7 %collective-permute-done.19.refs_4_ = bf16[128,512]{1,0:T(8,128)(2,1)S(1)} collective-permute-done((bf16[128,512]{1,0:T(8,128)(2,1)S(1)}, bf16[128,512]{1,0:T(8,128)(2,1)S(1)}, u32[]{:S(2)}, u32[]{:S(2)}) %collective-permute-start.19) | collective-permute-done | bytes 131104 | tf_op jit(solution)/shard_map/ppermute | solution.py:240
  66.0 1.7 %collective-permute-done.20.refs_5_ = bf16[128,512]{1,0:T(8,128)(2,1)S(1)} collective-permute-done((bf16[128,512]{1,0:T(8,128)(2,1)S(1)}, bf16[128,512]{1,0:T(8,128)(2,1)S(1)}, u32[]{:S(2)}, u32[]{:S(2)}) %collective-permute-start.20) | collective-permute-done | bytes 131104 | tf_op jit(solution)/shard_map/ppermute | solution.py:240
  67.7 1.6 %shard_map.60 = bf16[128,4096]{1,0:T(8,128)(2,1)} custom-call(s32[7]{0:T(128)S(1)} %pad_add_fusion.place_ref, bf16[128,512]{1,0:T(8,128)(2,1)S(1)} %get-tuple-element.25.refs_0_, bf16[128,512]{1,0:T(8,128)(2,1)S(1)} %collective-permute-done.16.refs_1_, bf16[128,512]{1,0:T(8,128)(2,1)S(1)} %collective-permute-done.17.refs_2_, ...), custom_call_target="tpu_custom_call" | custom-call | tf_op jit(solution)/shard_map/pallas_call | solution.py:219
  (25 shorter events, 0.4 us)
Async XLA Ops:
  0.0 1.8 %copy-start = (bf16[128,4096]{1,0:T(8,128)(2,1)S(1)}, bf16[128,4096]{1,0:T(8,128)(2,1)}, u32[]{:S(2)}) copy-start(bf16[128,4096]{1,0:T(8,128)(2,1)} %param.5) | copy-start | bytes 3145732
  1.2 1.2 %copy-start.1 = (s32[16]{0:T(128)S(1)}, s32[16]{0:T(128)}, u32[]{:S(2)}) copy-start(s32[16]{0:T(128)} %param.8) | copy-start | bytes 196
  1.3 1.7 %collective-permute-start.3 = (bf16[4,128,256]{2,1,0:T(8,128)(2,1)S(1)}, bf16[4,128,256]{2,1,0:T(8,128)(2,1)S(1)}, u32[]{:S(2)}, u32[]{:S(2)}) collective-permute-start(bf16[4,128,256]{2,1,0:T(8,128)(2,1)S(1)} %pad_maximum_fusion.4), channel_id=1, source_target_pairs={{0,1},{1,0},{2,3},{3,2},{4,5},{5,4},{6,7},{7,6},{8,9},{9,8},{10,11... | collective-permute-start | bytes 786440 | tf_op jit(solution)/shard_map/ppermute | solution.py:240
  2.0 16.3 %collective-permute-start = (bf16[4,128,512]{2,1,0:T(8,128)(2,1)S(1)}, bf16[4,128,512]{2,1,0:T(8,128)(2,1)S(1)}, u32[]{:S(2)}, u32[]{:S(2)}) collective-permute-start(bf16[4,128,512]{2,1,0:T(8,128)(2,1)S(1)} %pad_maximum_fusion), channel_id=1, source_target_pairs={{0,1},{1,0},{2,3},{3,2},{4,5},{5,4},{6,7},{7,6},{8,9},{9,8},{10,11... | collective-permute-start | bytes 1572872 | tf_op jit(solution)/shard_map/ppermute | solution.py:240
  3.0 7.4 %collective-permute-start.12 = (bf16[2,128,256]{2,1,0:T(8,128)(2,1)S(1)}, bf16[2,128,256]{2,1,0:T(8,128)(2,1)S(1)}, u32[]{:S(2)}, u32[]{:S(2)}) collective-permute-start(bf16[2,128,256]{2,1,0:T(8,128)(2,1)S(1)} %pad_maximum_fusion.11), channel_id=1, source_target_pairs={{0,2},{1,3},{2,0},{3,1},{4,6},{5,7},{6,4},{7,5},{8,10},{9,11},{10,... | collective-permute-start | bytes 393224 | tf_op jit(solution)/shard_map/ppermute | solution.py:240
  6.0 8.1 %collective-permute-start.4 = (bf16[2,128,256]{2,1,0:T(8,128)(2,1)S(1)}, bf16[2,128,256]{2,1,0:T(8,128)(2,1)S(1)}, u32[]{:S(2)}, u32[]{:S(2)}) collective-permute-start(bf16[2,128,256]{2,1,0:T(8,128)(2,1)S(1)} %pad_maximum_fusion.8), channel_id=1, source_target_pairs={{0,4},{1,5},{2,6},{3,7},{4,0},{5,1},{6,2},{7,3},{8,12},{9,13},{10,... | collective-permute-start | bytes 393224 | tf_op jit(solution)/shard_map/ppermute | solution.py:240
  7.6 8.1 %collective-permute-start.6 = (bf16[2,128,256]{2,1,0:T(8,128)(2,1)S(1)}, bf16[2,128,256]{2,1,0:T(8,128)(2,1)S(1)}, u32[]{:S(2)}, u32[]{:S(2)}) collective-permute-start(bf16[2,128,256]{2,1,0:T(8,128)(2,1)S(1)} %pad_maximum_fusion.9), channel_id=1, source_target_pairs={{0,6},{1,7},{2,4},{3,5},{4,2},{5,3},{6,0},{7,1},{8,14},{9,15},{10,... | collective-permute-start | bytes 393224 | tf_op jit(solution)/shard_map/ppermute | solution.py:240
  8.4 11.5 %collective-permute-start.11 = (bf16[2,128,256]{2,1,0:T(8,128)(2,1)S(1)}, bf16[2,128,256]{2,1,0:T(8,128)(2,1)S(1)}, u32[]{:S(2)}, u32[]{:S(2)}) collective-permute-start(bf16[2,128,256]{2,1,0:T(8,128)(2,1)S(1)} %pad_maximum_fusion.10.refs_2_), channel_id=1, source_target_pairs={{0,8},{8,24},{24,16},{16,0},{1,9},{9,25},{25,17},{17,1},{2,10},{10... | collective-permute-start | bytes 393224 | tf_op jit(solution)/shard_map/ppermute | solution.py:283
  10.4 9.5 %collective-permute-start.13 = (bf16[2,128,256]{2,1,0:T(8,128)(2,1)S(1)}, bf16[2,128,256]{2,1,0:T(8,128)(2,1)S(1)}, u32[]{:S(2)}, u32[]{:S(2)}) collective-permute-start(bf16[2,128,256]{2,1,0:T(8,128)(2,1)S(1)} %collective-permute-done.12.refs_3_), channel_id=1, source_target_pairs={{0,8},{8,24},{24,16},{16,0},{1,9},{9,25},{25,17},{17,1},{2,10},{10... | collective-permute-start | bytes 393224 | tf_op jit(solution)/shard_map/ppermute | solution.py:283
  14.1 7.3 %collective-permute-start.5 = (bf16[2,128,256]{2,1,0:T(8,128)(2,1)S(1)}, bf16[2,128,256]{2,1,0:T(8,128)(2,1)S(1)}, u32[]{:S(2)}, u32[]{:S(2)}) collective-permute-start(bf16[2,128,256]{2,1,0:T(8,128)(2,1)S(1)} %collective-permute-done.4.refs_4_), channel_id=1, source_target_pairs={{0,8},{8,24},{24,16},{16,0},{1,9},{9,25},{25,17},{17,1},{2,10},{10... | collective-permute-start | bytes 393224 | tf_op jit(solution)/shard_map/ppermute | solution.py:283
  15.7 8.6 %collective-permute-start.7 = (bf16[2,128,256]{2,1,0:T(8,128)(2,1)S(1)}, bf16[2,128,256]{2,1,0:T(8,128)(2,1)S(1)}, u32[]{:S(2)}, u32[]{:S(2)}) collective-permute-start(bf16[2,128,256]{2,1,0:T(8,128)(2,1)S(1)} %collective-permute-done.6.refs_5_), channel_id=1, source_target_pairs={{0,8},{8,24},{24,16},{16,0},{1,9},{9,25},{25,17},{17,1},{2,10},{10... | collective-permute-start | bytes 393224 | tf_op jit(solution)/shard_map/ppermute | solution.py:283
  18.3 18.3 %collective-permute-start.10 = (bf16[2,128,512]{2,1,0:T(8,128)(2,1)S(1)}, bf16[2,128,512]{2,1,0:T(8,128)(2,1)S(1)}, u32[]{:S(2)}, u32[]{:S(2)}) collective-permute-start(bf16[2,128,512]{2,1,0:T(8,128)(2,1)S(1)} %pad_maximum_fusion.6), channel_id=1, source_target_pairs={{0,6},{1,7},{2,4},{3,5},{4,2},{5,3},{6,0},{7,1},{8,14},{9,15},{10,... | collective-permute-start | bytes 786440 | tf_op jit(solution)/shard_map/ppermute | solution.py:240
  19.9 10.1 %collective-permute-start.14 = (bf16[4,128,256]{2,1,0:T(8,128)(2,1)S(1)}, bf16[4,128,256]{2,1,0:T(8,128)(2,1)S(1)}, u32[]{:S(2)}, u32[]{:S(2)}) collective-permute-start(bf16[4,128,256]{2,1,0:T(8,128)(2,1)S(1)} %pad_maximum_fusion.7), channel_id=1, source_target_pairs={{0,8},{8,24},{24,16},{16,0},{1,9},{9,25},{25,17},{17,1},{2,10},{10... | collective-permute-start | bytes 786440 | tf_op jit(solution)/shard_map/ppermute | solution.py:283
  24.3 11.4 %collective-permute-start.8 = (bf16[4,128,256]{2,1,0:T(8,128)(2,1)S(1)}, bf16[4,128,256]{2,1,0:T(8,128)(2,1)S(1)}, u32[]{:S(2)}, u32[]{:S(2)}) collective-permute-start(bf16[4,128,256]{2,1,0:T(8,128)(2,1)S(1)} %pad_maximum_fusion.5), channel_id=1, source_target_pairs={{0,8},{8,24},{24,16},{16,0},{1,9},{9,25},{25,17},{17,1},{2,10},{10... | collective-permute-start | bytes 786440 | tf_op jit(solution)/shard_map/ppermute | solution.py:283
  25.5 11.2 %collective-permute-start.2 = (bf16[2,128,512]{2,1,0:T(8,128)(2,1)S(1)}, bf16[2,128,512]{2,1,0:T(8,128)(2,1)S(1)}, u32[]{:S(2)}, u32[]{:S(2)}) collective-permute-start(bf16[2,128,512]{2,1,0:T(8,128)(2,1)S(1)} %pad_maximum_fusion.3), channel_id=1, source_target_pairs={{0,4},{1,5},{2,6},{3,7},{4,0},{5,1},{6,2},{7,3},{8,12},{9,13},{10,... | collective-permute-start | bytes 786440 | tf_op jit(solution)/shard_map/ppermute | solution.py:240
  26.7 15.1 %collective-permute-start.1 = (bf16[2,128,512]{2,1,0:T(8,128)(2,1)S(1)}, bf16[2,128,512]{2,1,0:T(8,128)(2,1)S(1)}, u32[]{:S(2)}, u32[]{:S(2)}) collective-permute-start(bf16[2,128,512]{2,1,0:T(8,128)(2,1)S(1)} %pad_maximum_fusion.2), channel_id=1, source_target_pairs={{0,2},{1,3},{2,0},{3,1},{4,6},{5,7},{6,4},{7,5},{8,10},{9,11},{10,... | collective-permute-start | bytes 786440 | tf_op jit(solution)/shard_map/ppermute | solution.py:240
  30.1 14.8 %collective-permute-start.15 = (bf16[4,128,256]{2,1,0:T(8,128)(2,1)S(1)}, bf16[4,128,256]{2,1,0:T(8,128)(2,1)S(1)}, u32[]{:S(2)}, u32[]{:S(2)}) collective-permute-start(bf16[4,128,256]{2,1,0:T(8,128)(2,1)S(1)} %collective-permute-done.14.refs_4_), channel_id=1, source_target_pairs={{0,8},{8,24},{24,16},{16,0},{1,9},{9,25},{25,17},{17,1},{2,10},{10... | collective-permute-start | bytes 786440 | tf_op jit(solution)/shard_map/ppermute | solution.py:283
  35.7 14.2 %collective-permute-start.9 = (bf16[4,128,256]{2,1,0:T(8,128)(2,1)S(1)}, bf16[4,128,256]{2,1,0:T(8,128)(2,1)S(1)}, u32[]{:S(2)}, u32[]{:S(2)}) collective-permute-start(bf16[4,128,256]{2,1,0:T(8,128)(2,1)S(1)} %collective-permute-done.8.refs_3_.refs_1_), channel_id=1, source_target_pairs={{0,8},{8,24},{24,16},{16,0},{1,9},{9,25},{25,17},{17,1},{2,10},{10... | collective-permute-start | bytes 786440 | tf_op jit(solution)/shard_map/ppermute | solution.py:283
  52.4 7.2 %collective-permute-start.21 = (bf16[128,512]{1,0:T(8,128)(2,1)S(1)}, bf16[128,512]{1,0:T(8,128)(2,1)S(1)}, u32[]{:S(2)}, u32[]{:S(2)}) collective-permute-start(bf16[128,512]{1,0:T(8,128)(2,1)S(1)} %get-tuple-element.31), channel_id=1, source_target_pairs={{0,6},{1,7},{2,4},{3,5},{4,2},{5,3},{6,0},{7,1},{8,14},{9,15},{10,... | collective-permute-start | bytes 393224 | tf_op jit(solution)/shard_map/ppermute | solution.py:240
  52.9 8.0 %collective-permute-start.22 = (bf16[128,512]{1,0:T(8,128)(2,1)S(1)}, bf16[128,512]{1,0:T(8,128)(2,1)S(1)}, u32[]{:S(2)}, u32[]{:S(2)}) collective-permute-start(bf16[128,512]{1,0:T(8,128)(2,1)S(1)} %get-tuple-element.32), channel_id=1, source_target_pairs={{0,7},{1,6},{2,5},{3,4},{4,3},{5,2},{6,1},{7,0},{8,15},{9,14},{10,... | collective-permute-start | bytes 393224 | tf_op jit(solution)/shard_map/ppermute | solution.py:240
  55.2 6.2 %collective-permute-start.16 = (bf16[128,512]{1,0:T(8,128)(2,1)S(1)}, bf16[128,512]{1,0:T(8,128)(2,1)S(1)}, u32[]{:S(2)}, u32[]{:S(2)}) collective-permute-start(bf16[128,512]{1,0:T(8,128)(2,1)S(1)} %get-tuple-element.26), channel_id=1, source_target_pairs={{0,1},{1,0},{2,3},{3,2},{4,5},{5,4},{6,7},{7,6},{8,9},{9,8},{10,11... | collective-permute-start | bytes 393224 | tf_op jit(solution)/shard_map/ppermute | solution.py:240
  57.9 6.4 %collective-permute-start.17 = (bf16[128,512]{1,0:T(8,128)(2,1)S(1)}, bf16[128,512]{1,0:T(8,128)(2,1)S(1)}, u32[]{:S(2)}, u32[]{:S(2)}) collective-permute-start(bf16[128,512]{1,0:T(8,128)(2,1)S(1)} %get-tuple-element.27), channel_id=1, source_target_pairs={{0,2},{1,3},{2,0},{3,1},{4,6},{5,7},{6,4},{7,5},{8,10},{9,11},{10,... | collective-permute-start | bytes 393224 | tf_op jit(solution)/shard_map/ppermute | solution.py:240
  59.4 5.9 %collective-permute-start.18 = (bf16[128,512]{1,0:T(8,128)(2,1)S(1)}, bf16[128,512]{1,0:T(8,128)(2,1)S(1)}, u32[]{:S(2)}, u32[]{:S(2)}) collective-permute-start(bf16[128,512]{1,0:T(8,128)(2,1)S(1)} %get-tuple-element.28), channel_id=1, source_target_pairs={{0,3},{1,2},{2,1},{3,0},{4,7},{5,6},{6,5},{7,4},{8,11},{9,10},{10,... | collective-permute-start | bytes 393224 | tf_op jit(solution)/shard_map/ppermute | solution.py:240
  59.6 6.4 %collective-permute-start.19 = (bf16[128,512]{1,0:T(8,128)(2,1)S(1)}, bf16[128,512]{1,0:T(8,128)(2,1)S(1)}, u32[]{:S(2)}, u32[]{:S(2)}) collective-permute-start(bf16[128,512]{1,0:T(8,128)(2,1)S(1)} %get-tuple-element.29), channel_id=1, source_target_pairs={{0,4},{1,5},{2,6},{3,7},{4,0},{5,1},{6,2},{7,3},{8,12},{9,13},{10,... | collective-permute-start | bytes 393224 | tf_op jit(solution)/shard_map/ppermute | solution.py:240
  60.9 6.8 %collective-permute-start.20 = (bf16[128,512]{1,0:T(8,128)(2,1)S(1)}, bf16[128,512]{1,0:T(8,128)(2,1)S(1)}, u32[]{:S(2)}, u32[]{:S(2)}) collective-permute-start(bf16[128,512]{1,0:T(8,128)(2,1)S(1)} %get-tuple-element.30), channel_id=1, source_target_pairs={{0,5},{1,4},{2,7},{3,6},{4,1},{5,0},{6,3},{7,2},{8,13},{9,12},{10,... | collective-permute-start | bytes 393224 | tf_op jit(solution)/shard_map/ppermute | solution.py:240
